TPU v7x, 32 devices: a whole 2x2x4 slice. The times are simulated.
32 devices in a mesh: grp: 2 (over y), gx: 4 (over z), gy: 2 (over x), gz: 2 (over core).
Axes of the slice: x: 2, y: 2, z: 4, core: 2. Of those that a mesh axis runs over, the one named last changes fastest.
Arguments:
- design: int32 [16, 16, 256], P(('grp', 'gx'), 'gy', 'gz'), parts along dimension 0, may hold values from 0 to 15
- supports: int32 [16, 16, 256], P(('grp', 'gx'), 'gy', 'gz'), parts along dimension 0, may hold values 0 or 1
- body_load: float32 [12, 3, 8, 16, 256], P('grp', None, 'gx', 'gy', 'gz'), parts along dimension 0, may hold values from -6 to 6
- start: float32 [12, 3, 8, 16, 256], P('grp', None, 'gx', 'gy', 'gz'), parts along dimension 0, may hold values from -1.8 to 1.8
- load_nodes: int32 [12, 16], P('grp'), parts along dimension 0, may hold values from 0 to 32767
- load_values: float32 [12, 16, 3], P('grp'), parts along dimension 0, may hold values from -24 to 24
Outputs:
- solution: float32 [12, 3, 8, 16, 256], P('grp', None, 'gx', 'gy', 'gz'), parts along dimension 0
- residual: float32 [12, 3, 8, 16, 256], P('grp', None, 'gx', 'gy', 'gz'), parts along dimension 0
There are 2 independent parts, one for each index of `grp`. A program takes and returns all parts, laid end to end along the dimension named above; each array names one. Nothing has to cross between parts.
Inputs may be any that keep to these rules, and one draw needn't show every extreme that they name: `supports`: 1 where all three displacements of the node are held fixed. `load_nodes`: flat index (i * 16 + j) * 256 + k of a loaded node; a node may be named several times.
All inputs are finite; a program needn't handle non-finite values. No bound on the sum of `supports` on one device may be relied on, other than what follows from the above.
Results may differ from a plain program's by a relative error of at most 0.0003.
Values sent between devices are 32-bit elements; how exact they have to be, the bound alone decides.
No kernel may reach another device: no remote copies, remote signals or barrier semaphores. Data moves between devices by JAX's collectives and lax.ppermute only.
A program may use at most 64 MiB of HBM per device.

v0:
```python
import jax
import jax.numpy as jnp
from jax import lax
from jax.experimental import pallas as pl
from jax.experimental.pallas import tpu as pltpu
from jax.sharding import PartitionSpec as P


LEVELS = 16

soft_modulus = 0.05
poisson_ratio = 0.3
lame = poisson_ratio / ((1.0 + poisson_ratio) * (1.0 - 2.0 * poisson_ratio))
shear = 1.0 / (2.0 * (1.0 + poisson_ratio))
THREE, TWO, ONE = 1.0 / 16.0, 1.0 / 48.0, 1.0 / 144.0
CORNER = THREE * (lame + 4.0 * shear) + 2.0 * TWO * (lame + 4.0 * shear) + ONE * (lame + 4.0 * shear)

VMEM, SMEM = pltpu.VMEM, pltpu.SMEM
F32 = jnp.float32


def up8(n):
    return -(-n // 8) * 8


def call(body, outs, ins, scratch=(), flops=0, smem=(), hbm=(), far_out=False):
    kinds = [SMEM if i in smem else pltpu.HBM if i in hbm else VMEM for i in range(len(ins))]
    ins = [x if k is SMEM else pltpu.with_memory_space_constraint(x, k) for x, k in zip(ins, kinds)]
    return pl.pallas_call(
        body,
        out_shape=[jax.ShapeDtypeStruct(s, F32) if far_out else VMEM(s, F32) for s in outs],
        in_specs=[pl.BlockSpec(memory_space=k) for k in kinds],
        out_specs=[pl.BlockSpec(memory_space=pl.ANY if far_out else VMEM)] * len(outs),
        scratch_shapes=[VMEM(s, F32) if isinstance(s, tuple) else s for s in scratch],
        compiler_params=pltpu.CompilerParams(vmem_limit_bytes=16 * 2**20),
        cost_estimate=pl.CostEstimate(flops=flops, bytes_accessed=0, transcendentals=0),
    )(*ins)


class Plan:
    def __init__(self, block, mesh):
        self.cases, self.comps, self.planes, self.rows, self.width = block
        self.fields = self.cases * self.comps
        self.ngx, self.ngy, self.tiles = mesh["gx"], mesh["gy"], mesh["gz"]
        if not (self.planes == self.tiles == 2 and self.rows % 8 == 0 and self.comps == 3):
            raise ValueError("block shape")
        self.depth = (self.tiles * self.width, self.ngy * self.rows)
        self.r0 = self.rows + 6
        self.main = up8((self.fields + 2) * self.rows)
        self.halo = up8((self.fields + 2) * 6)

    def per(self, count):
        return up8(self.fields * count)

    def tile(self, ref, base, count, comp, row):
        return ref[pl.ds(base + comp * count + row, self.cases, stride=self.comps * count), :]

    def put(self, ref, base, count, comp, row, value):
        ref[pl.ds(base + comp * count + row, self.cases, stride=self.comps * count), :] = value

    def raw(self, ref, base, comp, plane, row):
        start = base + (comp * self.planes + plane) * self.rows + row
        return ref[pl.ds(start, self.cases, stride=self.comps * self.planes * self.rows), :]

    def lanes(self, count=None):
        return lax.broadcasted_iota(jnp.int32, (count or self.cases, self.width), 1)

    def ahead(self, tiles, lane):
        moved = [pltpu.roll(v, self.width - 1, 1) for v in tiles]
        moved.append(jnp.zeros_like(tiles[0]))
        return [jnp.where(lane == self.width - 1, moved[t + 1], moved[t]) for t in range(self.tiles)]

    def behind(self, tiles, lane):
        moved = [pltpu.roll(v, 1, 1) for v in tiles]
        moved = [jnp.zeros_like(tiles[0])] + moved
        return [jnp.where(lane == 0, moved[t], moved[t + 1]) for t in range(self.tiles)]

    def wide(self, row):
        return jnp.broadcast_to(row, (self.cases, self.width))


def modes_z(p, load, mask, count, sign, out):
    lane = p.lanes()
    for r in range(count):
        m = [p.wide(mask(t, r)) for t in range(p.tiles)]
        ms = [x * sign for x in m]
        for comp in range(3):
            v = [load(t, comp, r) * (ms[t] if comp == 0 else m[t]) for t in range(p.tiles)]
            n = p.ahead(v, lane)
            for t in range(p.tiles):
                out[((comp * 2) * count + r) * p.tiles + t, 0 : p.cases, :] = v[t] + n[t]
                out[((comp * 2 + 1) * count + r) * p.tiles + t, 0 : p.cases, :] = n[t] - v[t]


def layer(p, own, other, flip, modulus, count, sign, emit):
    lane = p.lanes()

    def modes_y(ref, e, t):
        found = {}
        for comp in range(3):
            for c in (0, 1):
                at = ((comp * 2 + c) * count + e) * p.tiles + t
                a = ref[at, 0 : p.cases, :]
                b = ref[at + p.tiles, 0 : p.cases, :]
                found[comp, 0, c] = a + b
                found[comp, 1, c] = b - a
        return found

    carry = {}
    for e in range(count - 1):
        done = {}
        for t in range(p.tiles):
            near, far = modes_y(own, e, t), modes_y(other, e, t)
            u = [{}, {}, {}]
            for (comp, b, c), x in near.items():
                y = far[comp, b, c]
                plus, minus = (y - x, y + x) if flip and comp == 0 else (y + x, y - x)
                u[comp][0, b, c], u[comp][1, b, c] = plus, minus
            ux, uy, uz = u
            mod = p.wide(modulus(t, e))
            ea, eb, es = mod * (THREE * lame), mod * (2.0 * THREE * shear), mod * (THREE * shear)
            ed, ee, ef = mod * (TWO * (lame + 3.0 * shear)), mod * (TWO * lame), mod * (TWO * shear)
            eg = mod * (ONE * (lame + 4.0 * shear))
            q = ea * (ux[1, 0, 0] + uy[0, 1, 0] + uz[0, 0, 1])
            sxy = es * (uy[1, 0, 0] + ux[0, 1, 0])
            syz = es * (uz[0, 1, 0] + uy[0, 0, 1])
            sxz = es * (uz[1, 0, 0] + ux[0, 0, 1])
            s = ux[0, 1, 1] + uy[1, 0, 1] + uz[1, 1, 0]
            gx = {
                (1, 0, 0): q + eb * ux[1, 0, 0],
                (0, 1, 0): sxy,
                (0, 0, 1): sxz,
                (1, 0, 1): ed * ux[1, 0, 1] + ee * uy[0, 1, 1],
                (1, 1, 0): ed * ux[1, 1, 0] + ee * uz[0, 1, 1],
                (0, 1, 1): ef * (s + ux[0, 1, 1]),
                (1, 1, 1): eg * ux[1, 1, 1],
            }
            gy = {
                (0, 1, 0): q + eb * uy[0, 1, 0],
                (1, 0, 0): sxy,
                (0, 0, 1): syz,
                (0, 1, 1): ed * uy[0, 1, 1] + ee * ux[1, 0, 1],
                (1, 1, 0): ed * uy[1, 1, 0] + ee * uz[1, 0, 1],
                (1, 0, 1): ef * (s + uy[1, 0, 1]),
                (1, 1, 1): eg * uy[1, 1, 1],
            }
            gz = {
                (0, 0, 1): q + eb * uz[0, 0, 1],
                (1, 0, 0): sxz,
                (0, 1, 0): syz,
                (0, 1, 1): ed * uz[0, 1, 1] + ee * ux[1, 1, 0],
                (1, 0, 1): ed * uz[1, 0, 1] + ee * uy[1, 1, 0],
                (1, 1, 0): ef * (s + uz[1, 1, 0]),
                (1, 1, 1): eg * uz[1, 1, 1],
            }
            for comp, g in enumerate((gx, gy, gz)):
                h = {bc: g[(0,) + bc] - g[(1,) + bc] for bc in ((0, 1), (1, 0), (1, 1))}
                h[0, 0] = -g[1, 0, 0]
                for c in (0, 1):
                    if e:
                        done[comp, c, t] = carry[comp, c, t] + (h[0, c] - h[1, c])
                    carry[comp, c, t] = h[0, c] + h[1, c]
        if e:
            for comp in range(3):
                low = [done[comp, 0, t] - done[comp, 1, t] for t in range(p.tiles)]
                high = [done[comp, 0, t] + done[comp, 1, t] for t in range(p.tiles)]
                back = p.behind(high, lane)
                for t in range(p.tiles):
                    total = low[t] + back[t]
                    emit(t, comp, e - 1, total * sign if comp == 0 else total)


def single(p, ref, modulus, count, sign, way, emit):
    lane = p.lanes()
    cq, cb, cs = THREE * lame, 2.0 * THREE * shear, THREE * shear
    cd, ce, cf = TWO * (lame + 3.0 * shear), TWO * lame, TWO * shear
    cg = ONE * (lame + 4.0 * shear)
    carry = {}
    for e in range(count - 1):
        done = {}
        for t in range(p.tiles):
            m = [{}, {}, {}]
            for comp in range(3):
                for c in (0, 1):
                    at = ((comp * 2 + c) * count + e) * p.tiles + t
                    a = ref[at, 0 : p.cases, :]
                    b = ref[at + p.tiles, 0 : p.cases, :]
                    m[comp][0, c], m[comp][1, c] = a + b, b - a
            x, y, z = m
            mod = p.wide(modulus(t, e))
            q = cq * (x[0, 0] + y[1, 0] + z[0, 1])
            sxy = cs * (y[0, 0] + x[1, 0])
            sxz = cs * (z[0, 0] + x[0, 1])
            pair = z[1, 0] + y[0, 1]
            syz = cs * pair
            s = x[1, 1] + pair
            if way > 0:
                sh = {
                    (0, 1, 0): sxy - (cd * x[1, 0] + ce * z[1, 1]),
                    (0, 0, 1): sxz - (cd * x[0, 1] + ce * y[1, 1]),
                    (0, 1, 1): (2.0 * cf - cg) * x[1, 1] + cf * pair,
                    (1, 0, 0): -sxy,
                    (1, 1, 0): q + ((cb - cd) * y[1, 0] - ce * z[0, 1]),
                    (1, 0, 1): syz - cf * (s + y[0, 1]),
                    (1, 1, 1): (cd - cg) * y[1, 1] + ce * x[0, 1],
                    (2, 0, 0): -sxz,
                    (2, 0, 1): q + ((cb - cd) * z[0, 1] - ce * y[1, 0]),
                    (2, 1, 0): syz - cf * (s + z[1, 0]),
                    (2, 1, 1): (cd - cg) * z[1, 1] + ce * x[1, 0],
                }
            else:
                sh = {
                    (0, 1, 0): -sxy - (cd * x[1, 0] + ce * z[1, 1]),
                    (0, 0, 1): -sxz - (cd * x[0, 1] + ce * y[1, 1]),
                    (0, 1, 1): (-2.0 * cf - cg) * x[1, 1] - cf * pair,
                    (1, 0, 0): sxy,
                    (1, 1, 0): q + ((cb + cd) * y[1, 0] + ce * z[0, 1]),
                    (1, 0, 1): syz + cf * (s + y[0, 1]),
                    (1, 1, 1): (cd + cg) * y[1, 1] + ce * x[0, 1],
                    (2, 0, 0): sxz,
                    (2, 0, 1): q + ((cb + cd) * z[0, 1] + ce * y[1, 0]),
                    (2, 1, 0): syz + cf * (s + z[1, 0]),
                    (2, 1, 1): (cd + cg) * z[1, 1] + ce * x[1, 0],
                }
            sh[0, 0, 0] = -(q + cb * x[0, 0])
            for comp in range(3):
                h = {bc: mod * sh[(comp,) + bc] for bc in ((0, 0), (0, 1), (1, 0), (1, 1))}
                for c in (0, 1):
                    if e:
                        done[comp, c, t] = carry[comp, c, t] + (h[0, c] - h[1, c])
                    carry[comp, c, t] = h[0, c] + h[1, c]
        if e:
            for comp in range(3):
                low = [done[comp, 0, t] - done[comp, 1, t] for t in range(p.tiles)]
                high = [done[comp, 0, t] + done[comp, 1, t] for t in range(p.tiles)]
                back = p.behind(high, lane)
                for t in range(p.tiles):
                    total = low[t] + back[t]
                    emit(t, comp, e - 1, total * sign if comp == 0 else total)


OWN, PARTNER, RECEIVED, NEAR, FAR, SCALE = range(6)


def static(p, ref, kind, t, row):
    at = (kind * p.tiles + t) * up8(p.r0) + row
    return ref[at : at + 1, :]


def place():
    core = lax.axis_index("gz")
    return core, 1.0 - 2.0 * core.astype(F32)


def shards(mesh, design, supports, body_load, start, load_nodes, load_values):
    p = Plan(body_load.shape, mesh)
    C, D, Y, W, T, FL = p.cases, p.comps, p.rows, p.width, p.tiles, p.fields
    Q = p.planes
    n_raw = FL * Q * Y
    z_load = n_raw
    z_stat = z_load + FL * Y
    z_rows = z_stat + 2 * Q * Y
    y_load = Q * FL * 3
    y_stat = y_load + Q * FL * 2
    y_rows = up8(y_stat + Q * 6)
    R0, R1, R2 = Y + 6, Y + 4, Y + 2
    N1, N2, N3 = p.per(R1), p.per(R2), p.per(Y)
    M, H = p.main, p.halo
    both = p.ngy == 2

    x0 = start.reshape(n_raw, W)
    bl = body_load.reshape(n_raw, W)
    de = design.reshape(Q * Y, W)
    su = supports.reshape(Q * Y, W)

    def gather_body(x_hbm, b_hbm, d_hbm, s_hbm, z_ref, b_ref, *refs):
        y_refs, (d_ref, s_ref, sems) = refs[:-3], refs[-3:]
        core = lax.axis_index("gz")
        moves = [
            pltpu.make_async_copy(src, dst, sems.at[i])
            for i, (src, dst) in enumerate(
                ((x_hbm, z_ref.at[pl.ds(0, n_raw)]), (b_hbm, b_ref), (d_hbm, d_ref), (s_hbm, s_ref))
            )
        ]
        for move in moves:
            move.start()
        moves[2].wait()
        density = (d_ref[...].astype(F32) + 1.0) / LEVELS
        z_ref[z_stat : z_stat + Q * Y, :] = (
            soft_modulus + (1.0 - soft_modulus) * density * density * density
        )
        moves[3].wait()
        z_ref[z_stat + Q * Y : z_rows, :] = 1.0 - s_ref[...].astype(F32)
        if both:
            first = lax.axis_index("gy") == 0
            froms = [(jnp.where(first, Y - 3, 0), jnp.where(first, Y - 2, 0))]
        else:
            froms = [(Y - 3, Y - 2), (0, 0)]
        for y_ref, (three, _) in zip(y_refs, froms):
            if y_rows > y_stat + Q * 6:
                y_ref[y_stat + Q * 6 : y_rows, :] = jnp.zeros((y_rows - y_stat - Q * 6, W), F32)
            for q in range(Q):
                for kind in range(2):
                    for r in range(3):
                        at = y_stat + q * 6 + kind * 3 + r
                        y_ref[at : at + 1, :] = z_ref[pl.ds(z_stat + (kind * Q + q) * Y + three + r, 1), :]
        moves[0].wait()
        for y_ref, (three, _) in zip(y_refs, froms):
            for q in range(Q):
                for comp in range(D):
                    for r in range(3):
                        p.put(y_ref, q * FL * 3, 3, comp, r, p.raw(z_ref, 0, comp, q, three + r))
        moves[1].wait()
        for y_ref, (_, two) in zip(y_refs, froms):
            for q in range(Q):
                for comp in range(D):
                    for r in range(2):
                        p.put(y_ref, y_load + q * FL * 2, 2, comp, r, p.raw(b_ref, 0, comp, q, two + r))
        for f in range(FL):
            z_ref[z_load + f * Y : z_load + (f + 1) * Y, :] = b_ref[
                pl.ds(pl.multiple_of((f * Q + 1 - core) * Y, 8), Y), :
            ]

    z_msg, b_near, *y_msgs = call(
        gather_body,
        [(z_rows, W), (n_raw, W)] + [(y_rows, W)] * (1 if both else 2),
        [x0, bl, de, su],
        [VMEM((Q * Y, W), jnp.int32), VMEM((Q * Y, W), jnp.int32), pltpu.SemaphoreType.DMA((4,))],
        flops=10**5,
        hbm=(0, 1, 2, 3),
    )

    def cores(x):
        return lax.ppermute(x, "gz", [(i, 1 - i) for i in range(T)])

    def rows_along(x, step):
        return lax.ppermute(x, "gy", [(i, (i + step) % p.ngy) for i in range(p.ngy)])

    def planes_along(x):
        pairs = []
        for i in range(p.ngx):
            for j in range(p.ngy):
                for k in range(T):
                    to = i + 2 * k - 1
                    mine = (i * p.ngy + j) * T + k
                    if 0 <= to < p.ngx:
                        pairs.append((mine, (to * p.ngy + j) * T + 1 - k))
                    elif p.ngy % 2 == 0:
                        pairs.append((mine, (i * p.ngy + (j ^ 1)) * T + k))
                    else:
                        pairs.append((mine, mine))
        return lax.ppermute(x, ("gx", "gy", "gz"), pairs)

    if both:
        y_got = [rows_along(y_msgs[0], 1)]
    else:
        y_got = [rows_along(y_msgs[0], 1), rows_along(y_msgs[1], -1)]
    z_got = cores(z_msg)
    zy_got = [cores(y) for y in y_got]
    halos = len(y_got)

    def main_body(s_ref, z_ref, own_ref, par_ref):
        core = lax.axis_index("gz")
        for out, plane in ((own_ref, core), (par_ref, 1 - core)):
            for src, half in ((s_ref, core), (z_ref, 1 - core)):
                base = half * M
                for comp in range(D):
                    for r in range(Y):
                        p.put(out, base, Y, comp, r, p.raw(src, 0, comp, plane, r))
                for kind in range(2):
                    out[pl.ds(pl.multiple_of(base + (FL + kind) * Y, 8), Y), :] = src[
                        pl.ds(pl.multiple_of(z_stat + (kind * Q + plane) * Y, 8), Y), :
                    ]

    own_m, par_m = call(main_body, [(T * M, W)] * 2, [z_msg, z_got], flops=10**5)
    far_m = planes_along(own_m)

    def halo_body(*refs):
        y_refs, zy_refs = refs[:halos], refs[halos : 2 * halos]
        own_ref, par_ref = refs[2 * halos :]
        core = lax.axis_index("gz")
        row = lax.axis_index("gy")
        below = jnp.where(row > 0, 1.0, 0.0)
        above = jnp.where(row < p.ngy - 1, 1.0, 0.0)
        for out, plane in ((own_ref, core), (par_ref, 1 - core)):
            for ys, half in ((y_refs, core), (zy_refs, 1 - core)):
                base = half * H
                for r in range(6):
                    src, flag = (ys[0], below) if r < 3 else (ys[-1], above)
                    for comp in range(D):
                        p.put(out, base, 6, comp, r, p.tile(src, plane * (FL * 3), 3, comp, r % 3))
                    for kind in range(2):
                        v = src[pl.ds(y_stat + plane * 6 + kind * 3 + r % 3, 1), :]
                        out[pl.ds(base + (FL + kind) * 6 + r, 1), :] = v * flag

    own_h, par_h = call(halo_body, [(T * H, W)] * 2, y_got + zy_got, flops=10**5)
    far_h = planes_along(own_h)

    def field_at(refs, t, comp, r):
        main, halo = refs
        if 3 <= r < Y + 3:
            return p.tile(main, t * M, Y, comp, r - 3)
        return p.tile(halo, t * H, 6, comp, r if r < 3 else r - Y)

    def const_at(refs, kind, t, r):
        main, halo = refs
        if 3 <= r < Y + 3:
            at = t * M + (FL + kind) * Y + r - 3
            return main[at : at + 1, :]
        at = t * H + (FL + kind) * 6 + (r if r < 3 else r - Y)
        return halo[at : at + 1, :]

    def const_parts(refs, kind, t):
        main, halo = refs
        at = t * H + (FL + kind) * 6
        to = t * M + (FL + kind) * Y
        return halo[at : at + 3, :], main[to : to + Y, :], halo[at + 3 : at + 6, :]

    def points_body(node_ref, value_ref, out):
        core = lax.axis_index("gz")
        deep, across = p.depth
        base = ((lax.axis_index("gx") * Q + core) * across + lax.axis_index("gy") * Y - 2) * deep
        spots = jnp.concatenate([node_ref[c : c + 1, :] for c in range(C)], axis=1) - base
        total = C * n_loads
        if W & (W - 1):
            row = spots // W
            lane = spots - row * W
        else:
            row, lane = spots >> (W.bit_length() - 1), spots & (W - 1)
        hot = jnp.where(lax.broadcasted_iota(jnp.int32, (W, total), 0) == lane, 1.0, 0.0)
        rows8 = jnp.broadcast_to(row, (8, total))
        mine = lax.broadcasted_iota(jnp.int32, (8, total), 0)
        column = lax.broadcasted_iota(jnp.int32, (8, total), 1)
        mine = (column >= mine * n_loads) & (column < (mine + 1) * n_loads)
        values = []
        for comp in range(D):
            v = jnp.concatenate([value_ref[c, comp : comp + 1, :] for c in range(C)], axis=1)
            values.append(jnp.where(mine, jnp.broadcast_to(v, (8, total)), 0.0))
        left = [
            jnp.where(rows8 == r * T + t, values[comp], 0.0)
            for t in range(T)
            for comp in range(D)
            for r in range(R1)
        ]
        out[...] = lax.dot_general(
            jnp.concatenate(left, axis=0),
            hot,
            (((1,), (1,)), ((), ())),
            precision=lax.Precision.HIGHEST,
            preferred_element_type=F32,
        )

    n_loads = load_nodes.shape[1]
    (points,) = call(
        points_body,
        [(T * D * R1 * 8, W)],
        [load_nodes, jnp.swapaxes(load_values, 1, 2)],
        flops=10**6,
    )

    def loads_body(p_ref, b_ref, z_ref, *refs):
        y_refs, zy_refs = refs[:halos], refs[halos : 2 * halos]
        out = refs[2 * halos]
        core = lax.axis_index("gz")
        for half in range(2):
            t = core if half == 0 else 1 - core
            ys = y_refs if half == 0 else zy_refs
            for comp in range(D):
                for r in range(R1):
                    if r < 2:
                        v = p.tile(ys[0], y_load + core * (FL * 2), 2, comp, r)
                    elif r < Y + 2:
                        if half == 0:
                            v = p.raw(b_ref, 0, comp, core, r - 2)
                        else:
                            v = p.tile(z_ref, z_load, Y, comp, r - 2)
                    else:
                        v = p.tile(ys[-1], y_load + core * (FL * 2), 2, comp, r - Y - 2)
                    at = t * (D * R1) + comp * R1 + r
                    out[at, 0:C, :] = v + p_ref[pl.ds(pl.multiple_of(at * 8, 8), C), :]

    (loaded,) = call(
        loads_body,
        [(T * D * R1, 8, W)],
        [points, b_near, z_got] + y_got + zy_got,
        flops=10**6,
    )

    def near_start_body(own_m_ref, own_h_ref, par_m_ref, par_h_ref, modes_ref, part_ref, other_ref):
        core, sign = place()
        own, par = (own_m_ref, own_h_ref), (par_m_ref, par_h_ref)
        for refs, out in ((own, modes_ref), (par, other_ref)):
            modes_z(
                p,
                lambda t, k, r, refs=refs: field_at(refs, t, k, r),
                lambda t, r, refs=refs: const_at(refs, 1, t, r),
                R0,
                sign,
                out,
            )

        def modulus(t, e):
            return jnp.where(core == 0, const_at(own, 0, t, e), const_at(par, 0, t, e))

        def emit(t, comp, r, v):
            part_ref[(comp * R1 + r) * T + t, 0:C, :] = v

        layer(p, modes_ref, other_ref, False, modulus, R0, sign, emit)

    def field_shapes(count):
        return (6 * count * T, 8, W)

    modes, part = call(
        near_start_body,
        [field_shapes(R0), (D * R1 * T, 8, W)],
        [own_m, own_h, par_m, par_h],
        [field_shapes(R0)],
        flops=10**6,
    )

    def far_start_body(
        far_m_ref, far_h_ref, own_m_ref, own_h_ref, par_m_ref, par_h_ref, modes_ref, part_ref, load_ref,
        r_ref, d_ref, st_ref, other_ref,
    ):
        core, sign = place()
        far, own, par = (far_m_ref, far_h_ref), (own_m_ref, own_h_ref), (par_m_ref, par_h_ref)
        column = lax.axis_index("gx")
        inside = jnp.where(core == 0, column > 0, column < p.ngx - 1)
        valid = jnp.where(inside, 1.0, 0.0)
        lane_rows = lax.broadcasted_iota(jnp.int32, (R1, W), 1)
        pad = up8(R0)
        sums = []
        for t in range(T):
            spans = ((0, 3), (3, Y), (Y + 3, 3))
            own_e, par_e, far_e = (const_parts(x, 0, t) for x in (own, par, far))
            own_m, par_m, far_m = (const_parts(x, 1, t) for x in (own, par, far))
            for n, (first, count) in enumerate(spans):
                for kind, v in (
                    (OWN, own_m[n]),
                    (PARTNER, par_m[n]),
                    (RECEIVED, far_m[n] * valid),
                    (NEAR, jnp.where(core == 0, own_e[n], par_e[n])),
                    (FAR, jnp.where(core == 0, far_e[n] * valid, own_e[n])),
                ):
                    to = (kind * T + t) * pad + first
                    st_ref[to : to + count, :] = v
            near, rest = (NEAR * T + t) * pad, (FAR * T + t) * pad
            sums.append(
                (st_ref[near : near + R1, :] + st_ref[rest : rest + R1, :])
                + (st_ref[near + 1 : near + 1 + R1, :] + st_ref[rest + 1 : rest + 1 + R1, :])
            )
        back = p.behind(sums, lane_rows)
        for t in range(T):
            around = sums[t] + back[t]
            at = (OWN * T + t) * pad + 1
            mov = st_ref[at : at + R1, :]
            guarded = jnp.where(mov > 0, around, 1.0)
            to = (SCALE * T + t) * pad + 1
            st_ref[to : to + R1, :] = mov / (CORNER * guarded) + (1.0 - mov)
        modes_z(
            p,
            lambda t, k, r: field_at(far, t, k, r),
            lambda t, r: static(p, st_ref, RECEIVED, t, r),
            R0,
            -sign,
            other_ref,
        )

        def emit(t, comp, r, v):
            force = v + part_ref[(comp * R1 + r) * T + t, 0:C, :]
            mov = p.wide(static(p, st_ref, OWN, t, r + 1))
            here = field_at(own, t, comp, r + 1)
            load = load_ref[t * (D * R1) + comp * R1 + r, 0:C, :]
            res = mov * (load - force) - (1.0 - mov) * here
            p.put(d_ref, t * N1, R1, comp, r, p.wide(static(p, st_ref, SCALE, t, r + 1)) * res)
            if 2 <= r < Y + 2:
                p.put(r_ref, t * N3, Y, comp, r - 2, res)

        layer(p, modes_ref, other_ref, True, lambda t, e: static(p, st_ref, FAR, t, e), R0, -sign, emit)

    res0, dir0, consts = call(
        far_start_body,
        [(T * N3, W), (T * N1, W), (6 * T * up8(R0), W)],
        [far_m, far_h, own_m, own_h, par_m, par_h, modes, part, loaded],
        [field_shapes(R0)],
        flops=10**6,
    )

    def near_apply(own_ref, par_ref, st_ref, part_ref, modes_ref, other_ref, per, count, shift):
        _, sign = place()
        modes_z(p, lambda t, k, r: p.tile(own_ref, t * per, count, k, r), lambda t, r: static(p, st_ref, OWN, t, r + shift), count, sign, modes_ref)
        modes_z(p, lambda t, k, r: p.tile(par_ref, t * per, count, k, r), lambda t, r: static(p, st_ref, PARTNER, t, r + shift), count, sign, other_ref)

        def emit(t, comp, r, v):
            part_ref[(comp * (count - 2) + r) * T + t, 0:C, :] = v

        def more(t, comp, r, v):
            at = (comp * (count - 2) + r) * T + t
            part_ref[at, 0:C, :] = part_ref[at, 0:C, :] + v

        layer(p, modes_ref, other_ref, False, lambda t, e: static(p, st_ref, NEAR, t, e + shift), count, sign, emit)
        single(p, modes_ref, lambda t, e: static(p, st_ref, FAR, t, e + shift), count, -sign, -1, more)

    def far_apply(far_ref, own_ref, st_ref, part_ref, other_ref, per, count, shift, emit):
        _, sign = place()
        modes_z(p, lambda t, k, r: p.tile(far_ref, t * per, count, k, r), lambda t, r: static(p, st_ref, RECEIVED, t, r + shift), count, -sign, other_ref)

        def finish(t, comp, r, v):
            force = v + part_ref[(comp * (count - 2) + r) * T + t, 0:C, :]
            mov = p.wide(static(p, st_ref, OWN, t, r + 1 + shift))
            here = p.tile(own_ref, t * per, count, comp, r + 1)
            emit(t, comp, r, mov * force + (1.0 - mov) * here, here)

        single(p, other_ref, lambda t, e: static(p, st_ref, FAR, t, e + shift), count, -sign, 1, finish)

    far_d = planes_along(dir0)
    par_d = cores(dir0)

    def near_one_body(own_ref, par_ref, st_ref, part_ref, modes_ref, other_ref):
        near_apply(own_ref, par_ref, st_ref, part_ref, modes_ref, other_ref, N1, R1, 1)

    (part1,) = call(
        near_one_body, [(D * R2 * T, 8, W)], [dir0, par_d, consts], [field_shapes(R1)] * 2, flops=10**6
    )

    def far_one_body(far_ref, own_ref, st_ref, part_ref, q_ref, w_ref, other_ref):
        if N2 > FL * R2:
            for t in range(T):
                w_ref[t * N2 + FL * R2 : (t + 1) * N2, :] = jnp.zeros((N2 - FL * R2, W), F32)

        def emit(t, comp, r, image, here):
            scale = p.wide(static(p, st_ref, SCALE, t, r + 2))
            p.put(w_ref, t * N2, R2, comp, r, scale * image - here)
            if 1 <= r < Y + 1:
                p.put(q_ref, t * N3, Y, comp, r - 1, image)

        far_apply(far_ref, own_ref, st_ref, part_ref, other_ref, N1, R1, 1, emit)

    image0, second = call(
        far_one_body,
        [(T * N3, W), (T * N2, W)],
        [far_d, dir0, consts, part1],
        [field_shapes(R1)],
        flops=10**6,
    )

    far_w = planes_along(second)
    par_w = cores(second)

    def columns(number, sums, lane):
        table = jnp.zeros((C, W), F32)
        for j in range(C):
            column = jnp.sum(sums[j], axis=1, keepdims=True)
            table = jnp.where(lane == number * C + j, column, table)
        return table

    def gram_body(d_ref, q_ref, r_ref, w_ref, g_ref, mine_ref, send_ref):
        core = lax.axis_index("gz")
        lane = p.lanes()
        sums = [[jnp.zeros((C, W), F32) for _ in range(C)] for _ in range(3)]
        for t in range(T):
            for comp in range(D):
                for r in range(Y):
                    d = p.tile(d_ref, t * N1, R1, comp, r + 2)
                    w = p.tile(w_ref, t * N2, R2, comp, r + 1)
                    for j in range(C):
                        at = t * N3 + (j * D + comp) * Y + r
                        q = q_ref[at : at + 1, :]
                        sums[0][j] = sums[0][j] + d * q
                        sums[1][j] = sums[1][j] + d * r_ref[at : at + 1, :]
                        sums[2][j] = sums[2][j] + w * q
        table = columns(0, sums[0], lane) + columns(1, sums[1], lane) + columns(2, sums[2], lane)
        g_ref[...] = jnp.zeros((8, W), F32)
        g_ref[0:C, :] = table
        for out, t in ((mine_ref, core), (send_ref, 1 - core)):
            for number, src in enumerate((r_ref, q_ref)):
                out[number * N3 : (number + 1) * N3, :] = src[pl.ds(pl.multiple_of(t * N3, 8), N3), :]
            for comp in range(D):
                for r in range(Y):
                    p.put(out, 2 * N3, Y, comp, r, p.tile(d_ref, t * N1, R1, comp, r + 2))
                    p.put(out, 3 * N3, Y, comp, r, p.tile(w_ref, t * N2, R2, comp, r + 1))

    gram3, mine, send = call(gram_body, [(8, W), (4 * N3, W), (4 * N3, W)], [dir0, image0, res0, second], flops=10**6)

    def near_two_body(own_ref, par_ref, st_ref, part_ref, modes_ref, other_ref):
        near_apply(own_ref, par_ref, st_ref, part_ref, modes_ref, other_ref, N2, R2, 2)

    (part2,) = call(
        near_two_body, [(D * Y * T, 8, W)], [second, par_w, consts], [field_shapes(R2)] * 2, flops=10**6
    )
    kept = cores(send)

    def far_two_body(far_ref, own_ref, st_ref, part_ref, gram_ref, mine_ref, send_ref, other_ref, u_ref):
        core = lax.axis_index("gz")

        def emit(t, comp, r, image, here):
            p.put(u_ref, t * N3, Y, comp, r, image)
            sums_in.append((image, t, comp, r))

        sums_in = []
        far_apply(far_ref, own_ref, st_ref, part_ref, other_ref, N2, R2, 2, emit)
        sums = [jnp.zeros((C, W), F32) for _ in range(C)]
        for _, t, comp, r in sums_in:
            u = p.tile(u_ref, t * N3, Y, comp, r)
            for j in range(C):
                at = t * N2 + (j * D + comp) * R2 + r + 1
                sums[j] = sums[j] + u * own_ref[at : at + 1, :]
        table = gram_ref[0:C, :] + columns(3, sums, p.lanes())
        for out, t in ((mine_ref, core), (send_ref, 1 - core)):
            out[0:N3, :] = u_ref[pl.ds(pl.multiple_of(t * N3, 8), N3), :]
            out[N3 : N3 + 8, :] = jnp.zeros((8, W), F32)
            out[N3 : N3 + C, :] = table

    mine_u, send_u = call(
        far_two_body,
        [(N3 + 8, W), (N3 + 8, W)],
        [far_w, second, consts, part2, gram3],
        [field_shapes(R2), (T * N3, W)],
        flops=10**6,
    )
    kept_u = cores(send_u)

    table = mine_u[N3 : N3 + 8, :] + kept_u[N3 : N3 + 8, :]
    for axis, size in (("gy", p.ngy), ("gx", p.ngx)):
        if size & (size - 1):
            table = lax.psum(table, axis)
            continue
        step = 1
        while step < size:
            pairs = [(i * T + k, (i ^ step) * T + 1 - k) for i in range(size) for k in range(T)]
            table = table + lax.ppermute(table, (axis, "gz"), pairs)
            step *= 2

    def final_body(
        g_ref, x_ref, mine_ref, mine_u_ref, kept_ref, kept_u_ref, out_hbm, res_hbm, a_ref, out_ref, res_ref, sems
    ):
        core = lax.axis_index("gz")
        lane = lax.broadcasted_iota(jnp.int32, (1, W), 1)

        def splat(row, at):
            return jnp.broadcast_to(row[:, at : at + 1], (1, W))

        def factor(rows, first):
            a = {(i, j): splat(rows[i], first + j) for i in range(C) for j in range(i + 1)}
            low, inv = {}, []
            for k in range(C):
                inv.append(1.0 / a[k, k])
                for i in range(k + 1, C):
                    low[i, k] = a[i, k] * inv[k]
                for i in range(k + 1, C):
                    for j in range(k + 1, i + 1):
                        a[i, j] = a[i, j] - low[i, k] * a[j, k]
            return low, inv

        def solve(factors, right):
            low, inv = factors
            y = []
            for i in range(C):
                v = right[i]
                for k in range(i):
                    v = v - low[i, k] * y[k]
                y.append(v)
            x = [None] * C
            for i in reversed(range(C)):
                v = y[i] * inv[i]
                for k in range(i + 1, C):
                    v = v - low[k, i] * x[k]
                x[i] = v
            return x

        rows = [g_ref[i : i + 1, :] for i in range(C)]
        first = solve(factor(rows, 0), rows)
        reduced = []
        for i in range(C):
            v = jnp.where(
                lane < 2 * C, pltpu.roll(rows[i], C, 1) - rows[i], pltpu.roll(rows[i], W - C, 1)
            )
            for k in range(C):
                v = v - splat(rows[i], 2 * C + k) * first[k]
            reduced.append(v)
        on_second = solve(factor(reduced, 2 * C), reduced)
        for i in range(C):
            v = first[i]
            for k in range(C):
                v = v - splat(first[i], 2 * C + k) * on_second[k]
            for k in range(C):
                a_ref[i * C + k] = jnp.broadcast_to(v[:, C + k : C + k + 1], (Y, W))
                a_ref[C * C + i * C + k] = jnp.broadcast_to(on_second[i][:, C + k : C + k + 1], (Y, W))
        halves = ((mine_ref, mine_u_ref, core), (kept_ref, kept_u_ref, 1 - core))
        moves = []
        for number in range(2):
            target = (out_ref, res_ref)[number]
            for src, src_u, plane in halves:
                for comp in range(D):
                    fs = [(j * D + comp) * Y for j in range(C)]
                    at = N3 if number else 2 * N3
                    v = [src[at + f : at + f + Y, :] for f in fs]
                    u = [src_u[f : f + Y, :] if number else src[3 * N3 + f : 3 * N3 + f + Y, :] for f in fs]
                    for i in range(C):
                        at = pl.ds(pl.multiple_of(((i * D + comp) * Q + plane) * Y, 8), Y)
                        total = a_ref[i] * v[0] + a_ref[C * C + i] * u[0]
                        for j in range(1, C):
                            total = total + (a_ref[j * C + i] * v[j] + a_ref[C * C + j * C + i] * u[j])
                        if number:
                            target[at, :] = src[fs[i] : fs[i] + Y, :] - total
                        else:
                            target[at, :] = x_ref[at, :] + total
            moves.append(pltpu.make_async_copy(target, (out_hbm, res_hbm)[number], sems.at[number]))
            moves[-1].start()
        for move in moves:
            move.wait()

    out, res = call(
        final_body,
        [(n_raw, W)] * 2,
        [table, z_msg, mine, mine_u, kept, kept_u],
        [(2 * C * C, Y, W), (n_raw, W), (n_raw, W), pltpu.SemaphoreType.DMA((2,))],
        flops=10**5,
        far_out=True,
    )
    return out.reshape(start.shape), res.reshape(start.shape)


def solution(mesh):
    in_specs = (
        P(("grp", "gx"), "gy", "gz"),
        P(("grp", "gx"), "gy", "gz"),
        P("grp", None, "gx", "gy", "gz"),
        P("grp", None, "gx", "gy", "gz"),
        P("grp", None),
        P("grp", None, None),
    )
    out_specs = (P("grp", None, "gx", "gy", "gz"), P("grp", None, "gx", "gy", "gz"))

    def body(*args):
        return shards(dict(mesh.shape), *args)

    return jax.shard_map(body, mesh=mesh, in_specs=in_specs, out_specs=out_specs, check_vma=False)
```

profile of v0, /device:TPU:0, one launch (start us, length us, event | category | flops | bytes accessed | tf_op | source)
XLA Modules:
  0.0 41.7 jit_solution(5102629035817507486)
XLA Ops:
  0.6 1.0 %shard_map.77 = (f32[464,128]{1,0:T(8,128)S(1)}, f32[288,128]{1,0:T(8,128)S(1)}, f32[192,128]{1,0:T(8,128)S(1)}) custom-call(f32[288,128]{1,0:T(8,128)} %bitcast.8, f32[288,128]{1,0:T(8,128)} %bitcast.9, s32[16,128]{1,0:T(8,128)} %bitcast.10, s32[16,128]{1,0:T(8,128)} %bitcast.11), custom_call_target="tpu_custom_call" | custom-call | flops 100000 | tf_op jit(solution)/shard_map/pallas_call | solution.py:29
  1.7 0.6 %collective-permute-start = (f32[464,128]{1,0:T(8,128)S(1)}, f32[464,128]{1,0:T(8,128)S(1)}, u32[]{:S(2)}, u32[]{:S(2)}) collective-permute-start(f32[464,128]{1,0:T(8,128)S(1)} %get-tuple-element.23.s_ref.x_ref), channel_id=1, source_target_pairs={{0,1},{1,0},{2,3},{3,2},{4,5},{5,4},{6,7},{7,6},{8,9},{9,8},{10,11... | collective-permute-start | bytes 712712 | tf_op jit(solution)/shard_map/ppermute | solution.py:334
  2.2 2.6 %collective-permute-start.2 = (f32[192,128]{1,0:T(8,128)S(1)}, f32[192,128]{1,0:T(8,128)S(1)}, u32[]{:S(2)}, u32[]{:S(2)}) collective-permute-start(f32[192,128]{1,0:T(8,128)S(1)} %get-tuple-element.25), channel_id=1, source_target_pairs={{0,2},{2,0},{1,3},{3,1},{4,6},{6,4},{5,7},{7,5},{8,10},{10,8},{9,1... | collective-permute-start | bytes 294920 | tf_op jit(solution)/shard_map/ppermute | solution.py:337
  4.8 3.4 %collective-permute-done.2.refs_0_ = f32[192,128]{1,0:T(8,128)S(1)} collective-permute-done((f32[192,128]{1,0:T(8,128)S(1)}, f32[192,128]{1,0:T(8,128)S(1)}, u32[]{:S(2)}, u32[]{:S(2)}) %collective-permute-start.2) | collective-permute-done | bytes 98336 | tf_op jit(solution)/shard_map/ppermute | solution.py:337
  8.3 1.8 %collective-permute-start.1 = (f32[320,128]{1,0:T(8,128)S(1)}, f32[320,128]{1,0:T(8,128)S(1)}, u32[]{:S(2)}, u32[]{:S(2)}) collective-permute-start(f32[320,128]{1,0:T(8,128)S(1)} %get-tuple-element.24.own_m_ref), channel_id=1, source_target_pairs={{0,2},{1,4},{2,0},{3,6},{4,1},{5,8},{6,3},{7,10},{8,5},{9,12},{10,... | collective-permute-start | bytes 491528 | tf_op jit(solution)/shard_map/ppermute | solution.py:352
  10.2 1.2 %collective-permute-start.4 = (f32[240,128]{1,0:T(8,128)S(1)}, f32[240,128]{1,0:T(8,128)S(1)}, u32[]{:S(2)}, u32[]{:S(2)}) collective-permute-start(f32[240,128]{1,0:T(8,128)S(1)} %get-tuple-element.26.own_h_ref), channel_id=1, source_target_pairs={{0,2},{1,4},{2,0},{3,6},{4,1},{5,8},{6,3},{7,10},{8,5},{9,12},{10,... | collective-permute-start | bytes 368648 | tf_op jit(solution)/shard_map/ppermute | solution.py:352
  11.8 0.9 %shard_map.80 = (f32[168,8,128]{2,1,0:T(8,128)S(1)}, f32[72,8,128]{2,1,0:T(8,128)S(1)}) custom-call(f32[320,128]{1,0:T(8,128)S(1)} %get-tuple-element.24.own_m_ref, f32[240,128]{1,0:T(8,128)S(1)} %get-tuple-element.26.own_h_ref, f32[320,128]{1,0:T(8,128)S(1)} %get-tuple-element.27.par_m_ref, f32[240,128]{1,0:T(8,128)S(1)} %get-tuple-element.28.par_h_ref), custom_call_target="tpu_custom_call" | custom-call | flops 1000000 | tf_op jit(solution)/shard_map/pallas_call | solution.py:29
  12.8 2.4 %collective-permute-done.4.far_h_ref = f32[240,128]{1,0:T(8,128)S(1)} collective-permute-done((f32[240,128]{1,0:T(8,128)S(1)}, f32[240,128]{1,0:T(8,128)S(1)}, u32[]{:S(2)}, u32[]{:S(2)}) %collective-permute-start.4) | collective-permute-done | bytes 122912 | tf_op jit(solution)/shard_map/ppermute | solution.py:352
  15.1 0.8 %shard_map.83 = (f32[288,128]{1,0:T(8,128)S(1)}, f32[432,128]{1,0:T(8,128)S(1)}, f32[192,128]{1,0:T(8,128)S(1)}) custom-call(f32[320,128]{1,0:T(8,128)S(1)} %collective-permute-done.1.far_m_ref, f32[240,128]{1,0:T(8,128)S(1)} %collective-permute-done.4.far_h_ref, f32[320,128]{1,0:T(8,128)S(1)} %get-tuple-element.24.own_m_ref, ...), custom_call_target="tpu_custom_call" | custom-call | flops 1000000 | tf_op jit(solution)/shard_map/pallas_call | solution.py:29
  16.2 1.6 %collective-permute-start.5 = (f32[432,128]{1,0:T(8,128)S(1)}, f32[432,128]{1,0:T(8,128)S(1)}, u32[]{:S(2)}, u32[]{:S(2)}) collective-permute-start(f32[432,128]{1,0:T(8,128)S(1)} %get-tuple-element.32.own_ref.d_ref), channel_id=1, source_target_pairs={{0,2},{1,4},{2,0},{3,6},{4,1},{5,8},{6,3},{7,10},{8,5},{9,12},{10,... | collective-permute-start | bytes 663560 | tf_op jit(solution)/shard_map/ppermute | solution.py:352
  17.8 1.0 %shard_map.84.part_ref = f32[60,8,128]{2,1,0:T(8,128)S(1)} custom-call(f32[432,128]{1,0:T(8,128)S(1)} %get-tuple-element.32.own_ref.d_ref, f32[432,128]{1,0:T(8,128)S(1)} %collective-permute-done.6.par_ref, f32[192,128]{1,0:T(8,128)S(1)} %get-tuple-element.33.st_ref), custom_call_target="tpu_custom_call" | custom-call | flops 1000000 | tf_op jit(solution)/shard_map/pallas_call | solution.py:29
  18.8 3.3 %collective-permute-done.5.far_ref = f32[432,128]{1,0:T(8,128)S(1)} collective-permute-done((f32[432,128]{1,0:T(8,128)S(1)}, f32[432,128]{1,0:T(8,128)S(1)}, u32[]{:S(2)}, u32[]{:S(2)}) %collective-permute-start.5) | collective-permute-done | bytes 221216 | tf_op jit(solution)/shard_map/ppermute | solution.py:352
  22.1 0.5 %shard_map.85 = (f32[288,128]{1,0:T(8,128)S(1)}, f32[368,128]{1,0:T(8,128)S(1)}) custom-call(f32[432,128]{1,0:T(8,128)S(1)} %collective-permute-done.5.far_ref, f32[432,128]{1,0:T(8,128)S(1)} %get-tuple-element.32.own_ref.d_ref, f32[192,128]{1,0:T(8,128)S(1)} %get-tuple-element.33.st_ref, f32[60,8,128]{2,1,0:T(8,128)S(1)} %shard_map.84.part_ref), custom_call_target="tpu_custom_call" | custom-call | flops 1000000 | tf_op jit(solution)/shard_map/pallas_call | solution.py:29
  22.8 1.6 %collective-permute-start.7 = (f32[368,128]{1,0:T(8,128)S(1)}, f32[368,128]{1,0:T(8,128)S(1)}, u32[]{:S(2)}, u32[]{:S(2)}) collective-permute-start(f32[368,128]{1,0:T(8,128)S(1)} %get-tuple-element.34.own_ref.w_ref), channel_id=1, source_target_pairs={{0,2},{1,4},{2,0},{3,6},{4,1},{5,8},{6,3},{7,10},{8,5},{9,12},{10,... | collective-permute-start | bytes 565256 | tf_op jit(solution)/shard_map/ppermute | solution.py:352
  24.9 0.9 %shard_map.86.part_ref = f32[48,8,128]{2,1,0:T(8,128)S(1)} custom-call(f32[368,128]{1,0:T(8,128)S(1)} %get-tuple-element.34.own_ref.w_ref, f32[368,128]{1,0:T(8,128)S(1)} %collective-permute-done.8.par_ref, f32[192,128]{1,0:T(8,128)S(1)} %get-tuple-element.33.st_ref), custom_call_target="tpu_custom_call" | custom-call | flops 1000000 | tf_op jit(solution)/shard_map/pallas_call | solution.py:29
  25.8 2.6 %collective-permute-done.7.far_ref = f32[368,128]{1,0:T(8,128)S(1)} collective-permute-done((f32[368,128]{1,0:T(8,128)S(1)}, f32[368,128]{1,0:T(8,128)S(1)}, u32[]{:S(2)}, u32[]{:S(2)}) %collective-permute-start.7) | collective-permute-done | bytes 188448 | tf_op jit(solution)/shard_map/ppermute | solution.py:352
  28.4 0.6 %shard_map.88 = (f32[152,128]{1,0:T(8,128)S(1)}, f32[152,128]{1,0:T(8,128)S(1)}) custom-call(f32[368,128]{1,0:T(8,128)S(1)} %collective-permute-done.7.far_ref, f32[368,128]{1,0:T(8,128)S(1)} %get-tuple-element.34.own_ref.w_ref, f32[192,128]{1,0:T(8,128)S(1)} %get-tuple-element.33.st_ref, f32[48,8,128]{2,1,0:T(8,128)S(1)} %shard_map.86.part_ref, ...), custom_call_target="tpu_custom_call" | custom-call | flops 1000000 | tf_op jit(solution)/shard_map/pallas_call | solution.py:29
  29.5 0.8 %collective-permute-done.9.kept_u_ref = f32[152,128]{1,0:T(8,128)S(1)} collective-permute-done((f32[152,128]{1,0:T(8,128)S(1)}, f32[152,128]{1,0:T(8,128)S(1)}, u32[]{:S(2)}, u32[]{:S(2)}) %collective-permute-start.9) | collective-permute-done | bytes 77856 | tf_op jit(solution)/shard_map/ppermute | solution.py:334
  30.3 1.4 %collective-permute-start.10 = (f32[8,128]{1,0:T(8,128)S(1)}, f32[8,128]{1,0:T(8,128)S(1)}, u32[]{:S(2)}, u32[]{:S(2)}) collective-permute-start(f32[8,128]{1,0:T(8,128)S(1)} %slice_add_fusion), channel_id=1, source_target_pairs={{0,3},{1,2},{2,1},{3,0},{4,7},{5,6},{6,5},{7,4},{8,11},{9,10},{10,... | collective-permute-start | bytes 12296 | tf_op jit(solution)/shard_map/ppermute | solution.py:731
  31.7 1.6 %collective-permute-done.10 = f32[8,128]{1,0:T(8,128)S(1)} collective-permute-done((f32[8,128]{1,0:T(8,128)S(1)}, f32[8,128]{1,0:T(8,128)S(1)}, u32[]{:S(2)}, u32[]{:S(2)}) %collective-permute-start.10) | collective-permute-done | bytes 4128 | tf_op jit(solution)/shard_map/ppermute | solution.py:731
  33.7 2.6 %collective-permute-done.11 = f32[8,128]{1,0:T(8,128)S(1)} collective-permute-done((f32[8,128]{1,0:T(8,128)S(1)}, f32[8,128]{1,0:T(8,128)S(1)}, u32[]{:S(2)}, u32[]{:S(2)}) %collective-permute-start.11) | collective-permute-done | bytes 4128 | tf_op jit(solution)/shard_map/ppermute | solution.py:731
  36.3 1.4 %collective-permute-start.12 = (f32[8,128]{1,0:T(8,128)S(1)}, f32[8,128]{1,0:T(8,128)S(1)}, u32[]{:S(2)}, u32[]{:S(2)}) collective-permute-start(f32[8,128]{1,0:T(8,128)S(1)} %add.14), channel_id=1, source_target_pairs={{0,9},{1,8},{4,13},{5,12},{8,1},{9,0},{12,5},{13,4},{2,11},{3,10},... | collective-permute-start | bytes 12296 | tf_op jit(solution)/shard_map/ppermute | solution.py:731
  37.7 2.5 %collective-permute-done.12 = f32[8,128]{1,0:T(8,128)S(1)} collective-permute-done((f32[8,128]{1,0:T(8,128)S(1)}, f32[8,128]{1,0:T(8,128)S(1)}, u32[]{:S(2)}, u32[]{:S(2)}) %collective-permute-start.12) | collective-permute-done | bytes 4128 | tf_op jit(solution)/shard_map/ppermute | solution.py:731
  40.3 1.4 %shard_map.89 = (f32[288,128]{1,0:T(8,128)}, f32[288,128]{1,0:T(8,128)}) custom-call(f32[8,128]{1,0:T(8,128)S(1)} %add.15.g_ref, f32[464,128]{1,0:T(8,128)S(1)} %get-tuple-element.23.s_ref.x_ref, f32[576,128]{1,0:T(8,128)S(1)} %get-tuple-element.40.mine_ref, f32[152,128]{1,0:T(8,128)S(1)} %get-tuple-element.38.mine_u_ref, ...), custom_call_target="tpu_custom_call" | custom-call | flops 100000 | tf_op jit(solution)/shard_map/pallas_call | solution.py:29
  (25 shorter events, 2.5 us)
Async XLA Ops:
  1.7 6.5 %collective-permute-start = (f32[464,128]{1,0:T(8,128)S(1)}, f32[464,128]{1,0:T(8,128)S(1)}, u32[]{:S(2)}, u32[]{:S(2)}) collective-permute-start(f32[464,128]{1,0:T(8,128)S(1)} %get-tuple-element.23.s_ref.x_ref), channel_id=1, source_target_pairs={{0,1},{1,0},{2,3},{3,2},{4,5},{5,4},{6,7},{7,6},{8,9},{9,8},{10,11... | collective-permute-start | bytes 712712 | tf_op jit(solution)/shard_map/ppermute | solution.py:334
  2.2 5.9 %collective-permute-start.2 = (f32[192,128]{1,0:T(8,128)S(1)}, f32[192,128]{1,0:T(8,128)S(1)}, u32[]{:S(2)}, u32[]{:S(2)}) collective-permute-start(f32[192,128]{1,0:T(8,128)S(1)} %get-tuple-element.25), channel_id=1, source_target_pairs={{0,2},{2,0},{1,3},{3,1},{4,6},{6,4},{5,7},{7,5},{8,10},{10,8},{9,1... | collective-permute-start | bytes 294920 | tf_op jit(solution)/shard_map/ppermute | solution.py:337
  8.2 2.0 %collective-permute-start.3 = (f32[192,128]{1,0:T(8,128)S(1)}, f32[192,128]{1,0:T(8,128)S(1)}, u32[]{:S(2)}, u32[]{:S(2)}) collective-permute-start(f32[192,128]{1,0:T(8,128)S(1)} %collective-permute-done.2.refs_0_), channel_id=1, source_target_pairs={{0,1},{1,0},{2,3},{3,2},{4,5},{5,4},{6,7},{7,6},{8,9},{9,8},{10,11... | collective-permute-start | bytes 294920 | tf_op jit(solution)/shard_map/ppermute | solution.py:334
  8.3 6.8 %collective-permute-start.1 = (f32[320,128]{1,0:T(8,128)S(1)}, f32[320,128]{1,0:T(8,128)S(1)}, u32[]{:S(2)}, u32[]{:S(2)}) collective-permute-start(f32[320,128]{1,0:T(8,128)S(1)} %get-tuple-element.24.own_m_ref), channel_id=1, source_target_pairs={{0,2},{1,4},{2,0},{3,6},{4,1},{5,8},{6,3},{7,10},{8,5},{9,12},{10,... | collective-permute-start | bytes 491528 | tf_op jit(solution)/shard_map/ppermute | solution.py:352
  10.1 1.2 %copy-start = (f32[6,16,3]{1,2,0:T(4,128)S(1)}, f32[6,16,3]{1,2,0:T(4,128)}, u32[]{:S(2)}) copy-start(f32[6,16,3]{1,2,0:T(4,128)} %param.11) | copy-start | bytes 3460
  10.1 1.2 %copy-start.1 = (s32[6,16]{1,0:T(8,128)S(1)}, s32[6,16]{1,0:T(8,128)}, u32[]{:S(2)}) copy-start(s32[6,16]{1,0:T(8,128)} %node_ref.1) | copy-start | bytes 1156
  10.2 4.9 %collective-permute-start.4 = (f32[240,128]{1,0:T(8,128)S(1)}, f32[240,128]{1,0:T(8,128)S(1)}, u32[]{:S(2)}, u32[]{:S(2)}) collective-permute-start(f32[240,128]{1,0:T(8,128)S(1)} %get-tuple-element.26.own_h_ref), channel_id=1, source_target_pairs={{0,2},{1,4},{2,0},{3,6},{4,1},{5,8},{6,3},{7,10},{8,5},{9,12},{10,... | collective-permute-start | bytes 368648 | tf_op jit(solution)/shard_map/ppermute | solution.py:352
  16.0 1.8 %collective-permute-start.6 = (f32[432,128]{1,0:T(8,128)S(1)}, f32[432,128]{1,0:T(8,128)S(1)}, u32[]{:S(2)}, u32[]{:S(2)}) collective-permute-start(f32[432,128]{1,0:T(8,128)S(1)} %get-tuple-element.32.own_ref.d_ref), channel_id=1, source_target_pairs={{0,1},{1,0},{2,3},{3,2},{4,5},{5,4},{6,7},{7,6},{8,9},{9,8},{10,11... | collective-permute-start | bytes 663560 | tf_op jit(solution)/shard_map/ppermute | solution.py:334
  16.2 5.9 %collective-permute-start.5 = (f32[432,128]{1,0:T(8,128)S(1)}, f32[432,128]{1,0:T(8,128)S(1)}, u32[]{:S(2)}, u32[]{:S(2)}) collective-permute-start(f32[432,128]{1,0:T(8,128)S(1)} %get-tuple-element.32.own_ref.d_ref), channel_id=1, source_target_pairs={{0,2},{1,4},{2,0},{3,6},{4,1},{5,8},{6,3},{7,10},{8,5},{9,12},{10,... | collective-permute-start | bytes 663560 | tf_op jit(solution)/shard_map/ppermute | solution.py:352
  22.6 2.3 %collective-permute-start.8 = (f32[368,128]{1,0:T(8,128)S(1)}, f32[368,128]{1,0:T(8,128)S(1)}, u32[]{:S(2)}, u32[]{:S(2)}) collective-permute-start(f32[368,128]{1,0:T(8,128)S(1)} %get-tuple-element.34.own_ref.w_ref), channel_id=1, source_target_pairs={{0,1},{1,0},{2,3},{3,2},{4,5},{5,4},{6,7},{7,6},{8,9},{9,8},{10,11... | collective-permute-start | bytes 565256 | tf_op jit(solution)/shard_map/ppermute | solution.py:334
  22.8 5.6 %collective-permute-start.7 = (f32[368,128]{1,0:T(8,128)S(1)}, f32[368,128]{1,0:T(8,128)S(1)}, u32[]{:S(2)}, u32[]{:S(2)}) collective-permute-start(f32[368,128]{1,0:T(8,128)S(1)} %get-tuple-element.34.own_ref.w_ref), channel_id=1, source_target_pairs={{0,2},{1,4},{2,0},{3,6},{4,1},{5,8},{6,3},{7,10},{8,5},{9,12},{10,... | collective-permute-start | bytes 565256 | tf_op jit(solution)/shard_map/ppermute | solution.py:352
  29.0 1.3 %collective-permute-start.9 = (f32[152,128]{1,0:T(8,128)S(1)}, f32[152,128]{1,0:T(8,128)S(1)}, u32[]{:S(2)}, u32[]{:S(2)}) collective-permute-start(f32[152,128]{1,0:T(8,128)S(1)} %get-tuple-element.39), channel_id=1, source_target_pairs={{0,1},{1,0},{2,3},{3,2},{4,5},{5,4},{6,7},{7,6},{8,9},{9,8},{10,11... | collective-permute-start | bytes 233480 | tf_op jit(solution)/shard_map/ppermute | solution.py:334
  29.1 11.2 %collective-permute-start.13 = (f32[576,128]{1,0:T(8,128)S(1)}, f32[576,128]{1,0:T(8,128)S(1)}, u32[]{:S(2)}, u32[]{:S(2)}) collective-permute-start(f32[576,128]{1,0:T(8,128)S(1)} %get-tuple-element.41), channel_id=1, source_target_pairs={{0,1},{1,0},{2,3},{3,2},{4,5},{5,4},{6,7},{7,6},{8,9},{9,8},{10,11... | collective-permute-start | bytes 884744 | tf_op jit(solution)/shard_map/ppermute | solution.py:334
  30.3 3.0 %collective-permute-start.10 = (f32[8,128]{1,0:T(8,128)S(1)}, f32[8,128]{1,0:T(8,128)S(1)}, u32[]{:S(2)}, u32[]{:S(2)}) collective-permute-start(f32[8,128]{1,0:T(8,128)S(1)} %slice_add_fusion), channel_id=1, source_target_pairs={{0,3},{1,2},{2,1},{3,0},{4,7},{5,6},{6,5},{7,4},{8,11},{9,10},{10,... | collective-permute-start | bytes 12296 | tf_op jit(solution)/shard_map/ppermute | solution.py:731
  33.3 3.0 %collective-permute-start.11 = (f32[8,128]{1,0:T(8,128)S(1)}, f32[8,128]{1,0:T(8,128)S(1)}, u32[]{:S(2)}, u32[]{:S(2)}) collective-permute-start(f32[8,128]{1,0:T(8,128)S(1)} %add.13), channel_id=1, source_target_pairs={{0,5},{1,4},{4,1},{5,0},{8,13},{9,12},{12,9},{13,8},{2,7},{3,6},{6... | collective-permute-start | bytes 12296 | tf_op jit(solution)/shard_map/ppermute | solution.py:731
  36.3 3.9 %collective-permute-start.12 = (f32[8,128]{1,0:T(8,128)S(1)}, f32[8,128]{1,0:T(8,128)S(1)}, u32[]{:S(2)}, u32[]{:S(2)}) collective-permute-start(f32[8,128]{1,0:T(8,128)S(1)} %add.14), channel_id=1, source_target_pairs={{0,9},{1,8},{4,13},{5,12},{8,1},{9,0},{12,5},{13,4},{2,11},{3,10},... | collective-permute-start | bytes 12296 | tf_op jit(solution)/shard_map/ppermute | solution.py:731
where the time goes:
time: 41.9 us; the launch traced here: 41.7 us
  waiting for transfers between devices  19.2 us (46%)
  starting transfers between devices  13.4 us (32%)
  Pallas kernels  8.35 us (20%)
  between operations  0.71 us (2%)
    pallas_call x13, Pallas kernels, call(): pl.pallas_call(body, out_shape=[jax.ShapeDtypeStruct(s, F32) if far_out e...  8.35 us
    ppermute x4, waiting for transfers between devices, planes_along(): return lax.ppermute(x, ('gx', 'gy', 'gz'), pairs)  8.25 us
    ppermute x3, waiting for transfers between devices, shards(): table = table + lax.ppermute(table, (axis, 'gz'), pairs)  6.81 us
    ppermute x4, starting transfers between devices, planes_along(): return lax.ppermute(x, ('gx', 'gy', 'gz'), pairs)  6.23 us
    ppermute x1, waiting for transfers between devices, rows_along(): lax.ppermute(x, 'gy', [(i, (i + step) % p.ngy) for i in range(p.ngy)])  3.39 us
    ppermute x3, starting transfers between devices, shards(): table = table + lax.ppermute(table, (axis, 'gz'), pairs)  3.18 us
    ppermute x1, starting transfers between devices, rows_along(): lax.ppermute(x, 'gy', [(i, (i + step) % p.ngy) for i in range(p.ngy)])  2.55 us
    ppermute x6, starting transfers between devices, cores(): return lax.ppermute(x, 'gz', [(i, 1 - i) for i in range(T)])  1.45 us
  transfers between devices with their start and end apart: 14, of which 8 were waited for; matrix products, arithmetic and copies ran while one was open for 0% of the time, Pallas kernels for 9%

commit v1 on v0

--- a/solution.py
+++ b/solution.py
@@ -47,7 +47,6 @@
         self.depth = (self.tiles * self.width, self.ngy * self.rows)
         self.r0 = self.rows + 6
         self.main = up8((self.fields + 2) * self.rows)
-        self.halo = up8((self.fields + 2) * 6)
 
     def per(self, count):
         return up8(self.fields * count)
@@ -260,12 +259,13 @@
     z_load = n_raw
     z_stat = z_load + FL * Y
     z_rows = z_stat + 2 * Q * Y
-    y_load = Q * FL * 3
-    y_stat = y_load + Q * FL * 2
-    y_rows = up8(y_stat + Q * 6)
+    y_stat = FL * 3
+    y_load = y_stat + 6
+    y_part = up8(y_load + FL * 2)
+    d_part = up8(y_load)
     R0, R1, R2 = Y + 6, Y + 4, Y + 2
     N1, N2, N3 = p.per(R1), p.per(R2), p.per(Y)
-    M, H = p.main, p.halo
+    M = p.main
     both = p.ngy == 2
 
     x0 = start.reshape(n_raw, W)
@@ -274,7 +274,7 @@
     su = supports.reshape(Q * Y, W)
 
     def gather_body(x_hbm, b_hbm, d_hbm, s_hbm, z_ref, b_ref, *refs):
-        y_refs, (d_ref, s_ref, sems) = refs[:-3], refs[-3:]
+        d_ref, s_ref, sems = refs
         core = lax.axis_index("gz")
         moves = [
             pltpu.make_async_copy(src, dst, sems.at[i])
@@ -291,39 +291,16 @@
         )
         moves[3].wait()
         z_ref[z_stat + Q * Y : z_rows, :] = 1.0 - s_ref[...].astype(F32)
-        if both:
-            first = lax.axis_index("gy") == 0
-            froms = [(jnp.where(first, Y - 3, 0), jnp.where(first, Y - 2, 0))]
-        else:
-            froms = [(Y - 3, Y - 2), (0, 0)]
-        for y_ref, (three, _) in zip(y_refs, froms):
-            if y_rows > y_stat + Q * 6:
-                y_ref[y_stat + Q * 6 : y_rows, :] = jnp.zeros((y_rows - y_stat - Q * 6, W), F32)
-            for q in range(Q):
-                for kind in range(2):
-                    for r in range(3):
-                        at = y_stat + q * 6 + kind * 3 + r
-                        y_ref[at : at + 1, :] = z_ref[pl.ds(z_stat + (kind * Q + q) * Y + three + r, 1), :]
-        moves[0].wait()
-        for y_ref, (three, _) in zip(y_refs, froms):
-            for q in range(Q):
-                for comp in range(D):
-                    for r in range(3):
-                        p.put(y_ref, q * FL * 3, 3, comp, r, p.raw(z_ref, 0, comp, q, three + r))
         moves[1].wait()
-        for y_ref, (_, two) in zip(y_refs, froms):
-            for q in range(Q):
-                for comp in range(D):
-                    for r in range(2):
-                        p.put(y_ref, y_load + q * FL * 2, 2, comp, r, p.raw(b_ref, 0, comp, q, two + r))
         for f in range(FL):
             z_ref[z_load + f * Y : z_load + (f + 1) * Y, :] = b_ref[
                 pl.ds(pl.multiple_of((f * Q + 1 - core) * Y, 8), Y), :
             ]
-
-    z_msg, b_near, *y_msgs = call(
+        moves[0].wait()
+
+    z_msg, b_near = call(
         gather_body,
-        [(z_rows, W), (n_raw, W)] + [(y_rows, W)] * (1 if both else 2),
+        [(z_rows, W), (n_raw, W)],
         [x0, bl, de, su],
         [VMEM((Q * Y, W), jnp.int32), VMEM((Q * Y, W), jnp.int32), pltpu.SemaphoreType.DMA((4,))],
         flops=10**5,
@@ -336,31 +313,57 @@
     def rows_along(x, step):
         return lax.ppermute(x, "gy", [(i, (i + step) % p.ngy) for i in range(p.ngy)])
 
-    def planes_along(x):
+    def planes_along(x, step=0):
         pairs = []
         for i in range(p.ngx):
             for j in range(p.ngy):
                 for k in range(T):
                     to = i + 2 * k - 1
                     mine = (i * p.ngy + j) * T + k
+                    row = (j + step) % p.ngy
                     if 0 <= to < p.ngx:
-                        pairs.append((mine, (to * p.ngy + j) * T + 1 - k))
+                        pairs.append((mine, (to * p.ngy + row) * T + 1 - k))
+                    elif step:
+                        pairs.append((mine, (i * p.ngy + row) * T + k))
                     elif p.ngy % 2 == 0:
                         pairs.append((mine, (i * p.ngy + (j ^ 1)) * T + k))
                     else:
                         pairs.append((mine, mine))
         return lax.ppermute(x, ("gx", "gy", "gz"), pairs)
 
-    if both:
-        y_got = [rows_along(y_msgs[0], 1)]
-    else:
-        y_got = [rows_along(y_msgs[0], 1), rows_along(y_msgs[1], -1)]
     z_got = cores(z_msg)
-    zy_got = [cores(y) for y in y_got]
-    halos = len(y_got)
-
-    def main_body(s_ref, z_ref, own_ref, par_ref):
+
+    def main_body(s_ref, z_ref, b_ref, own_ref, par_ref, *y_refs):
         core = lax.axis_index("gz")
+        if both:
+            first = lax.axis_index("gy") == 0
+            froms = [(jnp.where(first, Y - 3, 0), jnp.where(first, Y - 2, 0))]
+        else:
+            froms = [(Y - 3, Y - 2), (0, 0)]
+        count = len(froms)
+        for y_ref, d_ref, (three, two) in zip(y_refs[:count], y_refs[count:], froms):
+            for src, half in ((s_ref, core), (z_ref, 1 - core)):
+                at, to = half * y_part, half * d_part
+                for comp in range(D):
+                    for r in range(3):
+                        v = p.raw(src, 0, comp, core, three + r)
+                        p.put(y_ref, at, 3, comp, r, v)
+                        p.put(d_ref, to, 3, comp, r, v)
+                    for r in range(2):
+                        if src is s_ref:
+                            v = p.raw(b_ref, 0, comp, core, two + r)
+                        else:
+                            v = p.tile(src, z_load, Y, comp, two + r)
+                        p.put(y_ref, at + y_load, 2, comp, r, v)
+                for kind in range(2):
+                    for r in range(3):
+                        v = src[pl.ds(z_stat + (kind * Q + core) * Y + three + r, 1), :]
+                        y_ref[pl.ds(at + y_stat + kind * 3 + r, 1), :] = v
+                        d_ref[pl.ds(to + y_stat + kind * 3 + r, 1), :] = v
+            for t in range(T):
+                for ref, part, used in ((y_ref, y_part, y_load + FL * 2), (d_ref, d_part, y_load)):
+                    if part > used:
+                        ref[t * part + used : (t + 1) * part, :] = jnp.zeros((part - used, W), F32)
         for out, plane in ((own_ref, core), (par_ref, 1 - core)):
             for src, half in ((s_ref, core), (z_ref, 1 - core)):
                 base = half * M
@@ -372,49 +375,49 @@
                         pl.ds(pl.multiple_of(z_stat + (kind * Q + plane) * Y, 8), Y), :
                     ]
 
-    own_m, par_m = call(main_body, [(T * M, W)] * 2, [z_msg, z_got], flops=10**5)
+    ways = (1,) if both else (1, -1)
+    halos = len(ways)
+    own_m, par_m, *sent = call(
+        main_body,
+        [(T * M, W)] * 2 + [(T * y_part, W)] * halos + [(T * d_part, W)] * halos,
+        [z_msg, z_got, b_near],
+        flops=10**5,
+    )
+    y_got = [rows_along(x, step) for x, step in zip(sent, ways)]
     far_m = planes_along(own_m)
-
-    def halo_body(*refs):
-        y_refs, zy_refs = refs[:halos], refs[halos : 2 * halos]
-        own_ref, par_ref = refs[2 * halos :]
-        core = lax.axis_index("gz")
+    far_y = [planes_along(x, step) for x, step in zip(sent[halos:], ways)]
+    par_y = [cores(x) for x in y_got]
+
+    def halo(main, refs, part):
         row = lax.axis_index("gy")
         below = jnp.where(row > 0, 1.0, 0.0)
         above = jnp.where(row < p.ngy - 1, 1.0, 0.0)
-        for out, plane in ((own_ref, core), (par_ref, 1 - core)):
-            for ys, half in ((y_refs, core), (zy_refs, 1 - core)):
-                base = half * H
-                for r in range(6):
-                    src, flag = (ys[0], below) if r < 3 else (ys[-1], above)
-                    for comp in range(D):
-                        p.put(out, base, 6, comp, r, p.tile(src, plane * (FL * 3), 3, comp, r % 3))
-                    for kind in range(2):
-                        v = src[pl.ds(y_stat + plane * 6 + kind * 3 + r % 3, 1), :]
-                        out[pl.ds(base + (FL + kind) * 6 + r, 1), :] = v * flag
-
-    own_h, par_h = call(halo_body, [(T * H, W)] * 2, y_got + zy_got, flops=10**5)
-    far_h = planes_along(own_h)
+        return main, refs[0], refs[-1], part, below, above
 
     def field_at(refs, t, comp, r):
-        main, halo = refs
+        main, low, high, part, _, _ = refs
         if 3 <= r < Y + 3:
             return p.tile(main, t * M, Y, comp, r - 3)
-        return p.tile(halo, t * H, 6, comp, r if r < 3 else r - Y)
+        if r < 3:
+            return p.tile(low, t * part, 3, comp, r)
+        return p.tile(high, t * part, 3, comp, r - Y - 3)
 
     def const_at(refs, kind, t, r):
-        main, halo = refs
+        main, low, high, part, below, above = refs
         if 3 <= r < Y + 3:
             at = t * M + (FL + kind) * Y + r - 3
             return main[at : at + 1, :]
-        at = t * H + (FL + kind) * 6 + (r if r < 3 else r - Y)
-        return halo[at : at + 1, :]
+        at = t * part + y_stat + kind * 3
+        if r < 3:
+            return low[at + r : at + r + 1, :] * below
+        at += r - Y - 3
+        return high[at : at + 1, :] * above
 
     def const_parts(refs, kind, t):
-        main, halo = refs
-        at = t * H + (FL + kind) * 6
+        main, low, high, part, below, above = refs
+        at = t * part + y_stat + kind * 3
         to = t * M + (FL + kind) * Y
-        return halo[at : at + 3, :], main[to : to + Y, :], halo[at + 3 : at + 6, :]
+        return low[at : at + 3, :] * below, main[to : to + Y, :], high[at : at + 3, :] * above
 
     def points_body(node_ref, value_ref, out):
         core = lax.axis_index("gz")
@@ -459,36 +462,35 @@
     )
 
     def loads_body(p_ref, b_ref, z_ref, *refs):
-        y_refs, zy_refs = refs[:halos], refs[halos : 2 * halos]
-        out = refs[2 * halos]
+        ys, out = refs[:halos], refs[halos]
         core = lax.axis_index("gz")
         for half in range(2):
             t = core if half == 0 else 1 - core
-            ys = y_refs if half == 0 else zy_refs
             for comp in range(D):
                 for r in range(R1):
                     if r < 2:
-                        v = p.tile(ys[0], y_load + core * (FL * 2), 2, comp, r)
+                        v = p.tile(ys[0], t * y_part + y_load, 2, comp, r)
                     elif r < Y + 2:
                         if half == 0:
                             v = p.raw(b_ref, 0, comp, core, r - 2)
                         else:
                             v = p.tile(z_ref, z_load, Y, comp, r - 2)
                     else:
-                        v = p.tile(ys[-1], y_load + core * (FL * 2), 2, comp, r - Y - 2)
+                        v = p.tile(ys[-1], t * y_part + y_load, 2, comp, r - Y - 2)
                     at = t * (D * R1) + comp * R1 + r
                     out[at, 0:C, :] = v + p_ref[pl.ds(pl.multiple_of(at * 8, 8), C), :]
 
     (loaded,) = call(
         loads_body,
         [(T * D * R1, 8, W)],
-        [points, b_near, z_got] + y_got + zy_got,
+        [points, b_near, z_got] + y_got,
         flops=10**6,
     )
 
-    def near_start_body(own_m_ref, own_h_ref, par_m_ref, par_h_ref, modes_ref, part_ref, other_ref):
+    def near_start_body(own_m_ref, par_m_ref, *refs):
+        modes_ref, part_ref, other_ref = refs[2 * halos :]
         core, sign = place()
-        own, par = (own_m_ref, own_h_ref), (par_m_ref, par_h_ref)
+        own, par = halo(own_m_ref, refs[:halos], y_part), halo(par_m_ref, refs[halos : 2 * halos], y_part)
         for refs, out in ((own, modes_ref), (par, other_ref)):
             modes_z(
                 p,
@@ -513,17 +515,16 @@
     modes, part = call(
         near_start_body,
         [field_shapes(R0), (D * R1 * T, 8, W)],
-        [own_m, own_h, par_m, par_h],
+        [own_m, par_m] + y_got + par_y,
         [field_shapes(R0)],
         flops=10**6,
     )
 
-    def far_start_body(
-        far_m_ref, far_h_ref, own_m_ref, own_h_ref, par_m_ref, par_h_ref, modes_ref, part_ref, load_ref,
-        r_ref, d_ref, st_ref, other_ref,
-    ):
+    def far_start_body(far_m_ref, own_m_ref, par_m_ref, modes_ref, part_ref, load_ref, *refs):
+        r_ref, d_ref, st_ref, other_ref = refs[3 * halos :]
         core, sign = place()
-        far, own, par = (far_m_ref, far_h_ref), (own_m_ref, own_h_ref), (par_m_ref, par_h_ref)
+        own, par = halo(own_m_ref, refs[:halos], y_part), halo(par_m_ref, refs[halos : 2 * halos], y_part)
+        far = halo(far_m_ref, refs[2 * halos : 3 * halos], d_part)
         column = lax.axis_index("gx")
         inside = jnp.where(core == 0, column > 0, column < p.ngx - 1)
         valid = jnp.where(inside, 1.0, 0.0)
@@ -581,7 +582,7 @@
     res0, dir0, consts = call(
         far_start_body,
         [(T * N3, W), (T * N1, W), (6 * T * up8(R0), W)],
-        [far_m, far_h, own_m, own_h, par_m, par_h, modes, part, loaded],
+        [far_m, own_m, par_m, modes, part, loaded] + y_got + par_y + far_y,
         [field_shapes(R0)],
         flops=10**6,
     )
@@ -721,15 +722,24 @@
     kept_u = cores(send_u)
 
     table = mine_u[N3 : N3 + 8, :] + kept_u[N3 : N3 + 8, :]
+
+    def crossed(x, axis, size, step):
+        pairs = [(i * T + k, (i ^ step) * T + 1 - k) for i in range(size) for k in range(T)]
+        return lax.ppermute(x, (axis, "gz"), pairs)
+
     for axis, size in (("gy", p.ngy), ("gx", p.ngx)):
         if size & (size - 1):
             table = lax.psum(table, axis)
             continue
         step = 1
         while step < size:
-            pairs = [(i * T + k, (i ^ step) * T + 1 - k) for i in range(size) for k in range(T)]
-            table = table + lax.ppermute(table, (axis, "gz"), pairs)
-            step *= 2
+            if step * 2 < size:
+                one, two, three = (crossed(table, axis, size, step * k) for k in (1, 2, 3))
+                table = (table + one) + (two + three)
+                step *= 4
+            else:
+                table = table + crossed(table, axis, size, step)
+                step *= 2
 
     def final_body(
         g_ref, x_ref, mine_ref, mine_u_ref, kept_ref, kept_u_ref, out_hbm, res_hbm, a_ref, out_ref, res_ref, sems

time: 41.9 us -> 41.2 us (0.983)
  waiting for transfers between devices: 19.2 us -> 16.2 us
  starting transfers between devices: 13.4 us -> 15.7 us
    ppermute x3 -> x4, waiting for transfers between devices: 6.81 us -> 4.5 us  [crossed(): return lax.ppermute(x, (axis, 'gz'), pairs)]
    ppermute x3 -> x4, starting transfers between devices: 3.18 us -> 5.37 us  [crossed(): return lax.ppermute(x, (axis, 'gz'), pairs)]
    ppermute x4, waiting for transfers between devices: 8.25 us -> 6.75 us  [planes_along(): return lax.ppermute(x, ('gx', 'gy', 'gz'), pairs)]
    ppermute x6, waiting for transfers between devices: 0.77 us -> 1.9 us  [cores(): return lax.ppermute(x, 'gz', [(i, 1 - i) for i in range(T)])]
    ppermute x4, starting transfers between devices: 6.23 us -> 5.36 us  [planes_along(): return lax.ppermute(x, ('gx', 'gy', 'gz'), pairs)]
    ppermute x6, starting transfers between devices: 1.45 us -> 2.05 us  [cores(): return lax.ppermute(x, 'gz', [(i, 1 - i) for i in range(T)])]
    pallas_call x13 -> x12, Pallas kernels: 8.35 us -> 8.38 us  [call(): pl.pallas_call(body, out_shape=[jax.ShapeDtypeStruct(s, F32) if far_out e...]
  transfers between devices with their start and end apart: 14 -> 15, of which waited for: 8 -> 9; matrix products, arithmetic and copies ran while one was open for 0% -> 0% of each run, Pallas kernels for 9% -> 9%
where the time goes in v1:
time: 41.2 us; the launch traced here: 41 us
  waiting for transfers between devices  16.2 us (39%)
  starting transfers between devices  15.7 us (38%)
  Pallas kernels  8.38 us (20%)
  between operations  0.73 us (2%)
    pallas_call x12, Pallas kernels, call(): pl.pallas_call(body, out_shape=[jax.ShapeDtypeStruct(s, F32) if far_out e...  8.38 us
    ppermute x4, waiting for transfers between devices, planes_along(): return lax.ppermute(x, ('gx', 'gy', 'gz'), pairs)  6.75 us
    ppermute x4, starting transfers between devices, crossed(): return lax.ppermute(x, (axis, 'gz'), pairs)  5.37 us
    ppermute x4, starting transfers between devices, planes_along(): return lax.ppermute(x, ('gx', 'gy', 'gz'), pairs)  5.36 us
    ppermute x4, waiting for transfers between devices, crossed(): return lax.ppermute(x, (axis, 'gz'), pairs)  4.5 us
    ppermute x1, waiting for transfers between devices, rows_along(): lax.ppermute(x, 'gy', [(i, (i + step) % p.ngy) for i in range(p.ngy)])  3.02 us
    ppermute x1, starting transfers between devices, rows_along(): lax.ppermute(x, 'gy', [(i, (i + step) % p.ngy) for i in range(p.ngy)])  2.91 us
    ppermute x6, starting transfers between devices, cores(): return lax.ppermute(x, 'gz', [(i, 1 - i) for i in range(T)])  2.05 us
  transfers between devices with their start and end apart: 15, of which 9 were waited for; matrix products, arithmetic and copies ran while one was open for 0% of the time, Pallas kernels for 9%

profile of v1, /device:TPU:0, one launch (start us, length us, event | category | flops | bytes accessed | tf_op | source)
XLA Modules:
  0.0 41.0 jit_solution(2008005703161358264)
XLA Ops:
  0.6 1.0 %shard_map.77 = (f32[464,128]{1,0:T(8,128)S(1)}, f32[288,128]{1,0:T(8,128)S(1)}) custom-call(f32[288,128]{1,0:T(8,128)} %bitcast.8, f32[288,128]{1,0:T(8,128)} %bitcast.9, s32[16,128]{1,0:T(8,128)} %bitcast.10, s32[16,128]{1,0:T(8,128)} %bitcast.11), custom_call_target="tpu_custom_call" | custom-call | flops 100000 | tf_op jit(solution)/shard_map/pallas_call | solution.py:29
  2.2 1.1 %collective-permute-done.z_ref = f32[464,128]{1,0:T(8,128)S(1)} collective-permute-done((f32[464,128]{1,0:T(8,128)S(1)}, f32[464,128]{1,0:T(8,128)S(1)}, u32[]{:S(2)}, u32[]{:S(2)}) %collective-permute-start) | collective-permute-done | bytes 237600 | tf_op jit(solution)/shard_map/ppermute | solution.py:311
  3.5 2.9 %collective-permute-start.2 = (f32[192,128]{1,0:T(8,128)S(1)}, f32[192,128]{1,0:T(8,128)S(1)}, u32[]{:S(2)}, u32[]{:S(2)}) collective-permute-start(f32[192,128]{1,0:T(8,128)S(1)} %get-tuple-element.26), channel_id=1, source_target_pairs={{0,2},{2,0},{1,3},{3,1},{4,6},{6,4},{5,7},{7,5},{8,10},{10,8},{9,1... | collective-permute-start | bytes 294920 | tf_op jit(solution)/shard_map/ppermute | solution.py:314
  6.5 3.0 %collective-permute-done.2.refs_0_ = f32[192,128]{1,0:T(8,128)S(1)} collective-permute-done((f32[192,128]{1,0:T(8,128)S(1)}, f32[192,128]{1,0:T(8,128)S(1)}, u32[]{:S(2)}, u32[]{:S(2)}) %collective-permute-start.2) | collective-permute-done | bytes 98336 | tf_op jit(solution)/shard_map/ppermute | solution.py:314
  9.6 1.7 %collective-permute-start.4 = (f32[128,128]{1,0:T(8,128)S(1)}, f32[128,128]{1,0:T(8,128)S(1)}, u32[]{:S(2)}, u32[]{:S(2)}) collective-permute-start(f32[128,128]{1,0:T(8,128)S(1)} %get-tuple-element.29), channel_id=1, source_target_pairs={{0,2},{1,6},{2,0},{3,4},{4,3},{5,10},{6,1},{7,8},{8,7},{9,14},{10,... | collective-permute-start | bytes 196616 | tf_op jit(solution)/shard_map/ppermute | solution.py:332
  11.9 0.8 %shard_map.79 = (f32[168,8,128]{2,1,0:T(8,128)S(1)}, f32[72,8,128]{2,1,0:T(8,128)S(1)}) custom-call(f32[320,128]{1,0:T(8,128)S(1)} %get-tuple-element.24.own_m_ref, f32[320,128]{1,0:T(8,128)S(1)} %get-tuple-element.25.par_m_ref, f32[192,128]{1,0:T(8,128)S(1)} %collective-permute-done.2.refs_0_, f32[192,128]{1,0:T(8,128)S(1)} %collective-permute-done.3.refs_1_), custom_call_target="tpu_custom_call" | custom-call | flops 1000000 | tf_op jit(solution)/shard_map/pallas_call | solution.py:29
  12.7 1.1 %collective-permute-done.4.refs_2_ = f32[128,128]{1,0:T(8,128)S(1)} collective-permute-done((f32[128,128]{1,0:T(8,128)S(1)}, f32[128,128]{1,0:T(8,128)S(1)}, u32[]{:S(2)}, u32[]{:S(2)}) %collective-permute-start.4) | collective-permute-done | bytes 65568 | tf_op jit(solution)/shard_map/ppermute | solution.py:332
  13.8 0.8 %shard_map.82 = (f32[288,128]{1,0:T(8,128)S(1)}, f32[432,128]{1,0:T(8,128)S(1)}, f32[192,128]{1,0:T(8,128)S(1)}) custom-call(f32[320,128]{1,0:T(8,128)S(1)} %collective-permute-done.1.far_m_ref, f32[320,128]{1,0:T(8,128)S(1)} %get-tuple-element.24.own_m_ref, f32[320,128]{1,0:T(8,128)S(1)} %get-tuple-element.25.par_m_ref, ...), custom_call_target="tpu_custom_call" | custom-call | flops 1000000 | tf_op jit(solution)/shard_map/pallas_call | solution.py:29
  14.7 0.9 %collective-permute-start.6 = (f32[432,128]{1,0:T(8,128)S(1)}, f32[432,128]{1,0:T(8,128)S(1)}, u32[]{:S(2)}, u32[]{:S(2)}) collective-permute-start(f32[432,128]{1,0:T(8,128)S(1)} %get-tuple-element.30.own_ref.d_ref), channel_id=1, source_target_pairs={{0,1},{1,0},{2,3},{3,2},{4,5},{5,4},{6,7},{7,6},{8,9},{9,8},{10,11... | collective-permute-start | bytes 663560 | tf_op jit(solution)/shard_map/ppermute | solution.py:311
  15.6 1.7 %collective-permute-start.5 = (f32[432,128]{1,0:T(8,128)S(1)}, f32[432,128]{1,0:T(8,128)S(1)}, u32[]{:S(2)}, u32[]{:S(2)}) collective-permute-start(f32[432,128]{1,0:T(8,128)S(1)} %get-tuple-element.30.own_ref.d_ref), channel_id=1, source_target_pairs={{0,2},{1,4},{2,0},{3,6},{4,1},{5,8},{6,3},{7,10},{8,5},{9,12},{10,... | collective-permute-start | bytes 663560 | tf_op jit(solution)/shard_map/ppermute | solution.py:332
  17.3 1.0 %shard_map.83.part_ref = f32[60,8,128]{2,1,0:T(8,128)S(1)} custom-call(f32[432,128]{1,0:T(8,128)S(1)} %get-tuple-element.30.own_ref.d_ref, f32[432,128]{1,0:T(8,128)S(1)} %collective-permute-done.6.par_ref, f32[192,128]{1,0:T(8,128)S(1)} %get-tuple-element.31.st_ref), custom_call_target="tpu_custom_call" | custom-call | flops 1000000 | tf_op jit(solution)/shard_map/pallas_call | solution.py:29
  18.3 3.2 %collective-permute-done.5.far_ref = f32[432,128]{1,0:T(8,128)S(1)} collective-permute-done((f32[432,128]{1,0:T(8,128)S(1)}, f32[432,128]{1,0:T(8,128)S(1)}, u32[]{:S(2)}, u32[]{:S(2)}) %collective-permute-start.5) | collective-permute-done | bytes 221216 | tf_op jit(solution)/shard_map/ppermute | solution.py:332
  22.1 1.8 %collective-permute-start.7 = (f32[368,128]{1,0:T(8,128)S(1)}, f32[368,128]{1,0:T(8,128)S(1)}, u32[]{:S(2)}, u32[]{:S(2)}) collective-permute-start(f32[368,128]{1,0:T(8,128)S(1)} %get-tuple-element.32.own_ref.w_ref), channel_id=1, source_target_pairs={{0,2},{1,4},{2,0},{3,6},{4,1},{5,8},{6,3},{7,10},{8,5},{9,12},{10,... | collective-permute-start | bytes 565256 | tf_op jit(solution)/shard_map/ppermute | solution.py:332
  24.4 0.9 %shard_map.85.part_ref = f32[48,8,128]{2,1,0:T(8,128)S(1)} custom-call(f32[368,128]{1,0:T(8,128)S(1)} %get-tuple-element.32.own_ref.w_ref, f32[368,128]{1,0:T(8,128)S(1)} %collective-permute-done.8.par_ref, f32[192,128]{1,0:T(8,128)S(1)} %get-tuple-element.31.st_ref), custom_call_target="tpu_custom_call" | custom-call | flops 1000000 | tf_op jit(solution)/shard_map/pallas_call | solution.py:29
  25.2 2.5 %collective-permute-done.7.far_ref = f32[368,128]{1,0:T(8,128)S(1)} collective-permute-done((f32[368,128]{1,0:T(8,128)S(1)}, f32[368,128]{1,0:T(8,128)S(1)}, u32[]{:S(2)}, u32[]{:S(2)}) %collective-permute-start.7) | collective-permute-done | bytes 188448 | tf_op jit(solution)/shard_map/ppermute | solution.py:332
  27.7 0.6 %shard_map.87 = (f32[152,128]{1,0:T(8,128)S(1)}, f32[152,128]{1,0:T(8,128)S(1)}) custom-call(f32[368,128]{1,0:T(8,128)S(1)} %collective-permute-done.7.far_ref, f32[368,128]{1,0:T(8,128)S(1)} %get-tuple-element.32.own_ref.w_ref, f32[192,128]{1,0:T(8,128)S(1)} %get-tuple-element.31.st_ref, f32[48,8,128]{2,1,0:T(8,128)S(1)} %shard_map.85.part_ref, ...), custom_call_target="tpu_custom_call" | custom-call | flops 1000000 | tf_op jit(solution)/shard_map/pallas_call | solution.py:29
  28.9 0.8 %collective-permute-done.9.kept_u_ref = f32[152,128]{1,0:T(8,128)S(1)} collective-permute-done((f32[152,128]{1,0:T(8,128)S(1)}, f32[152,128]{1,0:T(8,128)S(1)}, u32[]{:S(2)}, u32[]{:S(2)}) %collective-permute-start.9) | collective-permute-done | bytes 77856 | tf_op jit(solution)/shard_map/ppermute | solution.py:311
  29.6 1.5 %collective-permute-start.10 = (f32[8,128]{1,0:T(8,128)S(1)}, f32[8,128]{1,0:T(8,128)S(1)}, u32[]{:S(2)}, u32[]{:S(2)}) collective-permute-start(f32[8,128]{1,0:T(8,128)S(1)} %slice_add_fusion), channel_id=1, source_target_pairs={{0,3},{1,2},{2,1},{3,0},{4,7},{5,6},{6,5},{7,4},{8,11},{9,10},{10,... | collective-permute-start | bytes 12296 | tf_op jit(solution)/shard_map/ppermute | solution.py:728
  31.1 1.5 %collective-permute-done.10 = f32[8,128]{1,0:T(8,128)S(1)} collective-permute-done((f32[8,128]{1,0:T(8,128)S(1)}, f32[8,128]{1,0:T(8,128)S(1)}, u32[]{:S(2)}, u32[]{:S(2)}) %collective-permute-start.10) | collective-permute-done | bytes 4128 | tf_op jit(solution)/shard_map/ppermute | solution.py:728
  32.7 2.9 %collective-permute-start.13 = (f32[8,128]{1,0:T(8,128)S(1)}, f32[8,128]{1,0:T(8,128)S(1)}, u32[]{:S(2)}, u32[]{:S(2)}) collective-permute-start(f32[8,128]{1,0:T(8,128)S(1)} %add.16), channel_id=1, source_target_pairs={{0,13},{1,12},{4,9},{5,8},{8,5},{9,4},{12,1},{13,0},{2,15},{3,14},... | collective-permute-start | bytes 12296 | tf_op jit(solution)/shard_map/ppermute | solution.py:728
  35.6 1.0 %collective-permute-start.11 = (f32[8,128]{1,0:T(8,128)S(1)}, f32[8,128]{1,0:T(8,128)S(1)}, u32[]{:S(2)}, u32[]{:S(2)}) collective-permute-start(f32[8,128]{1,0:T(8,128)S(1)} %add.16), channel_id=1, source_target_pairs={{0,5},{1,4},{4,1},{5,0},{8,13},{9,12},{12,9},{13,8},{2,7},{3,6},{6... | collective-permute-start | bytes 12296 | tf_op jit(solution)/shard_map/ppermute | solution.py:728
  36.6 1.0 %collective-permute-done.13 = f32[8,128]{1,0:T(8,128)S(1)} collective-permute-done((f32[8,128]{1,0:T(8,128)S(1)}, f32[8,128]{1,0:T(8,128)S(1)}, u32[]{:S(2)}, u32[]{:S(2)}) %collective-permute-start.13) | collective-permute-done | bytes 4128 | tf_op jit(solution)/shard_map/ppermute | solution.py:728
  37.5 2.0 %collective-permute-done.12 = f32[8,128]{1,0:T(8,128)S(1)} collective-permute-done((f32[8,128]{1,0:T(8,128)S(1)}, f32[8,128]{1,0:T(8,128)S(1)}, u32[]{:S(2)}, u32[]{:S(2)}) %collective-permute-start.12) | collective-permute-done | bytes 4128 | tf_op jit(solution)/shard_map/ppermute | solution.py:728
  39.5 1.5 %shard_map.88 = (f32[288,128]{1,0:T(8,128)}, f32[288,128]{1,0:T(8,128)}) custom-call(f32[8,128]{1,0:T(8,128)S(1)} %add_add_fusion.g_ref, f32[464,128]{1,0:T(8,128)S(1)} %get-tuple-element.22.s_ref.x_ref, f32[576,128]{1,0:T(8,128)S(1)} %get-tuple-element.38.mine_ref, f32[152,128]{1,0:T(8,128)S(1)} %get-tuple-element.36.mine_u_ref, ...), custom_call_target="tpu_custom_call" | custom-call | flops 100000 | tf_op jit(solution)/shard_map/pallas_call | solution.py:29
  (25 shorter events, 3.0 us)
Async XLA Ops:
  1.7 1.7 %collective-permute-start = (f32[464,128]{1,0:T(8,128)S(1)}, f32[464,128]{1,0:T(8,128)S(1)}, u32[]{:S(2)}, u32[]{:S(2)}) collective-permute-start(f32[464,128]{1,0:T(8,128)S(1)} %get-tuple-element.22.s_ref.x_ref), channel_id=1, source_target_pairs={{0,1},{1,0},{2,3},{3,2},{4,5},{5,4},{6,7},{7,6},{8,9},{9,8},{10,11... | collective-permute-start | bytes 712712 | tf_op jit(solution)/shard_map/ppermute | solution.py:311
  3.4 7.9 %copy-start = (f32[6,16,3]{1,2,0:T(4,128)S(1)}, f32[6,16,3]{1,2,0:T(4,128)}, u32[]{:S(2)}) copy-start(f32[6,16,3]{1,2,0:T(4,128)} %param.11) | copy-start | bytes 3460
  3.5 7.8 %copy-start.1 = (s32[6,16]{1,0:T(8,128)S(1)}, s32[6,16]{1,0:T(8,128)}, u32[]{:S(2)}) copy-start(s32[6,16]{1,0:T(8,128)} %node_ref.1) | copy-start | bytes 1156
  3.5 6.0 %collective-permute-start.2 = (f32[192,128]{1,0:T(8,128)S(1)}, f32[192,128]{1,0:T(8,128)S(1)}, u32[]{:S(2)}, u32[]{:S(2)}) collective-permute-start(f32[192,128]{1,0:T(8,128)S(1)} %get-tuple-element.26), channel_id=1, source_target_pairs={{0,2},{2,0},{1,3},{3,1},{4,6},{6,4},{5,7},{7,5},{8,10},{10,8},{9,1... | collective-permute-start | bytes 294920 | tf_op jit(solution)/shard_map/ppermute | solution.py:314
  6.5 7.4 %collective-permute-start.1 = (f32[320,128]{1,0:T(8,128)S(1)}, f32[320,128]{1,0:T(8,128)S(1)}, u32[]{:S(2)}, u32[]{:S(2)}) collective-permute-start(f32[320,128]{1,0:T(8,128)S(1)} %get-tuple-element.24.own_m_ref), channel_id=1, source_target_pairs={{0,2},{1,4},{2,0},{3,6},{4,1},{5,8},{6,3},{7,10},{8,5},{9,12},{10,... | collective-permute-start | bytes 491528 | tf_op jit(solution)/shard_map/ppermute | solution.py:332
  9.6 2.3 %collective-permute-start.3 = (f32[192,128]{1,0:T(8,128)S(1)}, f32[192,128]{1,0:T(8,128)S(1)}, u32[]{:S(2)}, u32[]{:S(2)}) collective-permute-start(f32[192,128]{1,0:T(8,128)S(1)} %collective-permute-done.2.refs_0_), channel_id=1, source_target_pairs={{0,1},{1,0},{2,3},{3,2},{4,5},{5,4},{6,7},{7,6},{8,9},{9,8},{10,11... | collective-permute-start | bytes 294920 | tf_op jit(solution)/shard_map/ppermute | solution.py:311
  9.6 4.3 %collective-permute-start.4 = (f32[128,128]{1,0:T(8,128)S(1)}, f32[128,128]{1,0:T(8,128)S(1)}, u32[]{:S(2)}, u32[]{:S(2)}) collective-permute-start(f32[128,128]{1,0:T(8,128)S(1)} %get-tuple-element.29), channel_id=1, source_target_pairs={{0,2},{1,6},{2,0},{3,4},{4,3},{5,10},{6,1},{7,8},{8,7},{9,14},{10,... | collective-permute-start | bytes 196616 | tf_op jit(solution)/shard_map/ppermute | solution.py:332
  14.7 2.6 %collective-permute-start.6 = (f32[432,128]{1,0:T(8,128)S(1)}, f32[432,128]{1,0:T(8,128)S(1)}, u32[]{:S(2)}, u32[]{:S(2)}) collective-permute-start(f32[432,128]{1,0:T(8,128)S(1)} %get-tuple-element.30.own_ref.d_ref), channel_id=1, source_target_pairs={{0,1},{1,0},{2,3},{3,2},{4,5},{5,4},{6,7},{7,6},{8,9},{9,8},{10,11... | collective-permute-start | bytes 663560 | tf_op jit(solution)/shard_map/ppermute | solution.py:311
  15.6 5.9 %collective-permute-start.5 = (f32[432,128]{1,0:T(8,128)S(1)}, f32[432,128]{1,0:T(8,128)S(1)}, u32[]{:S(2)}, u32[]{:S(2)}) collective-permute-start(f32[432,128]{1,0:T(8,128)S(1)} %get-tuple-element.30.own_ref.d_ref), channel_id=1, source_target_pairs={{0,2},{1,4},{2,0},{3,6},{4,1},{5,8},{6,3},{7,10},{8,5},{9,12},{10,... | collective-permute-start | bytes 663560 | tf_op jit(solution)/shard_map/ppermute | solution.py:332
  22.0 2.3 %collective-permute-start.8 = (f32[368,128]{1,0:T(8,128)S(1)}, f32[368,128]{1,0:T(8,128)S(1)}, u32[]{:S(2)}, u32[]{:S(2)}) collective-permute-start(f32[368,128]{1,0:T(8,128)S(1)} %get-tuple-element.32.own_ref.w_ref), channel_id=1, source_target_pairs={{0,1},{1,0},{2,3},{3,2},{4,5},{5,4},{6,7},{7,6},{8,9},{9,8},{10,11... | collective-permute-start | bytes 565256 | tf_op jit(solution)/shard_map/ppermute | solution.py:311
  22.1 5.6 %collective-permute-start.7 = (f32[368,128]{1,0:T(8,128)S(1)}, f32[368,128]{1,0:T(8,128)S(1)}, u32[]{:S(2)}, u32[]{:S(2)}) collective-permute-start(f32[368,128]{1,0:T(8,128)S(1)} %get-tuple-element.32.own_ref.w_ref), channel_id=1, source_target_pairs={{0,2},{1,4},{2,0},{3,6},{4,1},{5,8},{6,3},{7,10},{8,5},{9,12},{10,... | collective-permute-start | bytes 565256 | tf_op jit(solution)/shard_map/ppermute | solution.py:332
  28.4 1.3 %collective-permute-start.9 = (f32[152,128]{1,0:T(8,128)S(1)}, f32[152,128]{1,0:T(8,128)S(1)}, u32[]{:S(2)}, u32[]{:S(2)}) collective-permute-start(f32[152,128]{1,0:T(8,128)S(1)} %get-tuple-element.37), channel_id=1, source_target_pairs={{0,1},{1,0},{2,3},{3,2},{4,5},{5,4},{6,7},{7,6},{8,9},{9,8},{10,11... | collective-permute-start | bytes 233480 | tf_op jit(solution)/shard_map/ppermute | solution.py:311
  28.5 11.0 %collective-permute-start.14 = (f32[576,128]{1,0:T(8,128)S(1)}, f32[576,128]{1,0:T(8,128)S(1)}, u32[]{:S(2)}, u32[]{:S(2)}) collective-permute-start(f32[576,128]{1,0:T(8,128)S(1)} %get-tuple-element.39), channel_id=1, source_target_pairs={{0,1},{1,0},{2,3},{3,2},{4,5},{5,4},{6,7},{7,6},{8,9},{9,8},{10,11... | collective-permute-start | bytes 884744 | tf_op jit(solution)/shard_map/ppermute | solution.py:311
  29.6 3.0 %collective-permute-start.10 = (f32[8,128]{1,0:T(8,128)S(1)}, f32[8,128]{1,0:T(8,128)S(1)}, u32[]{:S(2)}, u32[]{:S(2)}) collective-permute-start(f32[8,128]{1,0:T(8,128)S(1)} %slice_add_fusion), channel_id=1, source_target_pairs={{0,3},{1,2},{2,1},{3,0},{4,7},{5,6},{6,5},{7,4},{8,11},{9,10},{10,... | collective-permute-start | bytes 12296 | tf_op jit(solution)/shard_map/ppermute | solution.py:728
  32.7 4.8 %collective-permute-start.13 = (f32[8,128]{1,0:T(8,128)S(1)}, f32[8,128]{1,0:T(8,128)S(1)}, u32[]{:S(2)}, u32[]{:S(2)}) collective-permute-start(f32[8,128]{1,0:T(8,128)S(1)} %add.16), channel_id=1, source_target_pairs={{0,13},{1,12},{4,9},{5,8},{8,5},{9,4},{12,1},{13,0},{2,15},{3,14},... | collective-permute-start | bytes 12296 | tf_op jit(solution)/shard_map/ppermute | solution.py:728
  35.6 3.9 %collective-permute-start.12 = (f32[8,128]{1,0:T(8,128)S(1)}, f32[8,128]{1,0:T(8,128)S(1)}, u32[]{:S(2)}, u32[]{:S(2)}) collective-permute-start(f32[8,128]{1,0:T(8,128)S(1)} %add.16), channel_id=1, source_target_pairs={{0,9},{1,8},{4,13},{5,12},{8,1},{9,0},{12,5},{13,4},{2,11},{3,10},... | collective-permute-start | bytes 12296 | tf_op jit(solution)/shard_map/ppermute | solution.py:728
  35.6 3.9 %collective-permute-start.11 = (f32[8,128]{1,0:T(8,128)S(1)}, f32[8,128]{1,0:T(8,128)S(1)}, u32[]{:S(2)}, u32[]{:S(2)}) collective-permute-start(f32[8,128]{1,0:T(8,128)S(1)} %add.16), channel_id=1, source_target_pairs={{0,5},{1,4},{4,1},{5,0},{8,13},{9,12},{12,9},{13,8},{2,7},{3,6},{6... | collective-permute-start | bytes 12296 | tf_op jit(solution)/shard_map/ppermute | solution.py:728

commit v2 on v1

--- a/solution.py
+++ b/solution.py
@@ -46,7 +46,7 @@
             raise ValueError("block shape")
         self.depth = (self.tiles * self.width, self.ngy * self.rows)
         self.r0 = self.rows + 6
-        self.main = up8((self.fields + 2) * self.rows)
+        self.main = up8((self.fields + 4) * self.rows)
 
     def per(self, count):
         return up8(self.fields * count)
@@ -169,7 +169,7 @@
                     emit(t, comp, e - 1, total * sign if comp == 0 else total)
 
 
-def single(p, ref, modulus, count, sign, way, emit):
+def single(p, ref, modulus, count, sign, way, emit, flip=False):
     lane = p.lanes()
     cq, cb, cs = THREE * lame, 2.0 * THREE * shear, THREE * shear
     cd, ce, cf = TWO * (lame + 3.0 * shear), TWO * lame, TWO * shear
@@ -184,7 +184,10 @@
                     at = ((comp * 2 + c) * count + e) * p.tiles + t
                     a = ref[at, 0 : p.cases, :]
                     b = ref[at + p.tiles, 0 : p.cases, :]
-                    m[comp][0, c], m[comp][1, c] = a + b, b - a
+                    if flip and comp == 0:
+                        m[comp][0, c], m[comp][1, c] = -a - b, a - b
+                    else:
+                        m[comp][0, c], m[comp][1, c] = a + b, b - a
             x, y, z = m
             mod = p.wide(modulus(t, e))
             q = cq * (x[0, 0] + y[1, 0] + z[0, 1])
@@ -238,7 +241,7 @@
                     emit(t, comp, e - 1, total * sign if comp == 0 else total)
 
 
-OWN, PARTNER, RECEIVED, NEAR, FAR, SCALE = range(6)
+OWN, PARTNER, RECEIVED, NEAR, FAR, SCALE, BEYOND, PAST, SCALE_FAR = range(9)
 
 
 def static(p, ref, kind, t, row):
@@ -262,7 +265,7 @@
     y_stat = FL * 3
     y_load = y_stat + 6
     y_part = up8(y_load + FL * 2)
-    d_part = up8(y_load)
+    d_part = up8(y_stat + 12)
     R0, R1, R2 = Y + 6, Y + 4, Y + 2
     N1, N2, N3 = p.per(R1), p.per(R2), p.per(Y)
     M = p.main
@@ -360,8 +363,11 @@
                         v = src[pl.ds(z_stat + (kind * Q + core) * Y + three + r, 1), :]
                         y_ref[pl.ds(at + y_stat + kind * 3 + r, 1), :] = v
                         d_ref[pl.ds(to + y_stat + kind * 3 + r, 1), :] = v
+                        d_ref[pl.ds(to + y_stat + 6 + kind * 3 + r, 1), :] = src[
+                            pl.ds(z_stat + (kind * Q + 1 - core) * Y + three + r, 1), :
+                        ]
             for t in range(T):
-                for ref, part, used in ((y_ref, y_part, y_load + FL * 2), (d_ref, d_part, y_load)):
+                for ref, part, used in ((y_ref, y_part, y_load + FL * 2), (d_ref, d_part, y_stat + 12)):
                     if part > used:
                         ref[t * part + used : (t + 1) * part, :] = jnp.zeros((part - used, W), F32)
         for out, plane in ((own_ref, core), (par_ref, 1 - core)):
@@ -370,9 +376,10 @@
                 for comp in range(D):
                     for r in range(Y):
                         p.put(out, base, Y, comp, r, p.raw(src, 0, comp, plane, r))
-                for kind in range(2):
+                for kind in range(4):
+                    of = plane if kind < 2 else 1 - plane
                     out[pl.ds(pl.multiple_of(base + (FL + kind) * Y, 8), Y), :] = src[
-                        pl.ds(pl.multiple_of(z_stat + (kind * Q + plane) * Y, 8), Y), :
+                        pl.ds(pl.multiple_of(z_stat + (kind % 2 * Q + of) * Y, 8), Y), :
                     ]
 
     ways = (1,) if both else (1, -1)
@@ -530,11 +537,11 @@
         valid = jnp.where(inside, 1.0, 0.0)
         lane_rows = lax.broadcasted_iota(jnp.int32, (R1, W), 1)
         pad = up8(R0)
-        sums = []
         for t in range(T):
             spans = ((0, 3), (3, Y), (Y + 3, 3))
             own_e, par_e, far_e = (const_parts(x, 0, t) for x in (own, par, far))
             own_m, par_m, far_m = (const_parts(x, 1, t) for x in (own, par, far))
+            next_e, next_m = const_parts(far, 2, t), const_parts(far, 3, t)
             for n, (first, count) in enumerate(spans):
                 for kind, v in (
                     (OWN, own_m[n]),
@@ -542,22 +549,27 @@
                     (RECEIVED, far_m[n] * valid),
                     (NEAR, jnp.where(core == 0, own_e[n], par_e[n])),
                     (FAR, jnp.where(core == 0, far_e[n] * valid, own_e[n])),
+                    (BEYOND, next_m[n] * valid),
+                    (PAST, jnp.where(core == 0, next_e[n], far_e[n]) * valid),
                 ):
                     to = (kind * T + t) * pad + first
                     st_ref[to : to + count, :] = v
-            near, rest = (NEAR * T + t) * pad, (FAR * T + t) * pad
-            sums.append(
-                (st_ref[near : near + R1, :] + st_ref[rest : rest + R1, :])
-                + (st_ref[near + 1 : near + 1 + R1, :] + st_ref[rest + 1 : rest + 1 + R1, :])
-            )
-        back = p.behind(sums, lane_rows)
-        for t in range(T):
-            around = sums[t] + back[t]
-            at = (OWN * T + t) * pad + 1
-            mov = st_ref[at : at + R1, :]
-            guarded = jnp.where(mov > 0, around, 1.0)
-            to = (SCALE * T + t) * pad + 1
-            st_ref[to : to + R1, :] = mov / (CORNER * guarded) + (1.0 - mov)
+        for one, other, moved, scaled in ((NEAR, FAR, OWN, SCALE), (FAR, PAST, RECEIVED, SCALE_FAR)):
+            sums = []
+            for t in range(T):
+                near, rest = (one * T + t) * pad, (other * T + t) * pad
+                sums.append(
+                    (st_ref[near : near + R1, :] + st_ref[rest : rest + R1, :])
+                    + (st_ref[near + 1 : near + 1 + R1, :] + st_ref[rest + 1 : rest + 1 + R1, :])
+                )
+            back = p.behind(sums, lane_rows)
+            for t in range(T):
+                around = sums[t] + back[t]
+                at = (moved * T + t) * pad + 1
+                mov = st_ref[at : at + R1, :]
+                guarded = jnp.where(mov > 0, around, 1.0)
+                to = (scaled * T + t) * pad + 1
+                st_ref[to : to + R1, :] = mov / (CORNER * guarded) + (1.0 - mov)
         modes_z(
             p,
             lambda t, k, r: field_at(far, t, k, r),
@@ -581,7 +593,7 @@
 
     res0, dir0, consts = call(
         far_start_body,
-        [(T * N3, W), (T * N1, W), (6 * T * up8(R0), W)],
+        [(T * N3, W), (T * N1, W), (9 * T * up8(R0), W)],
         [far_m, own_m, par_m, modes, part, loaded] + y_got + par_y + far_y,
         [field_shapes(R0)],
         flops=10**6,
@@ -602,9 +614,9 @@
         layer(p, modes_ref, other_ref, False, lambda t, e: static(p, st_ref, NEAR, t, e + shift), count, sign, emit)
         single(p, modes_ref, lambda t, e: static(p, st_ref, FAR, t, e + shift), count, -sign, -1, more)
 
-    def far_apply(far_ref, own_ref, st_ref, part_ref, other_ref, per, count, shift, emit):
+    def far_apply(load, own_ref, st_ref, part_ref, other_ref, per, count, shift, emit):
         _, sign = place()
-        modes_z(p, lambda t, k, r: p.tile(far_ref, t * per, count, k, r), lambda t, r: static(p, st_ref, RECEIVED, t, r + shift), count, -sign, other_ref)
+        modes_z(p, load, lambda t, r: static(p, st_ref, RECEIVED, t, r + shift), count, -sign, other_ref)
 
         def finish(t, comp, r, v):
             force = v + part_ref[(comp * (count - 2) + r) * T + t, 0:C, :]
@@ -616,12 +628,17 @@
 
     far_d = planes_along(dir0)
     par_d = cores(dir0)
+    next_d = planes_along(par_d)
 
     def near_one_body(own_ref, par_ref, st_ref, part_ref, modes_ref, other_ref):
         near_apply(own_ref, par_ref, st_ref, part_ref, modes_ref, other_ref, N1, R1, 1)
 
-    (part1,) = call(
-        near_one_body, [(D * R2 * T, 8, W)], [dir0, par_d, consts], [field_shapes(R1)] * 2, flops=10**6
+    part1, modes1 = call(
+        near_one_body,
+        [(D * R2 * T, 8, W), field_shapes(R1)],
+        [dir0, par_d, consts],
+        [field_shapes(R1)],
+        flops=10**6,
     )
 
     def far_one_body(far_ref, own_ref, st_ref, part_ref, q_ref, w_ref, other_ref):
@@ -635,18 +652,31 @@
             if 1 <= r < Y + 1:
                 p.put(q_ref, t * N3, Y, comp, r - 1, image)
 
-        far_apply(far_ref, own_ref, st_ref, part_ref, other_ref, N1, R1, 1, emit)
-
-    image0, second = call(
+        load = lambda t, k, r: p.tile(far_ref, t * N1, R1, k, r)
+        far_apply(load, own_ref, st_ref, part_ref, other_ref, N1, R1, 1, emit)
+
+    image0, second, modes_far = call(
         far_one_body,
-        [(T * N3, W), (T * N2, W)],
+        [(T * N3, W), (T * N2, W), field_shapes(R1)],
         [far_d, dir0, consts, part1],
-        [field_shapes(R1)],
         flops=10**6,
     )
-
-    far_w = planes_along(second)
     par_w = cores(second)
+
+    def across_body(far_ref, own_ref, st_ref, part_ref):
+        _, sign = place()
+
+        def emit(t, comp, r, v):
+            part_ref[(comp * R2 + r) * T + t, 0:C, :] = v
+
+        def more(t, comp, r, v):
+            at = (comp * R2 + r) * T + t
+            part_ref[at, 0:C, :] = part_ref[at, 0:C, :] + v
+
+        layer(p, far_ref, own_ref, True, lambda t, e: static(p, st_ref, FAR, t, e + 1), R1, sign, emit)
+        single(p, far_ref, lambda t, e: static(p, st_ref, PAST, t, e + 1), R1, -sign, -1, more, True)
+
+    (part_far,) = call(across_body, [(D * R2 * T, 8, W)], [modes_far, modes1, consts], flops=10**6)
 
     def columns(number, sums, lane):
         table = jnp.zeros((C, W), F32)
@@ -686,20 +716,40 @@
     def near_two_body(own_ref, par_ref, st_ref, part_ref, modes_ref, other_ref):
         near_apply(own_ref, par_ref, st_ref, part_ref, modes_ref, other_ref, N2, R2, 2)
 
-    (part2,) = call(
-        near_two_body, [(D * Y * T, 8, W)], [second, par_w, consts], [field_shapes(R2)] * 2, flops=10**6
-    )
+    (part2,) = call(near_two_body, [(D * Y * T, 8, W)], [second, par_w, consts], [field_shapes(R2)] * 2, flops=10**6)
     kept = cores(send)
 
-    def far_two_body(far_ref, own_ref, st_ref, part_ref, gram_ref, mine_ref, send_ref, other_ref, u_ref):
-        core = lax.axis_index("gz")
+    def far_two_body(
+        next_ref, far_ref, own_ref, st_ref, part_far_ref, part_ref, gram_ref,
+        mine_ref, send_ref, next_modes_ref, w_ref, other_ref, u_ref,
+    ):
+        core, sign = place()
+        modes_z(
+            p,
+            lambda t, k, r: p.tile(next_ref, t * N1, R1, k, r),
+            lambda t, r: static(p, st_ref, BEYOND, t, r + 1),
+            R1,
+            -sign,
+            next_modes_ref,
+        )
+
+        def found(t, comp, r, v):
+            force = v + part_far_ref[(comp * R2 + r) * T + t, 0:C, :]
+            mov = p.wide(static(p, st_ref, RECEIVED, t, r + 2))
+            here = p.tile(far_ref, t * N1, R1, comp, r + 1)
+            image = mov * force + (1.0 - mov) * here
+            scale = p.wide(static(p, st_ref, SCALE_FAR, t, r + 2))
+            w_ref[(comp * R2 + r) * T + t, 0:C, :] = scale * image - here
+
+        single(p, next_modes_ref, lambda t, e: static(p, st_ref, PAST, t, e + 1), R1, -sign, 1, found)
 
         def emit(t, comp, r, image, here):
             p.put(u_ref, t * N3, Y, comp, r, image)
             sums_in.append((image, t, comp, r))
 
         sums_in = []
-        far_apply(far_ref, own_ref, st_ref, part_ref, other_ref, N2, R2, 2, emit)
+        load = lambda t, k, r: w_ref[(k * R2 + r) * T + t, 0:C, :]
+        far_apply(load, own_ref, st_ref, part_ref, other_ref, N2, R2, 2, emit)
         sums = [jnp.zeros((C, W), F32) for _ in range(C)]
         for _, t, comp, r in sums_in:
             u = p.tile(u_ref, t * N3, Y, comp, r)
@@ -715,8 +765,8 @@
     mine_u, send_u = call(
         far_two_body,
         [(N3 + 8, W), (N3 + 8, W)],
-        [far_w, second, consts, part2, gram3],
-        [field_shapes(R2), (T * N3, W)],
+        [next_d, far_d, second, consts, part_far, part2, gram3],
+        [field_shapes(R1), (D * R2 * T, 8, W), field_shapes(R2), (T * N3, W)],
         flops=10**6,
     )
     kept_u = cores(send_u)

time: 41.2 us -> 39.1 us (0.949)
  waiting for transfers between devices: 16.2 us -> 13.1 us
  Pallas kernels: 8.38 us -> 9.62 us
    ppermute x4, waiting for transfers between devices: 6.75 us -> 3.24 us  [planes_along(): return lax.ppermute(x, ('gx', 'gy', 'gz'), pairs)]
    pallas_call x12 -> x13, Pallas kernels: 8.38 us -> 9.62 us  [call(): pl.pallas_call(body, out_shape=[jax.ShapeDtypeStruct(s, F32) if far_out e...]
    ppermute x4, starting transfers between devices: 5.36 us -> 4.66 us  [planes_along(): return lax.ppermute(x, ('gx', 'gy', 'gz'), pairs)]
  transfers between devices with their start and end apart: 15 -> 15, of which waited for: 9 -> 9; matrix products, arithmetic and copies ran while one was open for 0% -> 0% of each run, Pallas kernels for 9% -> 13%
where the time goes in v2:
time: 39.1 us; the launch traced here: 38.9 us
  starting transfers between devices  15.4 us (39%)
  waiting for transfers between devices  13.1 us (34%)
  Pallas kernels  9.62 us (25%)
  between operations  0.73 us (2%)
    pallas_call x13, Pallas kernels, call(): pl.pallas_call(body, out_shape=[jax.ShapeDtypeStruct(s, F32) if far_out e...  9.62 us
    ppermute x4, starting transfers between devices, crossed(): return lax.ppermute(x, (axis, 'gz'), pairs)  5.76 us
    ppermute x4, waiting for transfers between devices, crossed(): return lax.ppermute(x, (axis, 'gz'), pairs)  4.84 us
    ppermute x4, starting transfers between devices, planes_along(): return lax.ppermute(x, ('gx', 'gy', 'gz'), pairs)  4.66 us
    ppermute x4, waiting for transfers between devices, planes_along(): return lax.ppermute(x, ('gx', 'gy', 'gz'), pairs)  3.24 us
    ppermute x1, waiting for transfers between devices, rows_along(): lax.ppermute(x, 'gy', [(i, (i + step) % p.ngy) for i in range(p.ngy)])  3.02 us
    ppermute x1, starting transfers between devices, rows_along(): lax.ppermute(x, 'gy', [(i, (i + step) % p.ngy) for i in range(p.ngy)])  2.91 us
    ppermute x6, starting transfers between devices, cores(): return lax.ppermute(x, 'gz', [(i, 1 - i) for i in range(T)])  2.07 us
  transfers between devices with their start and end apart: 15, of which 9 were waited for; matrix products, arithmetic and copies ran while one was open for 0% of the time, Pallas kernels for 13%

profile of v2, /device:TPU:0, one launch (start us, length us, event | category | flops | bytes accessed | tf_op | source)
XLA Modules:
  0.0 38.9 jit_solution(17039487030951522609)
XLA Ops:
  0.6 1.0 %shard_map.77 = (f32[464,128]{1,0:T(8,128)S(1)}, f32[288,128]{1,0:T(8,128)S(1)}) custom-call(f32[288,128]{1,0:T(8,128)} %bitcast.8, f32[288,128]{1,0:T(8,128)} %bitcast.9, s32[16,128]{1,0:T(8,128)} %bitcast.10, s32[16,128]{1,0:T(8,128)} %bitcast.11), custom_call_target="tpu_custom_call" | custom-call | flops 100000 | tf_op jit(solution)/shard_map/pallas_call | solution.py:29
  1.7 0.6 %collective-permute-start = (f32[464,128]{1,0:T(8,128)S(1)}, f32[464,128]{1,0:T(8,128)S(1)}, u32[]{:S(2)}, u32[]{:S(2)}) collective-permute-start(f32[464,128]{1,0:T(8,128)S(1)} %get-tuple-element.25.s_ref.x_ref), channel_id=1, source_target_pairs={{0,1},{1,0},{2,3},{3,2},{4,5},{5,4},{6,7},{7,6},{8,9},{9,8},{10,11... | collective-permute-start | bytes 712712 | tf_op jit(solution)/shard_map/ppermute | solution.py:314
  2.2 1.1 %collective-permute-done.z_ref = f32[464,128]{1,0:T(8,128)S(1)} collective-permute-done((f32[464,128]{1,0:T(8,128)S(1)}, f32[464,128]{1,0:T(8,128)S(1)}, u32[]{:S(2)}, u32[]{:S(2)}) %collective-permute-start) | collective-permute-done | bytes 237600 | tf_op jit(solution)/shard_map/ppermute | solution.py:314
  3.6 2.9 %collective-permute-start.2 = (f32[192,128]{1,0:T(8,128)S(1)}, f32[192,128]{1,0:T(8,128)S(1)}, u32[]{:S(2)}, u32[]{:S(2)}) collective-permute-start(f32[192,128]{1,0:T(8,128)S(1)} %get-tuple-element.29), channel_id=1, source_target_pairs={{0,2},{2,0},{1,3},{3,1},{4,6},{6,4},{5,7},{7,5},{8,10},{10,8},{9,1... | collective-permute-start | bytes 294920 | tf_op jit(solution)/shard_map/ppermute | solution.py:317
  6.5 3.0 %collective-permute-done.2.refs_0_ = f32[192,128]{1,0:T(8,128)S(1)} collective-permute-done((f32[192,128]{1,0:T(8,128)S(1)}, f32[192,128]{1,0:T(8,128)S(1)}, u32[]{:S(2)}, u32[]{:S(2)}) %collective-permute-start.2) | collective-permute-done | bytes 98336 | tf_op jit(solution)/shard_map/ppermute | solution.py:317
  9.6 1.7 %collective-permute-start.4 = (f32[144,128]{1,0:T(8,128)S(1)}, f32[144,128]{1,0:T(8,128)S(1)}, u32[]{:S(2)}, u32[]{:S(2)}) collective-permute-start(f32[144,128]{1,0:T(8,128)S(1)} %get-tuple-element.32), channel_id=1, source_target_pairs={{0,2},{1,6},{2,0},{3,4},{4,3},{5,10},{6,1},{7,8},{8,7},{9,14},{10,... | collective-permute-start | bytes 221192 | tf_op jit(solution)/shard_map/ppermute | solution.py:335
  11.9 0.9 %shard_map.79 = (f32[168,8,128]{2,1,0:T(8,128)S(1)}, f32[72,8,128]{2,1,0:T(8,128)S(1)}) custom-call(f32[352,128]{1,0:T(8,128)S(1)} %get-tuple-element.27.own_m_ref, f32[352,128]{1,0:T(8,128)S(1)} %get-tuple-element.28.par_m_ref, f32[192,128]{1,0:T(8,128)S(1)} %collective-permute-done.2.refs_0_, f32[192,128]{1,0:T(8,128)S(1)} %collective-permute-done.3.refs_1_), custom_call_target="tpu_custom_call" | custom-call | flops 1000000 | tf_op jit(solution)/shard_map/pallas_call | solution.py:29
  12.8 1.2 %collective-permute-done.4.refs_2_ = f32[144,128]{1,0:T(8,128)S(1)} collective-permute-done((f32[144,128]{1,0:T(8,128)S(1)}, f32[144,128]{1,0:T(8,128)S(1)}, u32[]{:S(2)}, u32[]{:S(2)}) %collective-permute-start.4) | collective-permute-done | bytes 73760 | tf_op jit(solution)/shard_map/ppermute | solution.py:335
  13.9 0.8 %shard_map.82 = (f32[288,128]{1,0:T(8,128)S(1)}, f32[432,128]{1,0:T(8,128)S(1)}, f32[288,128]{1,0:T(8,128)S(1)}) custom-call(f32[352,128]{1,0:T(8,128)S(1)} %collective-permute-done.1.far_m_ref, f32[352,128]{1,0:T(8,128)S(1)} %get-tuple-element.27.own_m_ref, f32[352,128]{1,0:T(8,128)S(1)} %get-tuple-element.28.par_m_ref, ...), custom_call_target="tpu_custom_call" | custom-call | flops 1000000 | tf_op jit(solution)/shard_map/pallas_call | solution.py:29
  14.8 0.9 %collective-permute-start.5 = (f32[432,128]{1,0:T(8,128)S(1)}, f32[432,128]{1,0:T(8,128)S(1)}, u32[]{:S(2)}, u32[]{:S(2)}) collective-permute-start(f32[432,128]{1,0:T(8,128)S(1)} %get-tuple-element.33.own_ref.d_ref), channel_id=1, source_target_pairs={{0,1},{1,0},{2,3},{3,2},{4,5},{5,4},{6,7},{7,6},{8,9},{9,8},{10,11... | collective-permute-start | bytes 663560 | tf_op jit(solution)/shard_map/ppermute | solution.py:314
  15.7 1.7 %collective-permute-start.7 = (f32[432,128]{1,0:T(8,128)S(1)}, f32[432,128]{1,0:T(8,128)S(1)}, u32[]{:S(2)}, u32[]{:S(2)}) collective-permute-start(f32[432,128]{1,0:T(8,128)S(1)} %get-tuple-element.33.own_ref.d_ref), channel_id=1, source_target_pairs={{0,2},{1,4},{2,0},{3,6},{4,1},{5,8},{6,3},{7,10},{8,5},{9,12},{10,... | collective-permute-start | bytes 663560 | tf_op jit(solution)/shard_map/ppermute | solution.py:335
  17.4 1.1 %collective-permute-start.6 = (f32[432,128]{1,0:T(8,128)S(1)}, f32[432,128]{1,0:T(8,128)S(1)}, u32[]{:S(2)}, u32[]{:S(2)}) collective-permute-start(f32[432,128]{1,0:T(8,128)S(1)} %collective-permute-done.5.par_ref), channel_id=1, source_target_pairs={{0,2},{1,4},{2,0},{3,6},{4,1},{5,8},{6,3},{7,10},{8,5},{9,12},{10,... | collective-permute-start | bytes 663560 | tf_op jit(solution)/shard_map/ppermute | solution.py:335
  18.5 1.0 %shard_map.83 = (f32[60,8,128]{2,1,0:T(8,128)S(1)}, f32[144,8,128]{2,1,0:T(8,128)S(1)}) custom-call(f32[432,128]{1,0:T(8,128)S(1)} %get-tuple-element.33.own_ref.d_ref, f32[432,128]{1,0:T(8,128)S(1)} %collective-permute-done.5.par_ref, f32[288,128]{1,0:T(8,128)S(1)} %get-tuple-element.34.st_ref), custom_call_target="tpu_custom_call" | custom-call | flops 1000000 | tf_op jit(solution)/shard_map/pallas_call | solution.py:29
  19.5 2.1 %collective-permute-done.7.far_ref = f32[432,128]{1,0:T(8,128)S(1)} collective-permute-done((f32[432,128]{1,0:T(8,128)S(1)}, f32[432,128]{1,0:T(8,128)S(1)}, u32[]{:S(2)}, u32[]{:S(2)}) %collective-permute-start.7) | collective-permute-done | bytes 221216 | tf_op jit(solution)/shard_map/ppermute | solution.py:335
  22.2 0.8 %shard_map.85.part_far_ref = f32[60,8,128]{2,1,0:T(8,128)S(1)} custom-call(f32[144,8,128]{2,1,0:T(8,128)S(1)} %get-tuple-element.37.far_ref, f32[144,8,128]{2,1,0:T(8,128)S(1)} %get-tuple-element.38.own_ref, f32[288,128]{1,0:T(8,128)S(1)} %get-tuple-element.34.st_ref), custom_call_target="tpu_custom_call" | custom-call | flops 1000000 | tf_op jit(solution)/shard_map/pallas_call | solution.py:29
  23.6 0.9 %shard_map.86.part_ref = f32[48,8,128]{2,1,0:T(8,128)S(1)} custom-call(f32[368,128]{1,0:T(8,128)S(1)} %get-tuple-element.36.own_ref.w_ref, f32[368,128]{1,0:T(8,128)S(1)} %collective-permute-done.8.par_ref, f32[288,128]{1,0:T(8,128)S(1)} %get-tuple-element.34.st_ref), custom_call_target="tpu_custom_call" | custom-call | flops 1000000 | tf_op jit(solution)/shard_map/pallas_call | solution.py:29
  24.5 1.0 %shard_map.88 = (f32[152,128]{1,0:T(8,128)S(1)}, f32[152,128]{1,0:T(8,128)S(1)}) custom-call(f32[432,128]{1,0:T(8,128)S(1)} %collective-permute-done.6.next_ref, f32[432,128]{1,0:T(8,128)S(1)} %collective-permute-done.7.far_ref, f32[368,128]{1,0:T(8,128)S(1)} %get-tuple-element.36.own_ref.w_ref, f32[288,128]{1,0:T(8,128)S(1)} %get-tuple-element.34.st_ref, ...), custom_call_target="tpu_custom_call" | custom-call | flops 1000000 | tf_op jit(solution)/shard_map/pallas_call | solution.py:29
  26.0 0.8 %collective-permute-done.9.kept_u_ref = f32[152,128]{1,0:T(8,128)S(1)} collective-permute-done((f32[152,128]{1,0:T(8,128)S(1)}, f32[152,128]{1,0:T(8,128)S(1)}, u32[]{:S(2)}, u32[]{:S(2)}) %collective-permute-start.9) | collective-permute-done | bytes 77856 | tf_op jit(solution)/shard_map/ppermute | solution.py:314
  26.8 1.7 %collective-permute-start.10 = (f32[8,128]{1,0:T(8,128)S(1)}, f32[8,128]{1,0:T(8,128)S(1)}, u32[]{:S(2)}, u32[]{:S(2)}) collective-permute-start(f32[8,128]{1,0:T(8,128)S(1)} %slice_add_fusion), channel_id=1, source_target_pairs={{0,3},{1,2},{2,1},{3,0},{4,7},{5,6},{6,5},{7,4},{8,11},{9,10},{10,... | collective-permute-start | bytes 12296 | tf_op jit(solution)/shard_map/ppermute | solution.py:778
  28.5 1.3 %collective-permute-done.10 = f32[8,128]{1,0:T(8,128)S(1)} collective-permute-done((f32[8,128]{1,0:T(8,128)S(1)}, f32[8,128]{1,0:T(8,128)S(1)}, u32[]{:S(2)}, u32[]{:S(2)}) %collective-permute-start.10) | collective-permute-done | bytes 4128 | tf_op jit(solution)/shard_map/ppermute | solution.py:778
  29.9 3.6 %collective-permute-start.13 = (f32[8,128]{1,0:T(8,128)S(1)}, f32[8,128]{1,0:T(8,128)S(1)}, u32[]{:S(2)}, u32[]{:S(2)}) collective-permute-start(f32[8,128]{1,0:T(8,128)S(1)} %add.16), channel_id=1, source_target_pairs={{0,13},{1,12},{4,9},{5,8},{8,5},{9,4},{12,1},{13,0},{2,15},{3,14},... | collective-permute-start | bytes 12296 | tf_op jit(solution)/shard_map/ppermute | solution.py:778
  34.0 0.9 %collective-permute-done.13 = f32[8,128]{1,0:T(8,128)S(1)} collective-permute-done((f32[8,128]{1,0:T(8,128)S(1)}, f32[8,128]{1,0:T(8,128)S(1)}, u32[]{:S(2)}, u32[]{:S(2)}) %collective-permute-start.13) | collective-permute-done | bytes 4128 | tf_op jit(solution)/shard_map/ppermute | solution.py:778
  34.8 2.6 %collective-permute-done.12 = f32[8,128]{1,0:T(8,128)S(1)} collective-permute-done((f32[8,128]{1,0:T(8,128)S(1)}, f32[8,128]{1,0:T(8,128)S(1)}, u32[]{:S(2)}, u32[]{:S(2)}) %collective-permute-start.12) | collective-permute-done | bytes 4128 | tf_op jit(solution)/shard_map/ppermute | solution.py:778
  37.5 1.4 %shard_map.89 = (f32[288,128]{1,0:T(8,128)}, f32[288,128]{1,0:T(8,128)}) custom-call(f32[8,128]{1,0:T(8,128)S(1)} %add_add_fusion.g_ref, f32[464,128]{1,0:T(8,128)S(1)} %get-tuple-element.25.s_ref.x_ref, f32[576,128]{1,0:T(8,128)S(1)} %get-tuple-element.44.mine_ref, f32[152,128]{1,0:T(8,128)S(1)} %get-tuple-element.42.mine_u_ref, ...), custom_call_target="tpu_custom_call" | custom-call | flops 100000 | tf_op jit(solution)/shard_map/pallas_call | solution.py:29
  (26 shorter events, 3.0 us)
Async XLA Ops:
  1.7 1.7 %collective-permute-start = (f32[464,128]{1,0:T(8,128)S(1)}, f32[464,128]{1,0:T(8,128)S(1)}, u32[]{:S(2)}, u32[]{:S(2)}) collective-permute-start(f32[464,128]{1,0:T(8,128)S(1)} %get-tuple-element.25.s_ref.x_ref), channel_id=1, source_target_pairs={{0,1},{1,0},{2,3},{3,2},{4,5},{5,4},{6,7},{7,6},{8,9},{9,8},{10,11... | collective-permute-start | bytes 712712 | tf_op jit(solution)/shard_map/ppermute | solution.py:314
  3.4 8.0 %copy-start = (f32[6,16,3]{1,2,0:T(4,128)S(1)}, f32[6,16,3]{1,2,0:T(4,128)}, u32[]{:S(2)}) copy-start(f32[6,16,3]{1,2,0:T(4,128)} %param.11) | copy-start | bytes 3460
  3.5 7.8 %copy-start.1 = (s32[6,16]{1,0:T(8,128)S(1)}, s32[6,16]{1,0:T(8,128)}, u32[]{:S(2)}) copy-start(s32[6,16]{1,0:T(8,128)} %node_ref.1) | copy-start | bytes 1156
  3.6 6.0 %collective-permute-start.2 = (f32[192,128]{1,0:T(8,128)S(1)}, f32[192,128]{1,0:T(8,128)S(1)}, u32[]{:S(2)}, u32[]{:S(2)}) collective-permute-start(f32[192,128]{1,0:T(8,128)S(1)} %get-tuple-element.29), channel_id=1, source_target_pairs={{0,2},{2,0},{1,3},{3,1},{4,6},{6,4},{5,7},{7,5},{8,10},{10,8},{9,1... | collective-permute-start | bytes 294920 | tf_op jit(solution)/shard_map/ppermute | solution.py:317
  6.5 7.5 %collective-permute-start.1 = (f32[352,128]{1,0:T(8,128)S(1)}, f32[352,128]{1,0:T(8,128)S(1)}, u32[]{:S(2)}, u32[]{:S(2)}) collective-permute-start(f32[352,128]{1,0:T(8,128)S(1)} %get-tuple-element.27.own_m_ref), channel_id=1, source_target_pairs={{0,2},{1,4},{2,0},{3,6},{4,1},{5,8},{6,3},{7,10},{8,5},{9,12},{10,... | collective-permute-start | bytes 540680 | tf_op jit(solution)/shard_map/ppermute | solution.py:335
  9.6 2.3 %collective-permute-start.3 = (f32[192,128]{1,0:T(8,128)S(1)}, f32[192,128]{1,0:T(8,128)S(1)}, u32[]{:S(2)}, u32[]{:S(2)}) collective-permute-start(f32[192,128]{1,0:T(8,128)S(1)} %collective-permute-done.2.refs_0_), channel_id=1, source_target_pairs={{0,1},{1,0},{2,3},{3,2},{4,5},{5,4},{6,7},{7,6},{8,9},{9,8},{10,11... | collective-permute-start | bytes 294920 | tf_op jit(solution)/shard_map/ppermute | solution.py:314
  9.6 4.4 %collective-permute-start.4 = (f32[144,128]{1,0:T(8,128)S(1)}, f32[144,128]{1,0:T(8,128)S(1)}, u32[]{:S(2)}, u32[]{:S(2)}) collective-permute-start(f32[144,128]{1,0:T(8,128)S(1)} %get-tuple-element.32), channel_id=1, source_target_pairs={{0,2},{1,6},{2,0},{3,4},{4,3},{5,10},{6,1},{7,8},{8,7},{9,14},{10,... | collective-permute-start | bytes 221192 | tf_op jit(solution)/shard_map/ppermute | solution.py:335
  14.8 2.6 %collective-permute-start.5 = (f32[432,128]{1,0:T(8,128)S(1)}, f32[432,128]{1,0:T(8,128)S(1)}, u32[]{:S(2)}, u32[]{:S(2)}) collective-permute-start(f32[432,128]{1,0:T(8,128)S(1)} %get-tuple-element.33.own_ref.d_ref), channel_id=1, source_target_pairs={{0,1},{1,0},{2,3},{3,2},{4,5},{5,4},{6,7},{7,6},{8,9},{9,8},{10,11... | collective-permute-start | bytes 663560 | tf_op jit(solution)/shard_map/ppermute | solution.py:314
  15.7 5.9 %collective-permute-start.7 = (f32[432,128]{1,0:T(8,128)S(1)}, f32[432,128]{1,0:T(8,128)S(1)}, u32[]{:S(2)}, u32[]{:S(2)}) collective-permute-start(f32[432,128]{1,0:T(8,128)S(1)} %get-tuple-element.33.own_ref.d_ref), channel_id=1, source_target_pairs={{0,2},{1,4},{2,0},{3,6},{4,1},{5,8},{6,3},{7,10},{8,5},{9,12},{10,... | collective-permute-start | bytes 663560 | tf_op jit(solution)/shard_map/ppermute | solution.py:335
  17.4 7.1 %collective-permute-start.6 = (f32[432,128]{1,0:T(8,128)S(1)}, f32[432,128]{1,0:T(8,128)S(1)}, u32[]{:S(2)}, u32[]{:S(2)}) collective-permute-start(f32[432,128]{1,0:T(8,128)S(1)} %collective-permute-done.5.par_ref), channel_id=1, source_target_pairs={{0,2},{1,4},{2,0},{3,6},{4,1},{5,8},{6,3},{7,10},{8,5},{9,12},{10,... | collective-permute-start | bytes 663560 | tf_op jit(solution)/shard_map/ppermute | solution.py:335
  22.1 1.5 %collective-permute-start.8 = (f32[368,128]{1,0:T(8,128)S(1)}, f32[368,128]{1,0:T(8,128)S(1)}, u32[]{:S(2)}, u32[]{:S(2)}) collective-permute-start(f32[368,128]{1,0:T(8,128)S(1)} %get-tuple-element.36.own_ref.w_ref), channel_id=1, source_target_pairs={{0,1},{1,0},{2,3},{3,2},{4,5},{5,4},{6,7},{7,6},{8,9},{9,8},{10,11... | collective-permute-start | bytes 565256 | tf_op jit(solution)/shard_map/ppermute | solution.py:314
  25.5 1.3 %collective-permute-start.9 = (f32[152,128]{1,0:T(8,128)S(1)}, f32[152,128]{1,0:T(8,128)S(1)}, u32[]{:S(2)}, u32[]{:S(2)}) collective-permute-start(f32[152,128]{1,0:T(8,128)S(1)} %get-tuple-element.43), channel_id=1, source_target_pairs={{0,1},{1,0},{2,3},{3,2},{4,5},{5,4},{6,7},{7,6},{8,9},{9,8},{10,11... | collective-permute-start | bytes 233480 | tf_op jit(solution)/shard_map/ppermute | solution.py:314
  25.9 11.5 %collective-permute-start.14 = (f32[576,128]{1,0:T(8,128)S(1)}, f32[576,128]{1,0:T(8,128)S(1)}, u32[]{:S(2)}, u32[]{:S(2)}) collective-permute-start(f32[576,128]{1,0:T(8,128)S(1)} %get-tuple-element.45), channel_id=1, source_target_pairs={{0,1},{1,0},{2,3},{3,2},{4,5},{5,4},{6,7},{7,6},{8,9},{9,8},{10,11... | collective-permute-start | bytes 884744 | tf_op jit(solution)/shard_map/ppermute | solution.py:314
  26.8 3.0 %collective-permute-start.10 = (f32[8,128]{1,0:T(8,128)S(1)}, f32[8,128]{1,0:T(8,128)S(1)}, u32[]{:S(2)}, u32[]{:S(2)}) collective-permute-start(f32[8,128]{1,0:T(8,128)S(1)} %slice_add_fusion), channel_id=1, source_target_pairs={{0,3},{1,2},{2,1},{3,0},{4,7},{5,6},{6,5},{7,4},{8,11},{9,10},{10,... | collective-permute-start | bytes 12296 | tf_op jit(solution)/shard_map/ppermute | solution.py:778
  29.9 5.0 %collective-permute-start.13 = (f32[8,128]{1,0:T(8,128)S(1)}, f32[8,128]{1,0:T(8,128)S(1)}, u32[]{:S(2)}, u32[]{:S(2)}) collective-permute-start(f32[8,128]{1,0:T(8,128)S(1)} %add.16), channel_id=1, source_target_pairs={{0,13},{1,12},{4,9},{5,8},{8,5},{9,4},{12,1},{13,0},{2,15},{3,14},... | collective-permute-start | bytes 12296 | tf_op jit(solution)/shard_map/ppermute | solution.py:778
  33.5 3.9 %collective-permute-start.12 = (f32[8,128]{1,0:T(8,128)S(1)}, f32[8,128]{1,0:T(8,128)S(1)}, u32[]{:S(2)}, u32[]{:S(2)}) collective-permute-start(f32[8,128]{1,0:T(8,128)S(1)} %add.16), channel_id=1, source_target_pairs={{0,9},{1,8},{4,13},{5,12},{8,1},{9,0},{12,5},{13,4},{2,11},{3,10},... | collective-permute-start | bytes 12296 | tf_op jit(solution)/shard_map/ppermute | solution.py:778
  33.5 3.9 %collective-permute-start.11 = (f32[8,128]{1,0:T(8,128)S(1)}, f32[8,128]{1,0:T(8,128)S(1)}, u32[]{:S(2)}, u32[]{:S(2)}) collective-permute-start(f32[8,128]{1,0:T(8,128)S(1)} %add.16), channel_id=1, source_target_pairs={{0,5},{1,4},{4,1},{5,0},{8,13},{9,12},{12,9},{13,8},{2,7},{3,6},{6... | collective-permute-start | bytes 12296 | tf_op jit(solution)/shard_map/ppermute | solution.py:778

commit v3 on v2

--- a/solution.py
+++ b/solution.py
@@ -91,74 +91,92 @@
                 out[((comp * 2 + 1) * count + r) * p.tiles + t, 0 : p.cases, :] = n[t] - v[t]
 
 
-def layer(p, own, other, flip, modulus, count, sign, emit):
+CQ, CB, CS = THREE * lame, 2.0 * THREE * shear, THREE * shear
+CD, CE, CF = TWO * (lame + 3.0 * shear), TWO * lame, TWO * shear
+CG = ONE * (lame + 4.0 * shear)
+
+
+def modes_y(p, ref, count, e, t, flip):
+    found = [{}, {}, {}]
+    for comp in range(3):
+        for c in (0, 1):
+            at = ((comp * 2 + c) * count + e) * p.tiles + t
+            a = ref[at, 0 : p.cases, :]
+            b = ref[at + p.tiles, 0 : p.cases, :]
+            if flip and comp == 0:
+                found[comp][0, c], found[comp][1, c] = -a - b, a - b
+            else:
+                found[comp][0, c], found[comp][1, c] = a + b, b - a
+    return found
+
+
+def between(total, change):
+    (x, y, z), (dx, dy, dz) = total, change
+    q = CQ * (dx[0, 0] + y[1, 0] + z[0, 1])
+    sxy = CS * (dy[0, 0] + x[1, 0])
+    sxz = CS * (dz[0, 0] + x[0, 1])
+    syz = CS * (z[1, 0] + y[0, 1])
+    s = x[1, 1] + dy[0, 1] + dz[1, 0]
+    return {
+        (0, 0, 0): -(q + CB * dx[0, 0]),
+        (0, 1, 0): sxy - (CD * dx[1, 0] + CE * z[1, 1]),
+        (0, 0, 1): sxz - (CD * dx[0, 1] + CE * y[1, 1]),
+        (0, 1, 1): CF * (s + x[1, 1]) - CG * dx[1, 1],
+        (1, 0, 0): -sxy,
+        (1, 1, 0): (q + CB * y[1, 0]) - (CD * dy[1, 0] + CE * dz[0, 1]),
+        (1, 0, 1): syz - CF * (s + dy[0, 1]),
+        (1, 1, 1): (CD * y[1, 1] + CE * dx[0, 1]) - CG * dy[1, 1],
+        (2, 0, 0): -sxz,
+        (2, 0, 1): (q + CB * z[0, 1]) - (CD * dz[0, 1] + CE * dy[1, 0]),
+        (2, 1, 0): syz - CF * (s + dz[1, 0]),
+        (2, 1, 1): (CD * z[1, 1] + CE * dx[1, 0]) - CG * dz[1, 1],
+    }
+
+
+def share(m, way):
+    x, y, z = m
+    q = CQ * (x[0, 0] + y[1, 0] + z[0, 1])
+    sxy = CS * (y[0, 0] + x[1, 0])
+    sxz = CS * (z[0, 0] + x[0, 1])
+    pair = z[1, 0] + y[0, 1]
+    syz = CS * pair
+    s = x[1, 1] + pair
+    found = {
+        (0, 0, 0): -(q + CB * x[0, 0]),
+        (1, 1, 1): (CD - way * CG) * y[1, 1] + CE * x[0, 1],
+        (2, 1, 1): (CD - way * CG) * z[1, 1] + CE * x[1, 0],
+        (0, 1, 1): (way * 2.0 * CF - CG) * x[1, 1] + (way * CF) * pair,
+    }
+    low, high = CD * x[1, 0] + CE * z[1, 1], CD * x[0, 1] + CE * y[1, 1]
+    if way > 0:
+        found[0, 1, 0], found[0, 0, 1] = sxy - low, sxz - high
+        found[1, 0, 0], found[2, 0, 0] = -sxy, -sxz
+        found[1, 1, 0] = q + ((CB - CD) * y[1, 0] - CE * z[0, 1])
+        found[2, 0, 1] = q + ((CB - CD) * z[0, 1] - CE * y[1, 0])
+        found[1, 0, 1] = syz - CF * (s + y[0, 1])
+        found[2, 1, 0] = syz - CF * (s + z[1, 0])
+    else:
+        found[0, 1, 0], found[0, 0, 1] = -sxy - low, -sxz - high
+        found[1, 0, 0], found[2, 0, 0] = sxy, sxz
+        found[1, 1, 0] = q + ((CB + CD) * y[1, 0] + CE * z[0, 1])
+        found[2, 0, 1] = q + ((CB + CD) * z[0, 1] + CE * y[1, 0])
+        found[1, 0, 1] = syz + CF * (s + y[0, 1])
+        found[2, 1, 0] = syz + CF * (s + z[1, 0])
+    return found
+
+
+def spread(p, forces, count, sign, emit):
     lane = p.lanes()
-
-    def modes_y(ref, e, t):
-        found = {}
-        for comp in range(3):
-            for c in (0, 1):
-                at = ((comp * 2 + c) * count + e) * p.tiles + t
-                a = ref[at, 0 : p.cases, :]
-                b = ref[at + p.tiles, 0 : p.cases, :]
-                found[comp, 0, c] = a + b
-                found[comp, 1, c] = b - a
-        return found
-
     carry = {}
     for e in range(count - 1):
         done = {}
         for t in range(p.tiles):
-            near, far = modes_y(own, e, t), modes_y(other, e, t)
-            u = [{}, {}, {}]
-            for (comp, b, c), x in near.items():
-                y = far[comp, b, c]
-                plus, minus = (y - x, y + x) if flip and comp == 0 else (y + x, y - x)
-                u[comp][0, b, c], u[comp][1, b, c] = plus, minus
-            ux, uy, uz = u
-            mod = p.wide(modulus(t, e))
-            ea, eb, es = mod * (THREE * lame), mod * (2.0 * THREE * shear), mod * (THREE * shear)
-            ed, ee, ef = mod * (TWO * (lame + 3.0 * shear)), mod * (TWO * lame), mod * (TWO * shear)
-            eg = mod * (ONE * (lame + 4.0 * shear))
-            q = ea * (ux[1, 0, 0] + uy[0, 1, 0] + uz[0, 0, 1])
-            sxy = es * (uy[1, 0, 0] + ux[0, 1, 0])
-            syz = es * (uz[0, 1, 0] + uy[0, 0, 1])
-            sxz = es * (uz[1, 0, 0] + ux[0, 0, 1])
-            s = ux[0, 1, 1] + uy[1, 0, 1] + uz[1, 1, 0]
-            gx = {
-                (1, 0, 0): q + eb * ux[1, 0, 0],
-                (0, 1, 0): sxy,
-                (0, 0, 1): sxz,
-                (1, 0, 1): ed * ux[1, 0, 1] + ee * uy[0, 1, 1],
-                (1, 1, 0): ed * ux[1, 1, 0] + ee * uz[0, 1, 1],
-                (0, 1, 1): ef * (s + ux[0, 1, 1]),
-                (1, 1, 1): eg * ux[1, 1, 1],
-            }
-            gy = {
-                (0, 1, 0): q + eb * uy[0, 1, 0],
-                (1, 0, 0): sxy,
-                (0, 0, 1): syz,
-                (0, 1, 1): ed * uy[0, 1, 1] + ee * ux[1, 0, 1],
-                (1, 1, 0): ed * uy[1, 1, 0] + ee * uz[1, 0, 1],
-                (1, 0, 1): ef * (s + uy[1, 0, 1]),
-                (1, 1, 1): eg * uy[1, 1, 1],
-            }
-            gz = {
-                (0, 0, 1): q + eb * uz[0, 0, 1],
-                (1, 0, 0): sxz,
-                (0, 1, 0): syz,
-                (0, 1, 1): ed * uz[0, 1, 1] + ee * ux[1, 1, 0],
-                (1, 0, 1): ed * uz[1, 0, 1] + ee * uy[1, 1, 0],
-                (1, 1, 0): ef * (s + uz[1, 1, 0]),
-                (1, 1, 1): eg * uz[1, 1, 1],
-            }
-            for comp, g in enumerate((gx, gy, gz)):
-                h = {bc: g[(0,) + bc] - g[(1,) + bc] for bc in ((0, 1), (1, 0), (1, 1))}
-                h[0, 0] = -g[1, 0, 0]
+            h = forces(e, t)
+            for comp in range(3):
                 for c in (0, 1):
                     if e:
-                        done[comp, c, t] = carry[comp, c, t] + (h[0, c] - h[1, c])
-                    carry[comp, c, t] = h[0, c] + h[1, c]
+                        done[comp, c, t] = carry[comp, c, t] + (h[comp, 0, c] - h[comp, 1, c])
+                    carry[comp, c, t] = h[comp, 0, c] + h[comp, 1, c]
         if e:
             for comp in range(3):
                 low = [done[comp, 0, t] - done[comp, 1, t] for t in range(p.tiles)]
@@ -169,76 +187,28 @@
                     emit(t, comp, e - 1, total * sign if comp == 0 else total)
 
 
-def single(p, ref, modulus, count, sign, way, emit, flip=False):
-    lane = p.lanes()
-    cq, cb, cs = THREE * lame, 2.0 * THREE * shear, THREE * shear
-    cd, ce, cf = TWO * (lame + 3.0 * shear), TWO * lame, TWO * shear
-    cg = ONE * (lame + 4.0 * shear)
-    carry = {}
-    for e in range(count - 1):
-        done = {}
-        for t in range(p.tiles):
-            m = [{}, {}, {}]
-            for comp in range(3):
-                for c in (0, 1):
-                    at = ((comp * 2 + c) * count + e) * p.tiles + t
-                    a = ref[at, 0 : p.cases, :]
-                    b = ref[at + p.tiles, 0 : p.cases, :]
-                    if flip and comp == 0:
-                        m[comp][0, c], m[comp][1, c] = -a - b, a - b
-                    else:
-                        m[comp][0, c], m[comp][1, c] = a + b, b - a
-            x, y, z = m
-            mod = p.wide(modulus(t, e))
-            q = cq * (x[0, 0] + y[1, 0] + z[0, 1])
-            sxy = cs * (y[0, 0] + x[1, 0])
-            sxz = cs * (z[0, 0] + x[0, 1])
-            pair = z[1, 0] + y[0, 1]
-            syz = cs * pair
-            s = x[1, 1] + pair
-            if way > 0:
-                sh = {
-                    (0, 1, 0): sxy - (cd * x[1, 0] + ce * z[1, 1]),
-                    (0, 0, 1): sxz - (cd * x[0, 1] + ce * y[1, 1]),
-                    (0, 1, 1): (2.0 * cf - cg) * x[1, 1] + cf * pair,
-                    (1, 0, 0): -sxy,
-                    (1, 1, 0): q + ((cb - cd) * y[1, 0] - ce * z[0, 1]),
-                    (1, 0, 1): syz - cf * (s + y[0, 1]),
-                    (1, 1, 1): (cd - cg) * y[1, 1] + ce * x[0, 1],
-                    (2, 0, 0): -sxz,
-                    (2, 0, 1): q + ((cb - cd) * z[0, 1] - ce * y[1, 0]),
-                    (2, 1, 0): syz - cf * (s + z[1, 0]),
-                    (2, 1, 1): (cd - cg) * z[1, 1] + ce * x[1, 0],
-                }
-            else:
-                sh = {
-                    (0, 1, 0): -sxy - (cd * x[1, 0] + ce * z[1, 1]),
-                    (0, 0, 1): -sxz - (cd * x[0, 1] + ce * y[1, 1]),
-                    (0, 1, 1): (-2.0 * cf - cg) * x[1, 1] - cf * pair,
-                    (1, 0, 0): sxy,
-                    (1, 1, 0): q + ((cb + cd) * y[1, 0] + ce * z[0, 1]),
-                    (1, 0, 1): syz + cf * (s + y[0, 1]),
-                    (1, 1, 1): (cd + cg) * y[1, 1] + ce * x[0, 1],
-                    (2, 0, 0): sxz,
-                    (2, 0, 1): q + ((cb + cd) * z[0, 1] + ce * y[1, 0]),
-                    (2, 1, 0): syz + cf * (s + z[1, 0]),
-                    (2, 1, 1): (cd + cg) * z[1, 1] + ce * x[1, 0],
-                }
-            sh[0, 0, 0] = -(q + cb * x[0, 0])
-            for comp in range(3):
-                h = {bc: mod * sh[(comp,) + bc] for bc in ((0, 0), (0, 1), (1, 0), (1, 1))}
-                for c in (0, 1):
-                    if e:
-                        done[comp, c, t] = carry[comp, c, t] + (h[0, c] - h[1, c])
-                    carry[comp, c, t] = h[0, c] + h[1, c]
-        if e:
-            for comp in range(3):
-                low = [done[comp, 0, t] - done[comp, 1, t] for t in range(p.tiles)]
-                high = [done[comp, 0, t] + done[comp, 1, t] for t in range(p.tiles)]
-                back = p.behind(high, lane)
-                for t in range(p.tiles):
-                    total = low[t] + back[t]
-                    emit(t, comp, e - 1, total * sign if comp == 0 else total)
+def layer(p, own, other, flip, modulus, count, sign, emit, outer=None):
+    def forces(e, t):
+        near, far = modes_y(p, own, count, e, t, flip), modes_y(p, other, count, e, t, False)
+        total = [{k: far[c][k] + v for k, v in near[c].items()} for c in range(3)]
+        change = [{k: far[c][k] - v for k, v in near[c].items()} for c in range(3)]
+        mod = p.wide(modulus(t, e))
+        h = {k: mod * v for k, v in between(total, change).items()}
+        if outer is not None:
+            rest = p.wide(outer(t, e))
+            for k, v in share(near, -1).items():
+                h[k] = h[k] - rest * v if k[0] == 0 else h[k] + rest * v
+        return h
+
+    spread(p, forces, count, sign, emit)
+
+
+def single(p, ref, modulus, count, sign, emit):
+    def forces(e, t):
+        mod = p.wide(modulus(t, e))
+        return {k: mod * v for k, v in share(modes_y(p, ref, count, e, t, False), 1).items()}
+
+    spread(p, forces, count, sign, emit)
 
 
 OWN, PARTNER, RECEIVED, NEAR, FAR, SCALE, BEYOND, PAST, SCALE_FAR = range(9)
@@ -607,12 +577,8 @@
         def emit(t, comp, r, v):
             part_ref[(comp * (count - 2) + r) * T + t, 0:C, :] = v
 
-        def more(t, comp, r, v):
-            at = (comp * (count - 2) + r) * T + t
-            part_ref[at, 0:C, :] = part_ref[at, 0:C, :] + v
-
-        layer(p, modes_ref, other_ref, False, lambda t, e: static(p, st_ref, NEAR, t, e + shift), count, sign, emit)
-        single(p, modes_ref, lambda t, e: static(p, st_ref, FAR, t, e + shift), count, -sign, -1, more)
+        near, far = (lambda t, e, kind=kind: static(p, st_ref, kind, t, e + shift) for kind in (NEAR, FAR))
+        layer(p, modes_ref, other_ref, False, near, count, sign, emit, far)
 
     def far_apply(load, own_ref, st_ref, part_ref, other_ref, per, count, shift, emit):
         _, sign = place()
@@ -624,7 +590,7 @@
             here = p.tile(own_ref, t * per, count, comp, r + 1)
             emit(t, comp, r, mov * force + (1.0 - mov) * here, here)
 
-        single(p, other_ref, lambda t, e: static(p, st_ref, FAR, t, e + shift), count, -sign, 1, finish)
+        single(p, other_ref, lambda t, e: static(p, st_ref, FAR, t, e + shift), count, -sign, finish)
 
     far_d = planes_along(dir0)
     par_d = cores(dir0)
@@ -669,12 +635,8 @@
         def emit(t, comp, r, v):
             part_ref[(comp * R2 + r) * T + t, 0:C, :] = v
 
-        def more(t, comp, r, v):
-            at = (comp * R2 + r) * T + t
-            part_ref[at, 0:C, :] = part_ref[at, 0:C, :] + v
-
-        layer(p, far_ref, own_ref, True, lambda t, e: static(p, st_ref, FAR, t, e + 1), R1, sign, emit)
-        single(p, far_ref, lambda t, e: static(p, st_ref, PAST, t, e + 1), R1, -sign, -1, more, True)
+        far, past = (lambda t, e, kind=kind: static(p, st_ref, kind, t, e + 1) for kind in (FAR, PAST))
+        layer(p, far_ref, own_ref, True, far, R1, sign, emit, past)
 
     (part_far,) = call(across_body, [(D * R2 * T, 8, W)], [modes_far, modes1, consts], flops=10**6)
 
@@ -685,8 +647,7 @@
             table = jnp.where(lane == number * C + j, column, table)
         return table
 
-    def gram_body(d_ref, q_ref, r_ref, w_ref, g_ref, mine_ref, send_ref):
-        core = lax.axis_index("gz")
+    def gram_body(d_ref, q_ref, r_ref, w_ref, g_ref):
         lane = p.lanes()
         sums = [[jnp.zeros((C, W), F32) for _ in range(C)] for _ in range(3)]
         for t in range(T):
@@ -703,27 +664,19 @@
         table = columns(0, sums[0], lane) + columns(1, sums[1], lane) + columns(2, sums[2], lane)
         g_ref[...] = jnp.zeros((8, W), F32)
         g_ref[0:C, :] = table
-        for out, t in ((mine_ref, core), (send_ref, 1 - core)):
-            for number, src in enumerate((r_ref, q_ref)):
-                out[number * N3 : (number + 1) * N3, :] = src[pl.ds(pl.multiple_of(t * N3, 8), N3), :]
-            for comp in range(D):
-                for r in range(Y):
-                    p.put(out, 2 * N3, Y, comp, r, p.tile(d_ref, t * N1, R1, comp, r + 2))
-                    p.put(out, 3 * N3, Y, comp, r, p.tile(w_ref, t * N2, R2, comp, r + 1))
-
-    gram3, mine, send = call(gram_body, [(8, W), (4 * N3, W), (4 * N3, W)], [dir0, image0, res0, second], flops=10**6)
+
+    (gram3,) = call(gram_body, [(8, W)], [dir0, image0, res0, second], flops=10**6)
 
     def near_two_body(own_ref, par_ref, st_ref, part_ref, modes_ref, other_ref):
         near_apply(own_ref, par_ref, st_ref, part_ref, modes_ref, other_ref, N2, R2, 2)
 
     (part2,) = call(near_two_body, [(D * Y * T, 8, W)], [second, par_w, consts], [field_shapes(R2)] * 2, flops=10**6)
-    kept = cores(send)
 
     def far_two_body(
         next_ref, far_ref, own_ref, st_ref, part_far_ref, part_ref, gram_ref,
-        mine_ref, send_ref, next_modes_ref, w_ref, other_ref, u_ref,
+        g_ref, u_ref, next_modes_ref, w_ref, other_ref,
     ):
-        core, sign = place()
+        _, sign = place()
         modes_z(
             p,
             lambda t, k, r: p.tile(next_ref, t * N1, R1, k, r),
@@ -741,7 +694,7 @@
             scale = p.wide(static(p, st_ref, SCALE_FAR, t, r + 2))
             w_ref[(comp * R2 + r) * T + t, 0:C, :] = scale * image - here
 
-        single(p, next_modes_ref, lambda t, e: static(p, st_ref, PAST, t, e + 1), R1, -sign, 1, found)
+        single(p, next_modes_ref, lambda t, e: static(p, st_ref, PAST, t, e + 1), R1, -sign, found)
 
         def emit(t, comp, r, image, here):
             p.put(u_ref, t * N3, Y, comp, r, image)
@@ -756,22 +709,34 @@
             for j in range(C):
                 at = t * N2 + (j * D + comp) * R2 + r + 1
                 sums[j] = sums[j] + u * own_ref[at : at + 1, :]
-        table = gram_ref[0:C, :] + columns(3, sums, p.lanes())
+        g_ref[...] = jnp.zeros((8, W), F32)
+        g_ref[0:C, :] = gram_ref[0:C, :] + columns(3, sums, p.lanes())
+
+    table, image2 = call(
+        far_two_body,
+        [(8, W), (T * N3, W)],
+        [next_d, far_d, second, consts, part_far, part2, gram3],
+        [field_shapes(R1), (D * R2 * T, 8, W), field_shapes(R2)],
+        flops=10**6,
+    )
+
+    def pack_body(r_ref, q_ref, d_ref, w_ref, u_ref, mine_ref, send_ref):
+        core = lax.axis_index("gz")
         for out, t in ((mine_ref, core), (send_ref, 1 - core)):
-            out[0:N3, :] = u_ref[pl.ds(pl.multiple_of(t * N3, 8), N3), :]
-            out[N3 : N3 + 8, :] = jnp.zeros((8, W), F32)
-            out[N3 : N3 + C, :] = table
-
-    mine_u, send_u = call(
-        far_two_body,
-        [(N3 + 8, W), (N3 + 8, W)],
-        [next_d, far_d, second, consts, part_far, part2, gram3],
-        [field_shapes(R1), (D * R2 * T, 8, W), field_shapes(R2), (T * N3, W)],
-        flops=10**6,
-    )
-    kept_u = cores(send_u)
-
-    table = mine_u[N3 : N3 + 8, :] + kept_u[N3 : N3 + 8, :]
+            for number, src in enumerate((r_ref, q_ref)):
+                out[number * N3 : (number + 1) * N3, :] = src[pl.ds(pl.multiple_of(t * N3, 8), N3), :]
+            out[4 * N3 : 5 * N3, :] = u_ref[pl.ds(pl.multiple_of(t * N3, 8), N3), :]
+            for comp in range(D):
+                for r in range(Y):
+                    p.put(out, 2 * N3, Y, comp, r, p.tile(d_ref, t * N1, R1, comp, r + 2))
+                    p.put(out, 3 * N3, Y, comp, r, p.tile(w_ref, t * N2, R2, comp, r + 1))
+
+    mine, send = call(
+        pack_body, [(5 * N3, W)] * 2, [res0, image0, dir0, second, image2], flops=10**6
+    )
+    kept = cores(send)
+
+    table = table + cores(table)
 
     def crossed(x, axis, size, step):
         pairs = [(i * T + k, (i ^ step) * T + 1 - k) for i in range(size) for k in range(T)]
@@ -792,7 +757,7 @@
                 step *= 2
 
     def final_body(
-        g_ref, x_ref, mine_ref, mine_u_ref, kept_ref, kept_u_ref, out_hbm, res_hbm, a_ref, out_ref, res_ref, sems
+        g_ref, x_ref, mine_ref, kept_ref, out_hbm, res_hbm, a_ref, out_ref, res_ref, sems
     ):
         core = lax.axis_index("gz")
         lane = lax.broadcasted_iota(jnp.int32, (1, W), 1)
@@ -846,35 +811,39 @@
             for k in range(C):
                 a_ref[i * C + k] = jnp.broadcast_to(v[:, C + k : C + k + 1], (Y, W))
                 a_ref[C * C + i * C + k] = jnp.broadcast_to(on_second[i][:, C + k : C + k + 1], (Y, W))
-        halves = ((mine_ref, mine_u_ref, core), (kept_ref, kept_u_ref, 1 - core))
         moves = []
+        span = D * Q * Y
         for number in range(2):
-            target = (out_ref, res_ref)[number]
-            for src, src_u, plane in halves:
-                for comp in range(D):
-                    fs = [(j * D + comp) * Y for j in range(C)]
-                    at = N3 if number else 2 * N3
-                    v = [src[at + f : at + f + Y, :] for f in fs]
-                    u = [src_u[f : f + Y, :] if number else src[3 * N3 + f : 3 * N3 + f + Y, :] for f in fs]
-                    for i in range(C):
-                        at = pl.ds(pl.multiple_of(((i * D + comp) * Q + plane) * Y, 8), Y)
-                        total = a_ref[i] * v[0] + a_ref[C * C + i] * u[0]
-                        for j in range(1, C):
-                            total = total + (a_ref[j * C + i] * v[j] + a_ref[C * C + j * C + i] * u[j])
+            target, to = ((out_ref, out_hbm), (res_ref, res_hbm))[number]
+            for i in range(C):
+                a = [a_ref[j * C + i] for j in range(C)]
+                b = [a_ref[C * C + j * C + i] for j in range(C)]
+                for src, plane in ((mine_ref, core), (kept_ref, 1 - core)):
+                    for comp in range(D):
+                        at = [(j * D + comp) * Y for j in range(C)]
+                        one, two = (1, 4) if number else (2, 3)
+                        terms = [
+                            a[j] * src[one * N3 + at[j] : one * N3 + at[j] + Y, :]
+                            + b[j] * src[two * N3 + at[j] : two * N3 + at[j] + Y, :]
+                            for j in range(C)
+                        ]
+                        total = sum(terms[1:], terms[0])
+                        rows = pl.ds(pl.multiple_of(((i * D + comp) * Q + plane) * Y, 8), Y)
                         if number:
-                            target[at, :] = src[fs[i] : fs[i] + Y, :] - total
+                            target[rows, :] = src[at[i] : at[i] + Y, :] - total
                         else:
-                            target[at, :] = x_ref[at, :] + total
-            moves.append(pltpu.make_async_copy(target, (out_hbm, res_hbm)[number], sems.at[number]))
-            moves[-1].start()
+                            target[rows, :] = x_ref[rows, :] + total
+                rows = pl.ds(i * span, span)
+                moves.append(pltpu.make_async_copy(target.at[rows], to.at[rows], sems.at[number * C + i]))
+                moves[-1].start()
         for move in moves:
             move.wait()
 
     out, res = call(
         final_body,
         [(n_raw, W)] * 2,
-        [table, z_msg, mine, mine_u, kept, kept_u],
-        [(2 * C * C, Y, W), (n_raw, W), (n_raw, W), pltpu.SemaphoreType.DMA((2,))],
+        [table, z_msg, mine, kept],
+        [(2 * C * C, Y, W), (n_raw, W), (n_raw, W), pltpu.SemaphoreType.DMA((2 * C,))],
         flops=10**5,
         far_out=True,
     )

time: 39.1 us -> 39.5 us (1.010)
  waiting for transfers between devices: 13.1 us -> 13.9 us
    ppermute x6, waiting for transfers between devices: 2.04 us -> 2.55 us  [cores(): return lax.ppermute(x, 'gz', [(i, 1 - i) for i in range(T)])]
    pallas_call x13 -> x14, Pallas kernels: 9.62 us -> 9.39 us  [call(): pl.pallas_call(body, out_shape=[jax.ShapeDtypeStruct(s, F32) if far_out e...]
  transfers between devices with their start and end apart: 15 -> 15, of which waited for: 9 -> 9; matrix products, arithmetic and copies ran while one was open for 0% -> 0% of each run, Pallas kernels for 13% -> 12%
where the time goes in v3:
time: 39.5 us; the launch traced here: 39.3 us
  starting transfers between devices  15.3 us (39%)
  waiting for transfers between devices  13.9 us (35%)
  Pallas kernels  9.39 us (24%)
  between operations  0.73 us (2%)
    pallas_call x14, Pallas kernels, call(): pl.pallas_call(body, out_shape=[jax.ShapeDtypeStruct(s, F32) if far_out e...  9.39 us
    ppermute x4, starting transfers between devices, crossed(): return lax.ppermute(x, (axis, 'gz'), pairs)  5.59 us
    ppermute x4, waiting for transfers between devices, crossed(): return lax.ppermute(x, (axis, 'gz'), pairs)  4.92 us
    ppermute x4, starting transfers between devices, planes_along(): return lax.ppermute(x, ('gx', 'gy', 'gz'), pairs)  4.66 us
    ppermute x4, waiting for transfers between devices, planes_along(): return lax.ppermute(x, ('gx', 'gy', 'gz'), pairs)  3.4 us
    ppermute x1, waiting for transfers between devices, rows_along(): lax.ppermute(x, 'gy', [(i, (i + step) % p.ngy) for i in range(p.ngy)])  3.02 us
    ppermute x1, starting transfers between devices, rows_along(): lax.ppermute(x, 'gy', [(i, (i + step) % p.ngy) for i in range(p.ngy)])  2.91 us
    ppermute x6, waiting for transfers between devices, cores(): return lax.ppermute(x, 'gz', [(i, 1 - i) for i in range(T)])  2.55 us
  transfers between devices with their start and end apart: 15, of which 9 were waited for; matrix products, arithmetic and copies ran while one was open for 0% of the time, Pallas kernels for 12%

profile of v3, /device:TPU:0, one launch (start us, length us, event | category | flops | bytes accessed | tf_op | source)
XLA Modules:
  0.0 39.3 jit_solution(12691699402206227710)
XLA Ops:
  0.6 1.0 %shard_map.77 = (f32[464,128]{1,0:T(8,128)S(1)}, f32[288,128]{1,0:T(8,128)S(1)}) custom-call(f32[288,128]{1,0:T(8,128)} %bitcast.8, f32[288,128]{1,0:T(8,128)} %bitcast.9, s32[16,128]{1,0:T(8,128)} %bitcast.10, s32[16,128]{1,0:T(8,128)} %bitcast.11), custom_call_target="tpu_custom_call" | custom-call | flops 100000 | tf_op jit(solution)/shard_map/pallas_call | solution.py:29
  1.7 0.6 %collective-permute-start = (f32[464,128]{1,0:T(8,128)S(1)}, f32[464,128]{1,0:T(8,128)S(1)}, u32[]{:S(2)}, u32[]{:S(2)}) collective-permute-start(f32[464,128]{1,0:T(8,128)S(1)} %get-tuple-element.24.s_ref.x_ref), channel_id=1, source_target_pairs={{0,1},{1,0},{2,3},{3,2},{4,5},{5,4},{6,7},{7,6},{8,9},{9,8},{10,11... | collective-permute-start | bytes 712712 | tf_op jit(solution)/shard_map/ppermute | solution.py:284
  2.2 1.1 %collective-permute-done.z_ref = f32[464,128]{1,0:T(8,128)S(1)} collective-permute-done((f32[464,128]{1,0:T(8,128)S(1)}, f32[464,128]{1,0:T(8,128)S(1)}, u32[]{:S(2)}, u32[]{:S(2)}) %collective-permute-start) | collective-permute-done | bytes 237600 | tf_op jit(solution)/shard_map/ppermute | solution.py:284
  3.6 2.9 %collective-permute-start.2 = (f32[192,128]{1,0:T(8,128)S(1)}, f32[192,128]{1,0:T(8,128)S(1)}, u32[]{:S(2)}, u32[]{:S(2)}) collective-permute-start(f32[192,128]{1,0:T(8,128)S(1)} %get-tuple-element.28), channel_id=1, source_target_pairs={{0,2},{2,0},{1,3},{3,1},{4,6},{6,4},{5,7},{7,5},{8,10},{10,8},{9,1... | collective-permute-start | bytes 294920 | tf_op jit(solution)/shard_map/ppermute | solution.py:287
  6.5 3.0 %collective-permute-done.2.refs_0_ = f32[192,128]{1,0:T(8,128)S(1)} collective-permute-done((f32[192,128]{1,0:T(8,128)S(1)}, f32[192,128]{1,0:T(8,128)S(1)}, u32[]{:S(2)}, u32[]{:S(2)}) %collective-permute-start.2) | collective-permute-done | bytes 98336 | tf_op jit(solution)/shard_map/ppermute | solution.py:287
  9.6 1.7 %collective-permute-start.4 = (f32[144,128]{1,0:T(8,128)S(1)}, f32[144,128]{1,0:T(8,128)S(1)}, u32[]{:S(2)}, u32[]{:S(2)}) collective-permute-start(f32[144,128]{1,0:T(8,128)S(1)} %get-tuple-element.31), channel_id=1, source_target_pairs={{0,2},{1,6},{2,0},{3,4},{4,3},{5,10},{6,1},{7,8},{8,7},{9,14},{10,... | collective-permute-start | bytes 221192 | tf_op jit(solution)/shard_map/ppermute | solution.py:305
  11.9 0.8 %shard_map.79 = (f32[168,8,128]{2,1,0:T(8,128)S(1)}, f32[72,8,128]{2,1,0:T(8,128)S(1)}) custom-call(f32[352,128]{1,0:T(8,128)S(1)} %get-tuple-element.26.own_m_ref, f32[352,128]{1,0:T(8,128)S(1)} %get-tuple-element.27.par_m_ref, f32[192,128]{1,0:T(8,128)S(1)} %collective-permute-done.2.refs_0_, f32[192,128]{1,0:T(8,128)S(1)} %collective-permute-done.3.refs_1_), custom_call_target="tpu_custom_call" | custom-call | flops 1000000 | tf_op jit(solution)/shard_map/pallas_call | solution.py:29
  12.7 1.2 %collective-permute-done.4.refs_2_ = f32[144,128]{1,0:T(8,128)S(1)} collective-permute-done((f32[144,128]{1,0:T(8,128)S(1)}, f32[144,128]{1,0:T(8,128)S(1)}, u32[]{:S(2)}, u32[]{:S(2)}) %collective-permute-start.4) | collective-permute-done | bytes 73760 | tf_op jit(solution)/shard_map/ppermute | solution.py:305
  13.9 0.8 %shard_map.82 = (f32[288,128]{1,0:T(8,128)S(1)}, f32[432,128]{1,0:T(8,128)S(1)}, f32[288,128]{1,0:T(8,128)S(1)}) custom-call(f32[352,128]{1,0:T(8,128)S(1)} %collective-permute-done.1.far_m_ref, f32[352,128]{1,0:T(8,128)S(1)} %get-tuple-element.26.own_m_ref, f32[352,128]{1,0:T(8,128)S(1)} %get-tuple-element.27.par_m_ref, ...), custom_call_target="tpu_custom_call" | custom-call | flops 1000000 | tf_op jit(solution)/shard_map/pallas_call | solution.py:29
  14.7 0.9 %collective-permute-start.5 = (f32[432,128]{1,0:T(8,128)S(1)}, f32[432,128]{1,0:T(8,128)S(1)}, u32[]{:S(2)}, u32[]{:S(2)}) collective-permute-start(f32[432,128]{1,0:T(8,128)S(1)} %get-tuple-element.32.own_ref.d_ref), channel_id=1, source_target_pairs={{0,1},{1,0},{2,3},{3,2},{4,5},{5,4},{6,7},{7,6},{8,9},{9,8},{10,11... | collective-permute-start | bytes 663560 | tf_op jit(solution)/shard_map/ppermute | solution.py:284
  15.6 1.7 %collective-permute-start.7 = (f32[432,128]{1,0:T(8,128)S(1)}, f32[432,128]{1,0:T(8,128)S(1)}, u32[]{:S(2)}, u32[]{:S(2)}) collective-permute-start(f32[432,128]{1,0:T(8,128)S(1)} %get-tuple-element.32.own_ref.d_ref), channel_id=1, source_target_pairs={{0,2},{1,4},{2,0},{3,6},{4,1},{5,8},{6,3},{7,10},{8,5},{9,12},{10,... | collective-permute-start | bytes 663560 | tf_op jit(solution)/shard_map/ppermute | solution.py:305
  17.4 1.1 %collective-permute-start.6 = (f32[432,128]{1,0:T(8,128)S(1)}, f32[432,128]{1,0:T(8,128)S(1)}, u32[]{:S(2)}, u32[]{:S(2)}) collective-permute-start(f32[432,128]{1,0:T(8,128)S(1)} %collective-permute-done.5.par_ref), channel_id=1, source_target_pairs={{0,2},{1,4},{2,0},{3,6},{4,1},{5,8},{6,3},{7,10},{8,5},{9,12},{10,... | collective-permute-start | bytes 663560 | tf_op jit(solution)/shard_map/ppermute | solution.py:305
  18.5 0.9 %shard_map.83 = (f32[60,8,128]{2,1,0:T(8,128)S(1)}, f32[144,8,128]{2,1,0:T(8,128)S(1)}) custom-call(f32[432,128]{1,0:T(8,128)S(1)} %get-tuple-element.32.own_ref.d_ref, f32[432,128]{1,0:T(8,128)S(1)} %collective-permute-done.5.par_ref, f32[288,128]{1,0:T(8,128)S(1)} %get-tuple-element.33.st_ref), custom_call_target="tpu_custom_call" | custom-call | flops 1000000 | tf_op jit(solution)/shard_map/pallas_call | solution.py:29
  19.4 2.2 %collective-permute-done.7.far_ref = f32[432,128]{1,0:T(8,128)S(1)} collective-permute-done((f32[432,128]{1,0:T(8,128)S(1)}, f32[432,128]{1,0:T(8,128)S(1)}, u32[]{:S(2)}, u32[]{:S(2)}) %collective-permute-start.7) | collective-permute-done | bytes 221216 | tf_op jit(solution)/shard_map/ppermute | solution.py:305
  22.2 0.7 %shard_map.85.part_far_ref = f32[60,8,128]{2,1,0:T(8,128)S(1)} custom-call(f32[144,8,128]{2,1,0:T(8,128)S(1)} %get-tuple-element.36.far_ref, f32[144,8,128]{2,1,0:T(8,128)S(1)} %get-tuple-element.37.own_ref, f32[288,128]{1,0:T(8,128)S(1)} %get-tuple-element.33.st_ref), custom_call_target="tpu_custom_call" | custom-call | flops 1000000 | tf_op jit(solution)/shard_map/pallas_call | solution.py:29
  23.6 0.8 %shard_map.86.part_ref = f32[48,8,128]{2,1,0:T(8,128)S(1)} custom-call(f32[368,128]{1,0:T(8,128)S(1)} %get-tuple-element.35.own_ref.w_ref, f32[368,128]{1,0:T(8,128)S(1)} %collective-permute-done.8.par_ref, f32[288,128]{1,0:T(8,128)S(1)} %get-tuple-element.33.st_ref), custom_call_target="tpu_custom_call" | custom-call | flops 1000000 | tf_op jit(solution)/shard_map/pallas_call | solution.py:29
  24.4 1.1 %shard_map.88 = (f32[8,128]{1,0:T(8,128)S(1)}, f32[288,128]{1,0:T(8,128)S(1)}) custom-call(f32[432,128]{1,0:T(8,128)S(1)} %collective-permute-done.6.next_ref, f32[432,128]{1,0:T(8,128)S(1)} %collective-permute-done.7.far_ref, f32[368,128]{1,0:T(8,128)S(1)} %get-tuple-element.35.own_ref.w_ref, f32[288,128]{1,0:T(8,128)S(1)} %get-tuple-element.33.st_ref, ...), custom_call_target="tpu_custom_call" | custom-call | flops 1000000 | tf_op jit(solution)/shard_map/pallas_call | solution.py:29
  26.1 1.2 %collective-permute-done.9 = f32[8,128]{1,0:T(8,128)S(1)} collective-permute-done((f32[8,128]{1,0:T(8,128)S(1)}, f32[8,128]{1,0:T(8,128)S(1)}, u32[]{:S(2)}, u32[]{:S(2)}) %collective-permute-start.9) | collective-permute-done | bytes 4128 | tf_op jit(solution)/shard_map/ppermute | solution.py:284
  27.3 1.6 %collective-permute-start.10 = (f32[8,128]{1,0:T(8,128)S(1)}, f32[8,128]{1,0:T(8,128)S(1)}, u32[]{:S(2)}, u32[]{:S(2)}) collective-permute-start(f32[8,128]{1,0:T(8,128)S(1)} %add.15), channel_id=1, source_target_pairs={{0,3},{1,2},{2,1},{3,0},{4,7},{5,6},{6,5},{7,4},{8,11},{9,10},{10,... | collective-permute-start | bytes 12296 | tf_op jit(solution)/shard_map/ppermute | solution.py:743
  28.9 1.4 %collective-permute-done.10 = f32[8,128]{1,0:T(8,128)S(1)} collective-permute-done((f32[8,128]{1,0:T(8,128)S(1)}, f32[8,128]{1,0:T(8,128)S(1)}, u32[]{:S(2)}, u32[]{:S(2)}) %collective-permute-start.10) | collective-permute-done | bytes 4128 | tf_op jit(solution)/shard_map/ppermute | solution.py:743
  30.3 3.5 %collective-permute-start.13 = (f32[8,128]{1,0:T(8,128)S(1)}, f32[8,128]{1,0:T(8,128)S(1)}, u32[]{:S(2)}, u32[]{:S(2)}) collective-permute-start(f32[8,128]{1,0:T(8,128)S(1)} %add.16), channel_id=1, source_target_pairs={{0,13},{1,12},{4,9},{5,8},{8,5},{9,4},{12,1},{13,0},{2,15},{3,14},... | collective-permute-start | bytes 12296 | tf_op jit(solution)/shard_map/ppermute | solution.py:743
  34.3 0.9 %collective-permute-done.13 = f32[8,128]{1,0:T(8,128)S(1)} collective-permute-done((f32[8,128]{1,0:T(8,128)S(1)}, f32[8,128]{1,0:T(8,128)S(1)}, u32[]{:S(2)}, u32[]{:S(2)}) %collective-permute-start.13) | collective-permute-done | bytes 4128 | tf_op jit(solution)/shard_map/ppermute | solution.py:743
  35.2 2.6 %collective-permute-done.12 = f32[8,128]{1,0:T(8,128)S(1)} collective-permute-done((f32[8,128]{1,0:T(8,128)S(1)}, f32[8,128]{1,0:T(8,128)S(1)}, u32[]{:S(2)}, u32[]{:S(2)}) %collective-permute-start.12) | collective-permute-done | bytes 4128 | tf_op jit(solution)/shard_map/ppermute | solution.py:743
  37.8 1.5 %shard_map.90 = (f32[288,128]{1,0:T(8,128)}, f32[288,128]{1,0:T(8,128)}) custom-call(f32[8,128]{1,0:T(8,128)S(1)} %add_add_fusion.g_ref, f32[464,128]{1,0:T(8,128)S(1)} %get-tuple-element.24.s_ref.x_ref, f32[720,128]{1,0:T(8,128)S(1)} %get-tuple-element.42.mine_ref, f32[720,128]{1,0:T(8,128)S(1)} %collective-permute-done.14.kept_ref), custom_call_target="tpu_custom_call" | custom-call | flops 100000 | tf_op jit(solution)/shard_map/pallas_call | solution.py:29
  (27 shorter events, 3.3 us)
Async XLA Ops:
  1.7 1.7 %collective-permute-start = (f32[464,128]{1,0:T(8,128)S(1)}, f32[464,128]{1,0:T(8,128)S(1)}, u32[]{:S(2)}, u32[]{:S(2)}) collective-permute-start(f32[464,128]{1,0:T(8,128)S(1)} %get-tuple-element.24.s_ref.x_ref), channel_id=1, source_target_pairs={{0,1},{1,0},{2,3},{3,2},{4,5},{5,4},{6,7},{7,6},{8,9},{9,8},{10,11... | collective-permute-start | bytes 712712 | tf_op jit(solution)/shard_map/ppermute | solution.py:284
  3.4 8.0 %copy-start = (f32[6,16,3]{1,2,0:T(4,128)S(1)}, f32[6,16,3]{1,2,0:T(4,128)}, u32[]{:S(2)}) copy-start(f32[6,16,3]{1,2,0:T(4,128)} %param.11) | copy-start | bytes 3460
  3.5 7.8 %copy-start.1 = (s32[6,16]{1,0:T(8,128)S(1)}, s32[6,16]{1,0:T(8,128)}, u32[]{:S(2)}) copy-start(s32[6,16]{1,0:T(8,128)} %node_ref.1) | copy-start | bytes 1156
  3.6 6.0 %collective-permute-start.2 = (f32[192,128]{1,0:T(8,128)S(1)}, f32[192,128]{1,0:T(8,128)S(1)}, u32[]{:S(2)}, u32[]{:S(2)}) collective-permute-start(f32[192,128]{1,0:T(8,128)S(1)} %get-tuple-element.28), channel_id=1, source_target_pairs={{0,2},{2,0},{1,3},{3,1},{4,6},{6,4},{5,7},{7,5},{8,10},{10,8},{9,1... | collective-permute-start | bytes 294920 | tf_op jit(solution)/shard_map/ppermute | solution.py:287
  6.5 7.5 %collective-permute-start.1 = (f32[352,128]{1,0:T(8,128)S(1)}, f32[352,128]{1,0:T(8,128)S(1)}, u32[]{:S(2)}, u32[]{:S(2)}) collective-permute-start(f32[352,128]{1,0:T(8,128)S(1)} %get-tuple-element.26.own_m_ref), channel_id=1, source_target_pairs={{0,2},{1,4},{2,0},{3,6},{4,1},{5,8},{6,3},{7,10},{8,5},{9,12},{10,... | collective-permute-start | bytes 540680 | tf_op jit(solution)/shard_map/ppermute | solution.py:305
  9.6 2.3 %collective-permute-start.3 = (f32[192,128]{1,0:T(8,128)S(1)}, f32[192,128]{1,0:T(8,128)S(1)}, u32[]{:S(2)}, u32[]{:S(2)}) collective-permute-start(f32[192,128]{1,0:T(8,128)S(1)} %collective-permute-done.2.refs_0_), channel_id=1, source_target_pairs={{0,1},{1,0},{2,3},{3,2},{4,5},{5,4},{6,7},{7,6},{8,9},{9,8},{10,11... | collective-permute-start | bytes 294920 | tf_op jit(solution)/shard_map/ppermute | solution.py:284
  9.6 4.4 %collective-permute-start.4 = (f32[144,128]{1,0:T(8,128)S(1)}, f32[144,128]{1,0:T(8,128)S(1)}, u32[]{:S(2)}, u32[]{:S(2)}) collective-permute-start(f32[144,128]{1,0:T(8,128)S(1)} %get-tuple-element.31), channel_id=1, source_target_pairs={{0,2},{1,6},{2,0},{3,4},{4,3},{5,10},{6,1},{7,8},{8,7},{9,14},{10,... | collective-permute-start | bytes 221192 | tf_op jit(solution)/shard_map/ppermute | solution.py:305
  14.7 2.6 %collective-permute-start.5 = (f32[432,128]{1,0:T(8,128)S(1)}, f32[432,128]{1,0:T(8,128)S(1)}, u32[]{:S(2)}, u32[]{:S(2)}) collective-permute-start(f32[432,128]{1,0:T(8,128)S(1)} %get-tuple-element.32.own_ref.d_ref), channel_id=1, source_target_pairs={{0,1},{1,0},{2,3},{3,2},{4,5},{5,4},{6,7},{7,6},{8,9},{9,8},{10,11... | collective-permute-start | bytes 663560 | tf_op jit(solution)/shard_map/ppermute | solution.py:284
  15.6 5.9 %collective-permute-start.7 = (f32[432,128]{1,0:T(8,128)S(1)}, f32[432,128]{1,0:T(8,128)S(1)}, u32[]{:S(2)}, u32[]{:S(2)}) collective-permute-start(f32[432,128]{1,0:T(8,128)S(1)} %get-tuple-element.32.own_ref.d_ref), channel_id=1, source_target_pairs={{0,2},{1,4},{2,0},{3,6},{4,1},{5,8},{6,3},{7,10},{8,5},{9,12},{10,... | collective-permute-start | bytes 663560 | tf_op jit(solution)/shard_map/ppermute | solution.py:305
  17.4 7.0 %collective-permute-start.6 = (f32[432,128]{1,0:T(8,128)S(1)}, f32[432,128]{1,0:T(8,128)S(1)}, u32[]{:S(2)}, u32[]{:S(2)}) collective-permute-start(f32[432,128]{1,0:T(8,128)S(1)} %collective-permute-done.5.par_ref), channel_id=1, source_target_pairs={{0,2},{1,4},{2,0},{3,6},{4,1},{5,8},{6,3},{7,10},{8,5},{9,12},{10,... | collective-permute-start | bytes 663560 | tf_op jit(solution)/shard_map/ppermute | solution.py:305
  22.1 1.5 %collective-permute-start.8 = (f32[368,128]{1,0:T(8,128)S(1)}, f32[368,128]{1,0:T(8,128)S(1)}, u32[]{:S(2)}, u32[]{:S(2)}) collective-permute-start(f32[368,128]{1,0:T(8,128)S(1)} %get-tuple-element.35.own_ref.w_ref), channel_id=1, source_target_pairs={{0,1},{1,0},{2,3},{3,2},{4,5},{5,4},{6,7},{7,6},{8,9},{9,8},{10,11... | collective-permute-start | bytes 565256 | tf_op jit(solution)/shard_map/ppermute | solution.py:284
  25.5 12.3 %collective-permute-start.14 = (f32[720,128]{1,0:T(8,128)S(1)}, f32[720,128]{1,0:T(8,128)S(1)}, u32[]{:S(2)}, u32[]{:S(2)}) collective-permute-start(f32[720,128]{1,0:T(8,128)S(1)} %get-tuple-element.43), channel_id=1, source_target_pairs={{0,1},{1,0},{2,3},{3,2},{4,5},{5,4},{6,7},{7,6},{8,9},{9,8},{10,11... | collective-permute-start | bytes 1105928 | tf_op jit(solution)/shard_map/ppermute | solution.py:284
  25.9 1.4 %collective-permute-start.9 = (f32[8,128]{1,0:T(8,128)S(1)}, f32[8,128]{1,0:T(8,128)S(1)}, u32[]{:S(2)}, u32[]{:S(2)}) collective-permute-start(f32[8,128]{1,0:T(8,128)S(1)} %get-tuple-element.40), channel_id=1, source_target_pairs={{0,1},{1,0},{2,3},{3,2},{4,5},{5,4},{6,7},{7,6},{8,9},{9,8},{10,11... | collective-permute-start | bytes 12296 | tf_op jit(solution)/shard_map/ppermute | solution.py:284
  27.3 3.0 %collective-permute-start.10 = (f32[8,128]{1,0:T(8,128)S(1)}, f32[8,128]{1,0:T(8,128)S(1)}, u32[]{:S(2)}, u32[]{:S(2)}) collective-permute-start(f32[8,128]{1,0:T(8,128)S(1)} %add.15), channel_id=1, source_target_pairs={{0,3},{1,2},{2,1},{3,0},{4,7},{5,6},{6,5},{7,4},{8,11},{9,10},{10,... | collective-permute-start | bytes 12296 | tf_op jit(solution)/shard_map/ppermute | solution.py:743
  30.3 4.9 %collective-permute-start.13 = (f32[8,128]{1,0:T(8,128)S(1)}, f32[8,128]{1,0:T(8,128)S(1)}, u32[]{:S(2)}, u32[]{:S(2)}) collective-permute-start(f32[8,128]{1,0:T(8,128)S(1)} %add.16), channel_id=1, source_target_pairs={{0,13},{1,12},{4,9},{5,8},{8,5},{9,4},{12,1},{13,0},{2,15},{3,14},... | collective-permute-start | bytes 12296 | tf_op jit(solution)/shard_map/ppermute | solution.py:743
  33.9 3.9 %collective-permute-start.12 = (f32[8,128]{1,0:T(8,128)S(1)}, f32[8,128]{1,0:T(8,128)S(1)}, u32[]{:S(2)}, u32[]{:S(2)}) collective-permute-start(f32[8,128]{1,0:T(8,128)S(1)} %add.16), channel_id=1, source_target_pairs={{0,9},{1,8},{4,13},{5,12},{8,1},{9,0},{12,5},{13,4},{2,11},{3,10},... | collective-permute-start | bytes 12296 | tf_op jit(solution)/shard_map/ppermute | solution.py:743
  33.9 3.9 %collective-permute-start.11 = (f32[8,128]{1,0:T(8,128)S(1)}, f32[8,128]{1,0:T(8,128)S(1)}, u32[]{:S(2)}, u32[]{:S(2)}) collective-permute-start(f32[8,128]{1,0:T(8,128)S(1)} %add.16), channel_id=1, source_target_pairs={{0,5},{1,4},{4,1},{5,0},{8,13},{9,12},{12,9},{13,8},{2,7},{3,6},{6... | collective-permute-start | bytes 12296 | tf_op jit(solution)/shard_map/ppermute | solution.py:743

commit v4 on v3

--- a/solution.py
+++ b/solution.py
@@ -165,6 +165,53 @@
     return found
 
 
+def both_shares(m, inner, outer):
+    x, y, z = m
+    volume = CQ * (y[1, 0] + z[0, 1])
+    pair = z[1, 0] + y[0, 1]
+    sy, sz, sp = CS * y[0, 0], CS * z[0, 0], CS * pair
+    even = {
+        (0, 0, 0): volume,
+        (0, 1, 0): sy + CE * z[1, 1],
+        (0, 0, 1): sz + CE * y[1, 1],
+        (0, 1, 1): CF * pair,
+        (1, 0, 0): sy,
+        (1, 1, 0): volume + ((CB + CD) * y[1, 0] + CE * z[0, 1]),
+        (1, 0, 1): sp + CF * (pair + y[0, 1]),
+        (1, 1, 1): (CD + CG) * y[1, 1],
+        (2, 0, 0): sz,
+        (2, 0, 1): volume + ((CB + CD) * z[0, 1] + CE * y[1, 0]),
+        (2, 1, 0): sp + CF * (pair + z[1, 0]),
+        (2, 1, 1): (CD + CG) * z[1, 1],
+    }
+    q, f = CQ * x[0, 0], CF * x[1, 1]
+    odd = {
+        (0, 0, 0): (CQ + CB) * x[0, 0],
+        (0, 1, 0): (CS + CD) * x[1, 0],
+        (0, 0, 1): (CS + CD) * x[0, 1],
+        (0, 1, 1): (2.0 * CF + CG) * x[1, 1],
+        (1, 0, 0): CS * x[1, 0],
+        (1, 1, 0): q,
+        (1, 0, 1): f,
+        (1, 1, 1): CE * x[0, 1],
+        (2, 0, 0): CS * x[0, 1],
+        (2, 0, 1): q,
+        (2, 1, 0): f,
+        (2, 1, 1): CE * x[1, 0],
+    }
+    total, gap = inner + outer, outer - inner
+    return {k: (gap * v + total * odd[k]) if k[0] == 0 else (total * v + gap * odd[k]) for k, v in even.items()}
+
+
+def twice(p, ref, flip, inner, outer, count, sign, emit):
+    def forces(e, t):
+        return both_shares(
+            modes_y(p, ref, count, e, t, flip), p.wide(inner(t, e)), p.wide(outer(t, e))
+        )
+
+    spread(p, forces, count, sign, emit)
+
+
 def spread(p, forces, count, sign, emit):
     lane = p.lanes()
     carry = {}
@@ -236,6 +283,9 @@
     y_load = y_stat + 6
     y_part = up8(y_load + FL * 2)
     d_part = up8(y_stat + 12)
+    raw_load = Q * FL * 3
+    raw_stat = raw_load + Q * FL * 2
+    raw_rows = up8(raw_stat + Q * 6)
     R0, R1, R2 = Y + 6, Y + 4, Y + 2
     N1, N2, N3 = p.per(R1), p.per(R2), p.per(Y)
     M = p.main
@@ -246,8 +296,17 @@
     de = design.reshape(Q * Y, W)
     su = supports.reshape(Q * Y, W)
 
+    def edges():
+        if both:
+            first = lax.axis_index("gy") == 0
+            return [(jnp.where(first, Y - 3, 0), jnp.where(first, Y - 2, 0))]
+        return [(Y - 3, Y - 2), (0, 0)]
+
+    ways = (1,) if both else (1, -1)
+    halos = len(ways)
+
     def gather_body(x_hbm, b_hbm, d_hbm, s_hbm, z_ref, b_ref, *refs):
-        d_ref, s_ref, sems = refs
+        y_refs, (d_ref, s_ref, sems) = refs[:halos], refs[halos:]
         core = lax.axis_index("gz")
         moves = [
             pltpu.make_async_copy(src, dst, sems.at[i])
@@ -264,16 +323,34 @@
         )
         moves[3].wait()
         z_ref[z_stat + Q * Y : z_rows, :] = 1.0 - s_ref[...].astype(F32)
+        for y_ref, (three, _) in zip(y_refs, edges()):
+            if raw_rows > raw_stat + Q * 6:
+                y_ref[raw_stat + Q * 6 : raw_rows, :] = jnp.zeros((raw_rows - raw_stat - Q * 6, W), F32)
+            for q in range(Q):
+                for kind in range(2):
+                    for r in range(3):
+                        at = raw_stat + q * 6 + kind * 3 + r
+                        y_ref[at : at + 1, :] = z_ref[pl.ds(z_stat + (kind * Q + q) * Y + three + r, 1), :]
+        moves[0].wait()
+        for y_ref, (three, _) in zip(y_refs, edges()):
+            for q in range(Q):
+                for comp in range(D):
+                    for r in range(3):
+                        p.put(y_ref, q * FL * 3, 3, comp, r, p.raw(z_ref, 0, comp, q, three + r))
         moves[1].wait()
+        for y_ref, (_, two) in zip(y_refs, edges()):
+            for q in range(Q):
+                for comp in range(D):
+                    for r in range(2):
+                        p.put(y_ref, raw_load + q * FL * 2, 2, comp, r, p.raw(b_ref, 0, comp, q, two + r))
         for f in range(FL):
             z_ref[z_load + f * Y : z_load + (f + 1) * Y, :] = b_ref[
                 pl.ds(pl.multiple_of((f * Q + 1 - core) * Y, 8), Y), :
             ]
-        moves[0].wait()
-
-    z_msg, b_near = call(
+
+    z_msg, b_near, *y_sent = call(
         gather_body,
-        [(z_rows, W), (n_raw, W)],
+        [(z_rows, W), (n_raw, W)] + [(raw_rows, W)] * halos,
         [x0, bl, de, su],
         [VMEM((Q * Y, W), jnp.int32), VMEM((Q * Y, W), jnp.int32), pltpu.SemaphoreType.DMA((4,))],
         flops=10**5,
@@ -304,42 +381,29 @@
                         pairs.append((mine, mine))
         return lax.ppermute(x, ("gx", "gy", "gz"), pairs)
 
+    y_raw = [rows_along(x, step) for x, step in zip(y_sent, ways)]
     z_got = cores(z_msg)
-
-    def main_body(s_ref, z_ref, b_ref, own_ref, par_ref, *y_refs):
+    zy_raw = [cores(x) for x in y_raw]
+
+    def main_body(s_ref, z_ref, own_ref, par_ref, *d_refs):
         core = lax.axis_index("gz")
-        if both:
-            first = lax.axis_index("gy") == 0
-            froms = [(jnp.where(first, Y - 3, 0), jnp.where(first, Y - 2, 0))]
-        else:
-            froms = [(Y - 3, Y - 2), (0, 0)]
-        count = len(froms)
-        for y_ref, d_ref, (three, two) in zip(y_refs[:count], y_refs[count:], froms):
+        for d_ref, (three, _) in zip(d_refs, edges()):
             for src, half in ((s_ref, core), (z_ref, 1 - core)):
-                at, to = half * y_part, half * d_part
+                to = half * d_part
                 for comp in range(D):
                     for r in range(3):
-                        v = p.raw(src, 0, comp, core, three + r)
-                        p.put(y_ref, at, 3, comp, r, v)
-                        p.put(d_ref, to, 3, comp, r, v)
-                    for r in range(2):
-                        if src is s_ref:
-                            v = p.raw(b_ref, 0, comp, core, two + r)
-                        else:
-                            v = p.tile(src, z_load, Y, comp, two + r)
-                        p.put(y_ref, at + y_load, 2, comp, r, v)
-                for kind in range(2):
+                        p.put(d_ref, to, 3, comp, r, p.raw(src, 0, comp, core, three + r))
+                for kind in range(4):
+                    of = core if kind < 2 else 1 - core
                     for r in range(3):
-                        v = src[pl.ds(z_stat + (kind * Q + core) * Y + three + r, 1), :]
-                        y_ref[pl.ds(at + y_stat + kind * 3 + r, 1), :] = v
-                        d_ref[pl.ds(to + y_stat + kind * 3 + r, 1), :] = v
-                        d_ref[pl.ds(to + y_stat + 6 + kind * 3 + r, 1), :] = src[
-                            pl.ds(z_stat + (kind * Q + 1 - core) * Y + three + r, 1), :
+                        d_ref[pl.ds(to + y_stat + kind * 3 + r, 1), :] = src[
+                            pl.ds(z_stat + (kind % 2 * Q + of) * Y + three + r, 1), :
                         ]
             for t in range(T):
-                for ref, part, used in ((y_ref, y_part, y_load + FL * 2), (d_ref, d_part, y_stat + 12)):
-                    if part > used:
-                        ref[t * part + used : (t + 1) * part, :] = jnp.zeros((part - used, W), F32)
+                if d_part > y_stat + 12:
+                    d_ref[t * d_part + y_stat + 12 : (t + 1) * d_part, :] = jnp.zeros(
+                        (d_part - y_stat - 12, W), F32
+                    )
         for out, plane in ((own_ref, core), (par_ref, 1 - core)):
             for src, half in ((s_ref, core), (z_ref, 1 - core)):
                 base = half * M
@@ -352,18 +416,30 @@
                         pl.ds(pl.multiple_of(z_stat + (kind % 2 * Q + of) * Y, 8), Y), :
                     ]
 
-    ways = (1,) if both else (1, -1)
-    halos = len(ways)
     own_m, par_m, *sent = call(
-        main_body,
-        [(T * M, W)] * 2 + [(T * y_part, W)] * halos + [(T * d_part, W)] * halos,
-        [z_msg, z_got, b_near],
-        flops=10**5,
-    )
-    y_got = [rows_along(x, step) for x, step in zip(sent, ways)]
+        main_body, [(T * M, W)] * 2 + [(T * d_part, W)] * halos, [z_msg, z_got], flops=10**5
+    )
+    far_y = [planes_along(x, step) for x, step in zip(sent, ways)]
     far_m = planes_along(own_m)
-    far_y = [planes_along(x, step) for x, step in zip(sent[halos:], ways)]
-    par_y = [cores(x) for x in y_got]
+
+    def rows_body(*refs):
+        core = lax.axis_index("gz")
+        outs = refs[2 * halos :]
+        for n in range(halos):
+            for out, plane in ((outs[n], core), (outs[halos + n], 1 - core)):
+                for src, half in ((refs[n], core), (refs[halos + n], 1 - core)):
+                    to = half * y_part
+                    for comp in range(D):
+                        for r in range(3):
+                            p.put(out, to, 3, comp, r, p.tile(src, plane * (FL * 3), 3, comp, r))
+                        for r in range(2):
+                            v = p.tile(src, raw_load + plane * (FL * 2), 2, comp, r)
+                            p.put(out, to + y_load, 2, comp, r, v)
+                    for r in range(6):
+                        out[pl.ds(to + y_stat + r, 1), :] = src[pl.ds(raw_stat + plane * 6 + r, 1), :]
+
+    got = call(rows_body, [(T * y_part, W)] * (2 * halos), y_raw + zy_raw, flops=10**5)
+    y_got, par_y = list(got[:halos]), list(got[halos:])
 
     def halo(main, refs, part):
         row = lax.axis_index("gy")
@@ -629,16 +705,29 @@
     )
     par_w = cores(second)
 
-    def across_body(far_ref, own_ref, st_ref, part_ref):
+    def beside_body(own_ref, st_ref, part_ref):
         _, sign = place()
 
         def emit(t, comp, r, v):
             part_ref[(comp * R2 + r) * T + t, 0:C, :] = v
 
+        single(p, own_ref, lambda t, e: static(p, st_ref, FAR, t, e + 1), R1, sign, emit)
+
+    (part_beside,) = call(beside_body, [(D * R2 * T, 8, W)], [modes1, consts], flops=10**6)
+
+    def across_body(far_ref, beside_ref, st_ref, part_ref):
+        _, sign = place()
+
+        def emit(t, comp, r, v):
+            at = (comp * R2 + r) * T + t
+            part_ref[at, 0:C, :] = beside_ref[at, 0:C, :] + v
+
         far, past = (lambda t, e, kind=kind: static(p, st_ref, kind, t, e + 1) for kind in (FAR, PAST))
-        layer(p, far_ref, own_ref, True, far, R1, sign, emit, past)
-
-    (part_far,) = call(across_body, [(D * R2 * T, 8, W)], [modes_far, modes1, consts], flops=10**6)
+        twice(p, far_ref, True, far, past, R1, sign, emit)
+
+    (part_far,) = call(
+        across_body, [(D * R2 * T, 8, W)], [modes_far, part_beside, consts], flops=10**6
+    )
 
     def columns(number, sums, lane):
         table = jnp.zeros((C, W), F32)
@@ -647,9 +736,23 @@
             table = jnp.where(lane == number * C + j, column, table)
         return table
 
-    def gram_body(d_ref, q_ref, r_ref, w_ref, g_ref):
+    def first_gram_body(d_ref, r_ref, g_ref):
+        sums = [jnp.zeros((C, W), F32) for _ in range(C)]
+        for t in range(T):
+            for comp in range(D):
+                for r in range(Y):
+                    d = p.tile(d_ref, t * N1, R1, comp, r + 2)
+                    for j in range(C):
+                        at = t * N3 + (j * D + comp) * Y + r
+                        sums[j] = sums[j] + d * r_ref[at : at + 1, :]
+        g_ref[...] = jnp.zeros((8, W), F32)
+        g_ref[0:C, :] = columns(1, sums, p.lanes())
+
+    (gram1,) = call(first_gram_body, [(8, W)], [dir0, res0], flops=10**6)
+
+    def gram_body(d_ref, q_ref, w_ref, first_ref, g_ref):
         lane = p.lanes()
-        sums = [[jnp.zeros((C, W), F32) for _ in range(C)] for _ in range(3)]
+        sums = [[jnp.zeros((C, W), F32) for _ in range(C)] for _ in range(2)]
         for t in range(T):
             for comp in range(D):
                 for r in range(Y):
@@ -659,18 +762,53 @@
                         at = t * N3 + (j * D + comp) * Y + r
                         q = q_ref[at : at + 1, :]
                         sums[0][j] = sums[0][j] + d * q
-                        sums[1][j] = sums[1][j] + d * r_ref[at : at + 1, :]
-                        sums[2][j] = sums[2][j] + w * q
-        table = columns(0, sums[0], lane) + columns(1, sums[1], lane) + columns(2, sums[2], lane)
-        g_ref[...] = jnp.zeros((8, W), F32)
-        g_ref[0:C, :] = table
-
-    (gram3,) = call(gram_body, [(8, W)], [dir0, image0, res0, second], flops=10**6)
-
-    def near_two_body(own_ref, par_ref, st_ref, part_ref, modes_ref, other_ref):
-        near_apply(own_ref, par_ref, st_ref, part_ref, modes_ref, other_ref, N2, R2, 2)
-
-    (part2,) = call(near_two_body, [(D * Y * T, 8, W)], [second, par_w, consts], [field_shapes(R2)] * 2, flops=10**6)
+                        sums[1][j] = sums[1][j] + w * q
+        g_ref[...] = first_ref[...]
+        g_ref[0:C, :] = first_ref[0:C, :] + columns(0, sums[0], lane) + columns(2, sums[1], lane)
+
+    (gram3,) = call(gram_body, [(8, W)], [dir0, image0, second, gram1], flops=10**6)
+
+    def own_two_body(own_ref, st_ref, part_ref, modes_ref):
+        _, sign = place()
+        modes_z(
+            p,
+            lambda t, k, r: p.tile(own_ref, t * N2, R2, k, r),
+            lambda t, r: static(p, st_ref, OWN, t, r + 2),
+            R2,
+            sign,
+            modes_ref,
+        )
+
+        def emit(t, comp, r, v):
+            part_ref[(comp * Y + r) * T + t, 0:C, :] = v
+
+        near, far = (lambda t, e, kind=kind: static(p, st_ref, kind, t, e + 2) for kind in (NEAR, FAR))
+        twice(p, modes_ref, False, near, far, R2, sign, emit)
+
+    (part_own,) = call(
+        own_two_body, [(D * Y * T, 8, W)], [second, consts], [field_shapes(R2)], flops=10**6
+    )
+
+    def near_two_body(par_ref, st_ref, own_part_ref, part_ref, modes_ref):
+        _, sign = place()
+        modes_z(
+            p,
+            lambda t, k, r: p.tile(par_ref, t * N2, R2, k, r),
+            lambda t, r: static(p, st_ref, PARTNER, t, r + 2),
+            R2,
+            sign,
+            modes_ref,
+        )
+
+        def emit(t, comp, r, v):
+            at = (comp * Y + r) * T + t
+            part_ref[at, 0:C, :] = own_part_ref[at, 0:C, :] + v
+
+        single(p, modes_ref, lambda t, e: static(p, st_ref, NEAR, t, e + 2), R2, sign, emit)
+
+    (part2,) = call(
+        near_two_body, [(D * Y * T, 8, W)], [par_w, consts, part_own], [field_shapes(R2)], flops=10**6
+    )
 
     def far_two_body(
         next_ref, far_ref, own_ref, st_ref, part_far_ref, part_ref, gram_ref,

time: 39.5 us -> 38.1 us (0.965)
  waiting for transfers between devices: 13.9 us -> 10.8 us
  starting transfers between devices: 15.3 us -> 16.6 us
    ppermute x4, starting transfers between devices: 4.66 us -> 6.07 us  [planes_along(): return lax.ppermute(x, ('gx', 'gy', 'gz'), pairs)]
    ppermute x6, waiting for transfers between devices: 2.55 us -> 1.25 us  [cores(): return lax.ppermute(x, 'gz', [(i, 1 - i) for i in range(T)])]
    ppermute x1, waiting for transfers between devices: 3.02 us -> 1.73 us  [rows_along(): lax.ppermute(x, 'gy', [(i, (i + step) % p.ngy) for i in range(p.ngy)])]
    pallas_call x14 -> x18, Pallas kernels: 9.39 us -> 9.7 us  [call(): pl.pallas_call(body, out_shape=[jax.ShapeDtypeStruct(s, F32) if far_out e...]
  transfers between devices with their start and end apart: 15 -> 15, of which waited for: 9 -> 7; matrix products, arithmetic and copies ran while one was open for 0% -> 0% of each run, Pallas kernels for 12% -> 14%
where the time goes in v4:
time: 38.1 us; the launch traced here: 37.9 us
  starting transfers between devices  16.6 us (44%)
  waiting for transfers between devices  10.8 us (28%)
  Pallas kernels  9.7 us (25%)
  between operations  0.75 us (2%)
    pallas_call x18, Pallas kernels, call(): pl.pallas_call(body, out_shape=[jax.ShapeDtypeStruct(s, F32) if far_out e...  9.7 us
    ppermute x4, starting transfers between devices, planes_along(): return lax.ppermute(x, ('gx', 'gy', 'gz'), pairs)  6.07 us
    ppermute x4, starting transfers between devices, crossed(): return lax.ppermute(x, (axis, 'gz'), pairs)  5.79 us
    ppermute x4, waiting for transfers between devices, crossed(): return lax.ppermute(x, (axis, 'gz'), pairs)  4.54 us
    ppermute x4, waiting for transfers between devices, planes_along(): return lax.ppermute(x, ('gx', 'gy', 'gz'), pairs)  3.32 us
    ppermute x1, starting transfers between devices, rows_along(): lax.ppermute(x, 'gy', [(i, (i + step) % p.ngy) for i in range(p.ngy)])  2.55 us
    ppermute x6, starting transfers between devices, cores(): return lax.ppermute(x, 'gz', [(i, 1 - i) for i in range(T)])  2.18 us
    ppermute x1, waiting for transfers between devices, rows_along(): lax.ppermute(x, 'gy', [(i, (i + step) % p.ngy) for i in range(p.ngy)])  1.73 us
  transfers between devices with their start and end apart: 15, of which 7 were waited for; matrix products, arithmetic and copies ran while one was open for 0% of the time, Pallas kernels for 14%

profile of v4, /device:TPU:0, one launch (start us, length us, event | category | flops | bytes accessed | tf_op | source)
XLA Modules:
  0.0 37.9 jit_solution(5490751863522683169)
XLA Ops:
  0.6 1.0 %shard_map.77 = (f32[464,128]{1,0:T(8,128)S(1)}, f32[288,128]{1,0:T(8,128)S(1)}, f32[192,128]{1,0:T(8,128)S(1)}) custom-call(f32[288,128]{1,0:T(8,128)} %bitcast.8, f32[288,128]{1,0:T(8,128)} %bitcast.9, s32[16,128]{1,0:T(8,128)} %bitcast.10, s32[16,128]{1,0:T(8,128)} %bitcast.11), custom_call_target="tpu_custom_call" | custom-call | flops 100000 | tf_op jit(solution)/shard_map/pallas_call | solution.py:29
  1.7 0.6 %collective-permute-start = (f32[464,128]{1,0:T(8,128)S(1)}, f32[464,128]{1,0:T(8,128)S(1)}, u32[]{:S(2)}, u32[]{:S(2)}) collective-permute-start(f32[464,128]{1,0:T(8,128)S(1)} %get-tuple-element.26.s_ref.x_ref), channel_id=1, source_target_pairs={{0,1},{1,0},{2,3},{3,2},{4,5},{5,4},{6,7},{7,6},{8,9},{9,8},{10,11... | collective-permute-start | bytes 712712 | tf_op jit(solution)/shard_map/ppermute | solution.py:361
  2.2 2.6 %collective-permute-start.2 = (f32[192,128]{1,0:T(8,128)S(1)}, f32[192,128]{1,0:T(8,128)S(1)}, u32[]{:S(2)}, u32[]{:S(2)}) collective-permute-start(f32[192,128]{1,0:T(8,128)S(1)} %get-tuple-element.29), channel_id=1, source_target_pairs={{0,2},{2,0},{1,3},{3,1},{4,6},{6,4},{5,7},{7,5},{8,10},{10,8},{9,1... | collective-permute-start | bytes 294920 | tf_op jit(solution)/shard_map/ppermute | solution.py:364
  5.0 1.5 %collective-permute-start.1 = (f32[352,128]{1,0:T(8,128)S(1)}, f32[352,128]{1,0:T(8,128)S(1)}, u32[]{:S(2)}, u32[]{:S(2)}) collective-permute-start(f32[352,128]{1,0:T(8,128)S(1)} %get-tuple-element.27.own_m_ref), channel_id=1, source_target_pairs={{0,2},{1,4},{2,0},{3,6},{4,1},{5,8},{6,3},{7,10},{8,5},{9,12},{10,... | collective-permute-start | bytes 540680 | tf_op jit(solution)/shard_map/ppermute | solution.py:382
  6.5 1.7 %collective-permute-done.2.refs_0_ = f32[192,128]{1,0:T(8,128)S(1)} collective-permute-done((f32[192,128]{1,0:T(8,128)S(1)}, f32[192,128]{1,0:T(8,128)S(1)}, u32[]{:S(2)}, u32[]{:S(2)}) %collective-permute-start.2) | collective-permute-done | bytes 98336 | tf_op jit(solution)/shard_map/ppermute | solution.py:364
  8.2 1.7 %collective-permute-start.4 = (f32[144,128]{1,0:T(8,128)S(1)}, f32[144,128]{1,0:T(8,128)S(1)}, u32[]{:S(2)}, u32[]{:S(2)}) collective-permute-start(f32[144,128]{1,0:T(8,128)S(1)} %get-tuple-element.35), channel_id=1, source_target_pairs={{0,2},{1,6},{2,0},{3,4},{4,3},{5,10},{6,1},{7,8},{8,7},{9,14},{10,... | collective-permute-start | bytes 221192 | tf_op jit(solution)/shard_map/ppermute | solution.py:382
  10.5 0.8 %shard_map.80 = (f32[168,8,128]{2,1,0:T(8,128)S(1)}, f32[72,8,128]{2,1,0:T(8,128)S(1)}) custom-call(f32[352,128]{1,0:T(8,128)S(1)} %get-tuple-element.27.own_m_ref, f32[352,128]{1,0:T(8,128)S(1)} %get-tuple-element.28.par_m_ref, f32[192,128]{1,0:T(8,128)S(1)} %get-tuple-element.30.refs_0_, f32[192,128]{1,0:T(8,128)S(1)} %get-tuple-element.31.refs_1_), custom_call_target="tpu_custom_call" | custom-call | flops 1000000 | tf_op jit(solution)/shard_map/pallas_call | solution.py:29
  11.4 1.1 %collective-permute-done.4.refs_2_ = f32[144,128]{1,0:T(8,128)S(1)} collective-permute-done((f32[144,128]{1,0:T(8,128)S(1)}, f32[144,128]{1,0:T(8,128)S(1)}, u32[]{:S(2)}, u32[]{:S(2)}) %collective-permute-start.4) | collective-permute-done | bytes 73760 | tf_op jit(solution)/shard_map/ppermute | solution.py:382
  12.5 0.8 %shard_map.83 = (f32[288,128]{1,0:T(8,128)S(1)}, f32[432,128]{1,0:T(8,128)S(1)}, f32[288,128]{1,0:T(8,128)S(1)}) custom-call(f32[352,128]{1,0:T(8,128)S(1)} %collective-permute-done.1.far_m_ref, f32[352,128]{1,0:T(8,128)S(1)} %get-tuple-element.27.own_m_ref, f32[352,128]{1,0:T(8,128)S(1)} %get-tuple-element.28.par_m_ref, ...), custom_call_target="tpu_custom_call" | custom-call | flops 1000000 | tf_op jit(solution)/shard_map/pallas_call | solution.py:29
  13.4 0.9 %collective-permute-start.5 = (f32[432,128]{1,0:T(8,128)S(1)}, f32[432,128]{1,0:T(8,128)S(1)}, u32[]{:S(2)}, u32[]{:S(2)}) collective-permute-start(f32[432,128]{1,0:T(8,128)S(1)} %get-tuple-element.36.own_ref.d_ref), channel_id=1, source_target_pairs={{0,1},{1,0},{2,3},{3,2},{4,5},{5,4},{6,7},{7,6},{8,9},{9,8},{10,11... | collective-permute-start | bytes 663560 | tf_op jit(solution)/shard_map/ppermute | solution.py:361
  14.3 1.7 %collective-permute-start.7 = (f32[432,128]{1,0:T(8,128)S(1)}, f32[432,128]{1,0:T(8,128)S(1)}, u32[]{:S(2)}, u32[]{:S(2)}) collective-permute-start(f32[432,128]{1,0:T(8,128)S(1)} %get-tuple-element.36.own_ref.d_ref), channel_id=1, source_target_pairs={{0,2},{1,4},{2,0},{3,6},{4,1},{5,8},{6,3},{7,10},{8,5},{9,12},{10,... | collective-permute-start | bytes 663560 | tf_op jit(solution)/shard_map/ppermute | solution.py:382
  16.0 1.1 %collective-permute-start.6 = (f32[432,128]{1,0:T(8,128)S(1)}, f32[432,128]{1,0:T(8,128)S(1)}, u32[]{:S(2)}, u32[]{:S(2)}) collective-permute-start(f32[432,128]{1,0:T(8,128)S(1)} %collective-permute-done.5.par_ref), channel_id=1, source_target_pairs={{0,2},{1,4},{2,0},{3,6},{4,1},{5,8},{6,3},{7,10},{8,5},{9,12},{10,... | collective-permute-start | bytes 663560 | tf_op jit(solution)/shard_map/ppermute | solution.py:382
  17.1 0.9 %shard_map.84 = (f32[60,8,128]{2,1,0:T(8,128)S(1)}, f32[144,8,128]{2,1,0:T(8,128)S(1)}) custom-call(f32[432,128]{1,0:T(8,128)S(1)} %get-tuple-element.36.own_ref.d_ref, f32[432,128]{1,0:T(8,128)S(1)} %collective-permute-done.5.par_ref, f32[288,128]{1,0:T(8,128)S(1)} %get-tuple-element.37.st_ref), custom_call_target="tpu_custom_call" | custom-call | flops 1000000 | tf_op jit(solution)/shard_map/pallas_call | solution.py:29
  18.0 2.2 %collective-permute-done.7.far_ref = f32[432,128]{1,0:T(8,128)S(1)} collective-permute-done((f32[432,128]{1,0:T(8,128)S(1)}, f32[432,128]{1,0:T(8,128)S(1)}, u32[]{:S(2)}, u32[]{:S(2)}) %collective-permute-start.7) | collective-permute-done | bytes 221216 | tf_op jit(solution)/shard_map/ppermute | solution.py:382
  23.0 1.0 %shard_map.92 = (f32[8,128]{1,0:T(8,128)S(1)}, f32[288,128]{1,0:T(8,128)S(1)}) custom-call(f32[432,128]{1,0:T(8,128)S(1)} %collective-permute-done.6.next_ref, f32[432,128]{1,0:T(8,128)S(1)} %collective-permute-done.7.far_ref, f32[368,128]{1,0:T(8,128)S(1)} %get-tuple-element.39.own_ref.w_ref, f32[288,128]{1,0:T(8,128)S(1)} %get-tuple-element.37.st_ref, ...), custom_call_target="tpu_custom_call" | custom-call | flops 1000000 | tf_op jit(solution)/shard_map/pallas_call | solution.py:29
  24.2 0.6 %collective-permute-start.14 = (f32[720,128]{1,0:T(8,128)S(1)}, f32[720,128]{1,0:T(8,128)S(1)}, u32[]{:S(2)}, u32[]{:S(2)}) collective-permute-start(f32[720,128]{1,0:T(8,128)S(1)} %get-tuple-element.47), channel_id=1, source_target_pairs={{0,1},{1,0},{2,3},{3,2},{4,5},{5,4},{6,7},{7,6},{8,9},{9,8},{10,11... | collective-permute-start | bytes 1105928 | tf_op jit(solution)/shard_map/ppermute | solution.py:361
  24.8 1.2 %collective-permute-done.9 = f32[8,128]{1,0:T(8,128)S(1)} collective-permute-done((f32[8,128]{1,0:T(8,128)S(1)}, f32[8,128]{1,0:T(8,128)S(1)}, u32[]{:S(2)}, u32[]{:S(2)}) %collective-permute-start.9) | collective-permute-done | bytes 4128 | tf_op jit(solution)/shard_map/ppermute | solution.py:361
  26.1 1.7 %collective-permute-start.10 = (f32[8,128]{1,0:T(8,128)S(1)}, f32[8,128]{1,0:T(8,128)S(1)}, u32[]{:S(2)}, u32[]{:S(2)}) collective-permute-start(f32[8,128]{1,0:T(8,128)S(1)} %add.15), channel_id=1, source_target_pairs={{0,3},{1,2},{2,1},{3,0},{4,7},{5,6},{6,5},{7,4},{8,11},{9,10},{10,... | collective-permute-start | bytes 12296 | tf_op jit(solution)/shard_map/ppermute | solution.py:881
  27.8 1.3 %collective-permute-done.10 = f32[8,128]{1,0:T(8,128)S(1)} collective-permute-done((f32[8,128]{1,0:T(8,128)S(1)}, f32[8,128]{1,0:T(8,128)S(1)}, u32[]{:S(2)}, u32[]{:S(2)}) %collective-permute-start.10) | collective-permute-done | bytes 4128 | tf_op jit(solution)/shard_map/ppermute | solution.py:881
  29.1 3.4 %collective-permute-start.13 = (f32[8,128]{1,0:T(8,128)S(1)}, f32[8,128]{1,0:T(8,128)S(1)}, u32[]{:S(2)}, u32[]{:S(2)}) collective-permute-start(f32[8,128]{1,0:T(8,128)S(1)} %add.16), channel_id=1, source_target_pairs={{0,13},{1,12},{4,9},{5,8},{8,5},{9,4},{12,1},{13,0},{2,15},{3,14},... | collective-permute-start | bytes 12296 | tf_op jit(solution)/shard_map/ppermute | solution.py:881
  32.5 0.7 %collective-permute-start.11 = (f32[8,128]{1,0:T(8,128)S(1)}, f32[8,128]{1,0:T(8,128)S(1)}, u32[]{:S(2)}, u32[]{:S(2)}) collective-permute-start(f32[8,128]{1,0:T(8,128)S(1)} %add.16), channel_id=1, source_target_pairs={{0,5},{1,4},{4,1},{5,0},{8,13},{9,12},{12,9},{13,8},{2,7},{3,6},{6... | collective-permute-start | bytes 12296 | tf_op jit(solution)/shard_map/ppermute | solution.py:881
  33.2 0.8 %collective-permute-done.13 = f32[8,128]{1,0:T(8,128)S(1)} collective-permute-done((f32[8,128]{1,0:T(8,128)S(1)}, f32[8,128]{1,0:T(8,128)S(1)}, u32[]{:S(2)}, u32[]{:S(2)}) %collective-permute-start.13) | collective-permute-done | bytes 4128 | tf_op jit(solution)/shard_map/ppermute | solution.py:881
  34.0 2.5 %collective-permute-done.12 = f32[8,128]{1,0:T(8,128)S(1)} collective-permute-done((f32[8,128]{1,0:T(8,128)S(1)}, f32[8,128]{1,0:T(8,128)S(1)}, u32[]{:S(2)}, u32[]{:S(2)}) %collective-permute-start.12) | collective-permute-done | bytes 4128 | tf_op jit(solution)/shard_map/ppermute | solution.py:881
  36.4 1.5 %shard_map.94 = (f32[288,128]{1,0:T(8,128)}, f32[288,128]{1,0:T(8,128)}) custom-call(f32[8,128]{1,0:T(8,128)S(1)} %add_add_fusion.g_ref, f32[464,128]{1,0:T(8,128)S(1)} %get-tuple-element.26.s_ref.x_ref, f32[720,128]{1,0:T(8,128)S(1)} %get-tuple-element.46.mine_ref, f32[720,128]{1,0:T(8,128)S(1)} %collective-permute-done.14.kept_ref), custom_call_target="tpu_custom_call" | custom-call | flops 100000 | tf_op jit(solution)/shard_map/pallas_call | solution.py:29
  (31 shorter events, 3.8 us)
Async XLA Ops:
  1.7 3.1 %collective-permute-start = (f32[464,128]{1,0:T(8,128)S(1)}, f32[464,128]{1,0:T(8,128)S(1)}, u32[]{:S(2)}, u32[]{:S(2)}) collective-permute-start(f32[464,128]{1,0:T(8,128)S(1)} %get-tuple-element.26.s_ref.x_ref), channel_id=1, source_target_pairs={{0,1},{1,0},{2,3},{3,2},{4,5},{5,4},{6,7},{7,6},{8,9},{9,8},{10,11... | collective-permute-start | bytes 712712 | tf_op jit(solution)/shard_map/ppermute | solution.py:361
  2.2 5.9 %collective-permute-start.2 = (f32[192,128]{1,0:T(8,128)S(1)}, f32[192,128]{1,0:T(8,128)S(1)}, u32[]{:S(2)}, u32[]{:S(2)}) collective-permute-start(f32[192,128]{1,0:T(8,128)S(1)} %get-tuple-element.29), channel_id=1, source_target_pairs={{0,2},{2,0},{1,3},{3,1},{4,6},{6,4},{5,7},{7,5},{8,10},{10,8},{9,1... | collective-permute-start | bytes 294920 | tf_op jit(solution)/shard_map/ppermute | solution.py:364
  4.8 5.1 %copy-start = (f32[6,16,3]{1,2,0:T(4,128)S(1)}, f32[6,16,3]{1,2,0:T(4,128)}, u32[]{:S(2)}) copy-start(f32[6,16,3]{1,2,0:T(4,128)} %param.11) | copy-start | bytes 3460
  5.0 5.0 %copy-start.1 = (s32[6,16]{1,0:T(8,128)S(1)}, s32[6,16]{1,0:T(8,128)}, u32[]{:S(2)}) copy-start(s32[6,16]{1,0:T(8,128)} %node_ref.1) | copy-start | bytes 1156
  5.0 7.6 %collective-permute-start.1 = (f32[352,128]{1,0:T(8,128)S(1)}, f32[352,128]{1,0:T(8,128)S(1)}, u32[]{:S(2)}, u32[]{:S(2)}) collective-permute-start(f32[352,128]{1,0:T(8,128)S(1)} %get-tuple-element.27.own_m_ref), channel_id=1, source_target_pairs={{0,2},{1,4},{2,0},{3,6},{4,1},{5,8},{6,3},{7,10},{8,5},{9,12},{10,... | collective-permute-start | bytes 540680 | tf_op jit(solution)/shard_map/ppermute | solution.py:382
  8.2 2.2 %collective-permute-start.3 = (f32[192,128]{1,0:T(8,128)S(1)}, f32[192,128]{1,0:T(8,128)S(1)}, u32[]{:S(2)}, u32[]{:S(2)}) collective-permute-start(f32[192,128]{1,0:T(8,128)S(1)} %collective-permute-done.2.refs_0_), channel_id=1, source_target_pairs={{0,1},{1,0},{2,3},{3,2},{4,5},{5,4},{6,7},{7,6},{8,9},{9,8},{10,11... | collective-permute-start | bytes 294920 | tf_op jit(solution)/shard_map/ppermute | solution.py:361
  8.2 4.4 %collective-permute-start.4 = (f32[144,128]{1,0:T(8,128)S(1)}, f32[144,128]{1,0:T(8,128)S(1)}, u32[]{:S(2)}, u32[]{:S(2)}) collective-permute-start(f32[144,128]{1,0:T(8,128)S(1)} %get-tuple-element.35), channel_id=1, source_target_pairs={{0,2},{1,6},{2,0},{3,4},{4,3},{5,10},{6,1},{7,8},{8,7},{9,14},{10,... | collective-permute-start | bytes 221192 | tf_op jit(solution)/shard_map/ppermute | solution.py:382
  13.4 2.6 %collective-permute-start.5 = (f32[432,128]{1,0:T(8,128)S(1)}, f32[432,128]{1,0:T(8,128)S(1)}, u32[]{:S(2)}, u32[]{:S(2)}) collective-permute-start(f32[432,128]{1,0:T(8,128)S(1)} %get-tuple-element.36.own_ref.d_ref), channel_id=1, source_target_pairs={{0,1},{1,0},{2,3},{3,2},{4,5},{5,4},{6,7},{7,6},{8,9},{9,8},{10,11... | collective-permute-start | bytes 663560 | tf_op jit(solution)/shard_map/ppermute | solution.py:361
  14.3 5.9 %collective-permute-start.7 = (f32[432,128]{1,0:T(8,128)S(1)}, f32[432,128]{1,0:T(8,128)S(1)}, u32[]{:S(2)}, u32[]{:S(2)}) collective-permute-start(f32[432,128]{1,0:T(8,128)S(1)} %get-tuple-element.36.own_ref.d_ref), channel_id=1, source_target_pairs={{0,2},{1,4},{2,0},{3,6},{4,1},{5,8},{6,3},{7,10},{8,5},{9,12},{10,... | collective-permute-start | bytes 663560 | tf_op jit(solution)/shard_map/ppermute | solution.py:382
  16.0 7.0 %collective-permute-start.6 = (f32[432,128]{1,0:T(8,128)S(1)}, f32[432,128]{1,0:T(8,128)S(1)}, u32[]{:S(2)}, u32[]{:S(2)}) collective-permute-start(f32[432,128]{1,0:T(8,128)S(1)} %collective-permute-done.5.par_ref), channel_id=1, source_target_pairs={{0,2},{1,4},{2,0},{3,6},{4,1},{5,8},{6,3},{7,10},{8,5},{9,12},{10,... | collective-permute-start | bytes 663560 | tf_op jit(solution)/shard_map/ppermute | solution.py:382
  20.7 1.9 %collective-permute-start.8 = (f32[368,128]{1,0:T(8,128)S(1)}, f32[368,128]{1,0:T(8,128)S(1)}, u32[]{:S(2)}, u32[]{:S(2)}) collective-permute-start(f32[368,128]{1,0:T(8,128)S(1)} %get-tuple-element.39.own_ref.w_ref), channel_id=1, source_target_pairs={{0,1},{1,0},{2,3},{3,2},{4,5},{5,4},{6,7},{7,6},{8,9},{9,8},{10,11... | collective-permute-start | bytes 565256 | tf_op jit(solution)/shard_map/ppermute | solution.py:361
  24.2 12.2 %collective-permute-start.14 = (f32[720,128]{1,0:T(8,128)S(1)}, f32[720,128]{1,0:T(8,128)S(1)}, u32[]{:S(2)}, u32[]{:S(2)}) collective-permute-start(f32[720,128]{1,0:T(8,128)S(1)} %get-tuple-element.47), channel_id=1, source_target_pairs={{0,1},{1,0},{2,3},{3,2},{4,5},{5,4},{6,7},{7,6},{8,9},{9,8},{10,11... | collective-permute-start | bytes 1105928 | tf_op jit(solution)/shard_map/ppermute | solution.py:361
  24.8 1.3 %collective-permute-start.9 = (f32[8,128]{1,0:T(8,128)S(1)}, f32[8,128]{1,0:T(8,128)S(1)}, u32[]{:S(2)}, u32[]{:S(2)}) collective-permute-start(f32[8,128]{1,0:T(8,128)S(1)} %get-tuple-element.44), channel_id=1, source_target_pairs={{0,1},{1,0},{2,3},{3,2},{4,5},{5,4},{6,7},{7,6},{8,9},{9,8},{10,11... | collective-permute-start | bytes 12296 | tf_op jit(solution)/shard_map/ppermute | solution.py:361
  26.1 3.0 %collective-permute-start.10 = (f32[8,128]{1,0:T(8,128)S(1)}, f32[8,128]{1,0:T(8,128)S(1)}, u32[]{:S(2)}, u32[]{:S(2)}) collective-permute-start(f32[8,128]{1,0:T(8,128)S(1)} %add.15), channel_id=1, source_target_pairs={{0,3},{1,2},{2,1},{3,0},{4,7},{5,6},{6,5},{7,4},{8,11},{9,10},{10,... | collective-permute-start | bytes 12296 | tf_op jit(solution)/shard_map/ppermute | solution.py:881
  29.1 4.8 %collective-permute-start.13 = (f32[8,128]{1,0:T(8,128)S(1)}, f32[8,128]{1,0:T(8,128)S(1)}, u32[]{:S(2)}, u32[]{:S(2)}) collective-permute-start(f32[8,128]{1,0:T(8,128)S(1)} %add.16), channel_id=1, source_target_pairs={{0,13},{1,12},{4,9},{5,8},{8,5},{9,4},{12,1},{13,0},{2,15},{3,14},... | collective-permute-start | bytes 12296 | tf_op jit(solution)/shard_map/ppermute | solution.py:881
  32.5 3.9 %collective-permute-start.12 = (f32[8,128]{1,0:T(8,128)S(1)}, f32[8,128]{1,0:T(8,128)S(1)}, u32[]{:S(2)}, u32[]{:S(2)}) collective-permute-start(f32[8,128]{1,0:T(8,128)S(1)} %add.16), channel_id=1, source_target_pairs={{0,9},{1,8},{4,13},{5,12},{8,1},{9,0},{12,5},{13,4},{2,11},{3,10},... | collective-permute-start | bytes 12296 | tf_op jit(solution)/shard_map/ppermute | solution.py:881
  32.5 3.9 %collective-permute-start.11 = (f32[8,128]{1,0:T(8,128)S(1)}, f32[8,128]{1,0:T(8,128)S(1)}, u32[]{:S(2)}, u32[]{:S(2)}) collective-permute-start(f32[8,128]{1,0:T(8,128)S(1)} %add.16), channel_id=1, source_target_pairs={{0,5},{1,4},{4,1},{5,0},{8,13},{9,12},{12,9},{13,8},{2,7},{3,6},{6... | collective-permute-start | bytes 12296 | tf_op jit(solution)/shard_map/ppermute | solution.py:881
